TPU v7x, 32 devices: a whole 2x2x4 slice. The times are simulated.
32 devices in a mesh: wide: 8 (over y, x, core), narrow: 4 (over z).
Axes of the slice: x: 2, y: 2, z: 4, core: 2. Of those that a mesh axis runs over, the one named last changes fastest.
Arguments:
- tokens: bfloat16 [65536, 768], P(('wide', 'narrow')), may hold values from -6 to 6
- cotangent: bfloat16 [65536, 768], P(('wide', 'narrow')), may hold values from -6 to 6
- lengths: int32 [64, 24], P(('wide', 'narrow')), may hold values from 1 to 128, 1024 in all within a row
- features: float32 [64, 384], replicated, may hold values from -5 to 5
- ln1_gain: bfloat16 [768], P('wide'), may hold values from 0.5 to 1.5
- ln1_bias: bfloat16 [768], P('wide'), may hold values from -1.75 to 1.75
- q_weight: bfloat16 [768, 768], P('wide'), may hold values from -0.21875 to 0.21875
- q_bias: bfloat16 [768], P('wide'), may hold values from -3 to 3
- k_weight: bfloat16 [768, 768], P('wide'), may hold values from -0.21875 to 0.21875
- k_bias: bfloat16 [768], P('wide'), may hold values from -3 to 3
- v_weight: bfloat16 [768, 768], P('wide'), may hold values from -0.21875 to 0.21875
- v_bias: bfloat16 [768], P('wide'), may hold values from -3 to 3
- out_weight: bfloat16 [768, 768], P('wide'), may hold values from -0.875 to 0.875
- out_bias: bfloat16 [768], P('wide'), may hold values from -3 to 3
- ln2_gain: bfloat16 [768], P('wide'), may hold values from 0.5 to 1.5
- ln2_bias: bfloat16 [768], P('wide'), may hold values from -1.75 to 1.75
- up_weight: bfloat16 [768, 3072], P('wide'), may hold values from -0.21875 to 0.21875
- up_bias: bfloat16 [3072], P('wide'), may hold values from -3 to 3
- down_weight: bfloat16 [3072, 768], P('wide'), may hold values from -0.109375 to 0.109375
- down_bias: bfloat16 [768], P('wide'), may hold values from -3 to 3
Outputs:
- output: bfloat16 [65536, 768], P(('wide', 'narrow'))
- input_grad: float32 [65536, 768], P(('wide', 'narrow'))
- ln1_gain_grad: float32 [768], P('wide')
- ln1_bias_grad: float32 [768], P('wide')
- q_weight_grad: float32 [768, 768], P('wide')
- q_bias_grad: float32 [768], P('wide')
- k_weight_grad: float32 [768, 768], P('wide')
- k_bias_grad: float32 [768], P('wide')
- v_weight_grad: float32 [768, 768], P('wide')
- v_bias_grad: float32 [768], P('wide')
- out_weight_grad: float32 [768, 768], P('wide')
- out_bias_grad: float32 [768], P('wide')
- ln2_gain_grad: float32 [768], P('wide')
- ln2_bias_grad: float32 [768], P('wide')
- up_weight_grad: float32 [768, 3072], P('wide')
- up_bias_grad: float32 [3072], P('wide')
- down_weight_grad: float32 [3072, 768], P('wide')
- down_bias_grad: float32 [768], P('wide')
Inputs may be any that keep to these rules, and one draw needn't show every extreme that they name: Each row holds the 24 piece lengths of one sequence in order, summing to 1024; the largest is exactly 128.
All inputs are finite; a program needn't handle non-finite values.
Results may differ from a plain program's by a relative error of at most 0.03.
Values may be sent and summed in bfloat16 or wider, within the bound.
A program may use at most 192 MiB of HBM per device.

v0:
```python
from functools import partial
import math

import jax
import jax.numpy as jnp
from jax import lax
from jax.sharding import PartitionSpec as P

D = 768
HEADS = 12
HD = 64
FEAT = 32
SEGS = 24


EPSILON = 1e-05
HIGHEST = lax.Precision.HIGHEST


def pieces(lens_row, seq_len):
    seg_end = jnp.cumsum(lens_row)
    seg_start = seg_end - lens_row
    places = jnp.arange(seq_len, dtype=jnp.int32)
    segment = jnp.sum((places[:, None] >= seg_end[None, :]).astype(jnp.int32), axis=1)
    slots = jnp.arange(SEGS, dtype=jnp.int32)
    begins = jnp.sum(jnp.where(segment[:, None] == slots[None, :], seg_start[None, :], 0), axis=1)
    position = places - begins
    valid = (segment < SEGS - 1).astype(jnp.float32)
    allowed = (places[None, :] <= places[:, None]) & (segment[None, :] == segment[:, None])
    return (position, valid, allowed)


def rotate(heads_field, position):
    half = HD // 2
    rates = jnp.exp(jnp.arange(half, dtype=jnp.float32) * (-2.0 * math.log(10000.0) / HD))
    angles = position.astype(jnp.float32)[:, None] * rates[None, :]
    cosine = jnp.cos(angles)[:, None, :]
    sine = jnp.sin(angles)[:, None, :]
    first = heads_field[..., :half]
    second = heads_field[..., half:]
    return jnp.concatenate(
        [first * cosine - second * sine, second * cosine + first * sine], axis=-1
    )


def featurize(rotated, features):
    table = features.reshape(HD, HEADS, FEAT)
    scores = jnp.einsum("lhe,ehm->lhm", rotated, table, precision=HIGHEST) * 0.125
    return jax.nn.elu(scores) + 1.0


def normalize(stream, gain, shift):
    average = jnp.mean(stream, axis=-1, keepdims=True)
    centered = stream - average
    variance = jnp.mean(centered * centered, axis=-1, keepdims=True)
    return centered * lax.rsqrt(variance + EPSILON) * gain + shift


def contract_rows(left, right):
    return lax.dot_general(
        left, right, (((0,), (0,)), ((), ())), preferred_element_type=jnp.float32
    )


def times_transposed(left, right):
    return lax.dot_general(
        left, right, (((1,), (1,)), ((), ())), preferred_element_type=jnp.float32
    )


def column_sums(matrix):
    return jnp.sum(matrix.astype(jnp.float32), axis=0)


def collect(shards):
    return (
        lax.all_gather(shards[0], "wide", axis=0, tiled=True),
        lax.all_gather(shards[1], "wide", axis=0, tiled=True),
        lax.all_gather(shards[2], "wide", axis=0, tiled=True),
        lax.all_gather(shards[3], "wide", axis=0, tiled=True),
        lax.all_gather(shards[4], "wide", axis=0, tiled=True),
        lax.all_gather(shards[5], "wide", axis=0, tiled=True),
        lax.all_gather(shards[6], "wide", axis=0, tiled=True),
        lax.all_gather(shards[7], "wide", axis=0, tiled=True),
        lax.all_gather(shards[8], "wide", axis=0, tiled=True),
        lax.all_gather(shards[9], "wide", axis=0, tiled=True),
        lax.all_gather(shards[10], "wide", axis=0, tiled=True),
        lax.all_gather(shards[11], "wide", axis=0, tiled=True),
        lax.all_gather(shards[12], "wide", axis=0, tiled=True),
        lax.all_gather(shards[13], "wide", axis=0, tiled=True),
        lax.all_gather(shards[14], "wide", axis=0, tiled=True),
        lax.all_gather(shards[15], "wide", axis=0, tiled=True),
    )


def settle(grads):
    shares = (
        lax.psum_scatter(grads[0], "wide", scatter_dimension=0, tiled=True),
        lax.psum_scatter(grads[1], "wide", scatter_dimension=0, tiled=True),
        lax.psum_scatter(grads[2], "wide", scatter_dimension=0, tiled=True),
        lax.psum_scatter(grads[3], "wide", scatter_dimension=0, tiled=True),
        lax.psum_scatter(grads[4], "wide", scatter_dimension=0, tiled=True),
        lax.psum_scatter(grads[5], "wide", scatter_dimension=0, tiled=True),
        lax.psum_scatter(grads[6], "wide", scatter_dimension=0, tiled=True),
        lax.psum_scatter(grads[7], "wide", scatter_dimension=0, tiled=True),
        lax.psum_scatter(grads[8], "wide", scatter_dimension=0, tiled=True),
        lax.psum_scatter(grads[9], "wide", scatter_dimension=0, tiled=True),
        lax.psum_scatter(grads[10], "wide", scatter_dimension=0, tiled=True),
        lax.psum_scatter(grads[11], "wide", scatter_dimension=0, tiled=True),
        lax.psum_scatter(grads[12], "wide", scatter_dimension=0, tiled=True),
        lax.psum_scatter(grads[13], "wide", scatter_dimension=0, tiled=True),
        lax.psum_scatter(grads[14], "wide", scatter_dimension=0, tiled=True),
        lax.psum_scatter(grads[15], "wide", scatter_dimension=0, tiled=True),
    )
    return (
        lax.psum(shares[0].astype(jnp.bfloat16), "narrow").astype(jnp.float32),
        lax.psum(shares[1].astype(jnp.bfloat16), "narrow").astype(jnp.float32),
        lax.psum(shares[2].astype(jnp.bfloat16), "narrow").astype(jnp.float32),
        lax.psum(shares[3].astype(jnp.bfloat16), "narrow").astype(jnp.float32),
        lax.psum(shares[4].astype(jnp.bfloat16), "narrow").astype(jnp.float32),
        lax.psum(shares[5].astype(jnp.bfloat16), "narrow").astype(jnp.float32),
        lax.psum(shares[6].astype(jnp.bfloat16), "narrow").astype(jnp.float32),
        lax.psum(shares[7].astype(jnp.bfloat16), "narrow").astype(jnp.float32),
        lax.psum(shares[8].astype(jnp.bfloat16), "narrow").astype(jnp.float32),
        lax.psum(shares[9].astype(jnp.bfloat16), "narrow").astype(jnp.float32),
        lax.psum(shares[10].astype(jnp.bfloat16), "narrow").astype(jnp.float32),
        lax.psum(shares[11].astype(jnp.bfloat16), "narrow").astype(jnp.float32),
        lax.psum(shares[12].astype(jnp.bfloat16), "narrow").astype(jnp.float32),
        lax.psum(shares[13].astype(jnp.bfloat16), "narrow").astype(jnp.float32),
        lax.psum(shares[14].astype(jnp.bfloat16), "narrow").astype(jnp.float32),
        lax.psum(shares[15].astype(jnp.bfloat16), "narrow").astype(jnp.float32),
    )


def head_forward(operands, allowed):
    query_feat, key_feat, head_value = operands
    scores = jnp.where(allowed, times_transposed(query_feat, key_feat), 0.0)
    denominator = jnp.sum(scores, axis=1)
    numerator = jnp.dot(scores.astype(jnp.bfloat16), head_value, preferred_element_type=jnp.float32)
    return (numerator, denominator)


def head_backward(operands, allowed, valid):
    query_feat, key_feat, head_value, numerator, denominator, head_grad = operands
    scores = jnp.where(allowed, times_transposed(query_feat, key_feat), 0.0)
    scores_low = scores.astype(jnp.bfloat16)
    scaled = head_grad * valid[:, None]
    grad_num = (scaled / denominator[:, None]).astype(jnp.bfloat16)
    grad_den = -jnp.sum(scaled * numerator, axis=1) / (denominator * denominator)
    grad_scores = (times_transposed(grad_num, head_value) + grad_den[:, None]).astype(jnp.bfloat16)
    grad_scores = jnp.where(allowed, grad_scores, jnp.zeros((), jnp.bfloat16))
    grad_value = contract_rows(scores_low, grad_num)
    grad_query = jnp.dot(grad_scores, key_feat, preferred_element_type=jnp.float32)
    grad_key = contract_rows(grad_scores, query_feat)
    return (grad_query, grad_key, grad_value)


def run_layer(weights, shards, rows, upward, lens_row, features):
    (
        gain_first,
        shift_first,
        query_mat,
        query_add,
        key_mat,
        key_add,
        value_mat,
        value_add,
        proj_mat,
        proj_add,
        gain_second,
        shift_second,
        up_mat,
        up_add,
        down_mat,
        down_add,
    ) = weights
    seq_len = rows.shape[0]
    stream = rows.astype(jnp.float32)
    position, valid, allowed = pieces(lens_row, seq_len)
    normed_one, norm_one_back = jax.vjp(
        normalize, stream, gain_first.astype(jnp.float32), shift_first.astype(jnp.float32)
    )
    hidden_one = normed_one.astype(jnp.bfloat16)
    query_pre = jnp.dot(
        hidden_one, query_mat, preferred_element_type=jnp.float32
    ) + query_add.astype(jnp.float32)
    key_pre = jnp.dot(hidden_one, key_mat, preferred_element_type=jnp.float32) + key_add.astype(
        jnp.float32
    )
    values = (
        jnp.dot(hidden_one, value_mat, preferred_element_type=jnp.float32)
        + value_add.astype(jnp.float32)
    ).astype(jnp.bfloat16)

    def features_of(projected):
        return featurize(rotate(projected.reshape(seq_len, HEADS, HD), position), features)

    query_feat_full, query_back = jax.vjp(features_of, query_pre)
    key_feat_full, key_back = jax.vjp(features_of, key_pre)
    heads_query = jnp.transpose(query_feat_full.astype(jnp.bfloat16), (1, 0, 2))
    heads_key = jnp.transpose(key_feat_full.astype(jnp.bfloat16), (1, 0, 2))
    heads_value = jnp.transpose(values.reshape(seq_len, HEADS, HD), (1, 0, 2))
    numerator, denominator = lax.map(
        partial(head_forward, allowed=allowed), (heads_query, heads_key, heads_value)
    )
    mixed = numerator / denominator[:, :, None] * valid[None, :, None]
    attended = jnp.transpose(mixed, (1, 0, 2)).reshape(seq_len, D).astype(jnp.bfloat16)
    residual = stream + (
        jnp.dot(attended, proj_mat, preferred_element_type=jnp.float32)
        + proj_add.astype(jnp.float32)
    )
    normed_two, norm_two_back = jax.vjp(
        normalize, residual, gain_second.astype(jnp.float32), shift_second.astype(jnp.float32)
    )
    hidden_two = normed_two.astype(jnp.bfloat16)
    upper = jnp.dot(hidden_two, up_mat, preferred_element_type=jnp.float32) + up_add.astype(
        jnp.float32
    )
    activated, gelu_back = jax.vjp(partial(jax.nn.gelu, approximate=False), upper)
    act_low = activated.astype(jnp.bfloat16)
    result = residual + (
        jnp.dot(act_low, down_mat, preferred_element_type=jnp.float32)
        + down_add.astype(jnp.float32)
    )
    output = result.astype(jnp.bfloat16)
    anchored = lax.optimization_barrier((shards, result))
    again = collect(anchored[0])
    query_mat, key_mat, value_mat, proj_mat, up_mat, down_mat = (
        again[2],
        again[4],
        again[6],
        again[8],
        again[12],
        again[14],
    )
    grad_out = upward.astype(jnp.float32)
    down_grad = contract_rows(act_low, upward)
    down_bias_grad = column_sums(upward)
    grad_act = times_transposed(upward, down_mat)
    grad_upper = gelu_back(grad_act)[0].astype(jnp.bfloat16)
    up_grad = contract_rows(hidden_two, grad_upper)
    up_bias_grad = column_sums(grad_upper)
    grad_hidden_two = times_transposed(grad_upper, up_mat)
    grad_residual_norm, gain_two_grad, shift_two_grad = norm_two_back(grad_hidden_two)
    grad_residual = grad_out + grad_residual_norm
    grad_proj_in = grad_residual.astype(jnp.bfloat16)
    proj_grad = contract_rows(attended, grad_proj_in)
    proj_bias_grad = column_sums(grad_proj_in)
    grad_attended = times_transposed(grad_proj_in, proj_mat)
    heads_grad = jnp.transpose(grad_attended.reshape(seq_len, HEADS, HD), (1, 0, 2))
    grad_qfeat, grad_kfeat, grad_vheads = lax.map(
        partial(head_backward, allowed=allowed, valid=valid),
        (heads_query, heads_key, heads_value, numerator, denominator, heads_grad),
    )
    grad_query = query_back(jnp.transpose(grad_qfeat, (1, 0, 2)))[0].astype(jnp.bfloat16)
    grad_key = key_back(jnp.transpose(grad_kfeat, (1, 0, 2)))[0].astype(jnp.bfloat16)
    grad_value = jnp.transpose(grad_vheads, (1, 0, 2)).reshape(seq_len, D).astype(jnp.bfloat16)
    query_grad = contract_rows(hidden_one, grad_query)
    query_bias_grad = column_sums(grad_query)
    key_grad = contract_rows(hidden_one, grad_key)
    key_bias_grad = column_sums(grad_key)
    value_grad = contract_rows(hidden_one, grad_value)
    value_bias_grad = column_sums(grad_value)
    grad_hidden_one = (
        times_transposed(grad_query, query_mat)
        + times_transposed(grad_key, key_mat)
        + times_transposed(grad_value, value_mat)
    )
    grad_stream_norm, gain_one_grad, shift_one_grad = norm_one_back(grad_hidden_one)
    input_grad = grad_residual + grad_stream_norm
    grads = (
        gain_one_grad,
        shift_one_grad,
        query_grad,
        query_bias_grad,
        key_grad,
        key_bias_grad,
        value_grad,
        value_bias_grad,
        proj_grad,
        proj_bias_grad,
        gain_two_grad,
        shift_two_grad,
        up_grad,
        up_bias_grad,
        down_grad,
        down_bias_grad,
    )
    return ((output, input_grad), grads)


def on_device(
    tokens,
    cotangent,
    lengths,
    features,
    ln1_gain,
    ln1_bias,
    q_weight,
    q_bias,
    k_weight,
    k_bias,
    v_weight,
    v_bias,
    out_weight,
    out_bias,
    ln2_gain,
    ln2_bias,
    up_weight,
    up_bias,
    down_weight,
    down_bias,
):
    shards = (
        ln1_gain,
        ln1_bias,
        q_weight,
        q_bias,
        k_weight,
        k_bias,
        v_weight,
        v_bias,
        out_weight,
        out_bias,
        ln2_gain,
        ln2_bias,
        up_weight,
        up_bias,
        down_weight,
        down_bias,
    )
    micro_count = lengths.shape[0]
    seq_len = tokens.shape[0] // micro_count
    stream = tokens.reshape(micro_count, seq_len, D)
    upstream = cotangent.reshape(micro_count, seq_len, D)

    def process(totals, operands):
        rows, upward, lens_row = operands
        weights = collect(shards)
        outcome, grads = run_layer(weights, shards, rows, upward, lens_row, features)
        grads = settle(grads)
        totals = tuple((total + member for total, member in zip(totals, grads)))
        return (totals, outcome)

    totals = tuple((jnp.zeros(piece.shape, jnp.float32) for piece in shards))
    totals, outcome = lax.scan(process, totals, (stream, upstream, lengths))
    output = outcome[0].reshape(micro_count * seq_len, D)
    input_grad = outcome[1].reshape(micro_count * seq_len, D)
    return (
        output,
        input_grad,
        totals[0],
        totals[1],
        totals[2],
        totals[3],
        totals[4],
        totals[5],
        totals[6],
        totals[7],
        totals[8],
        totals[9],
        totals[10],
        totals[11],
        totals[12],
        totals[13],
        totals[14],
        totals[15],
    )


def solution(mesh):
    in_specs = (
        P(("wide", "narrow"), None),
        P(("wide", "narrow"), None),
        P(("wide", "narrow"), None),
        P(),
        P("wide"),
        P("wide"),
        P("wide", None),
        P("wide"),
        P("wide", None),
        P("wide"),
        P("wide", None),
        P("wide"),
        P("wide", None),
        P("wide"),
        P("wide"),
        P("wide"),
        P("wide", None),
        P("wide"),
        P("wide", None),
        P("wide"),
    )
    out_specs = (
        P(("wide", "narrow"), None),
        P(("wide", "narrow"), None),
        P("wide"),
        P("wide"),
        P("wide", None),
        P("wide"),
        P("wide", None),
        P("wide"),
        P("wide", None),
        P("wide"),
        P("wide", None),
        P("wide"),
        P("wide"),
        P("wide"),
        P("wide", None),
        P("wide"),
        P("wide", None),
        P("wide"),
    )
    return jax.shard_map(
        on_device, mesh=mesh, in_specs=in_specs, out_specs=out_specs, check_vma=False
    )
```

profile of v0, /device:TPU:0, one launch (start us, length us, event | category | flops | bytes accessed | tf_op | source)
XLA Modules:
  0.0 1814.9 jit_solution(2300165558334829276)
XLA Ops:
  9.0 1799.1 %while.82 = (s32[]{:T(128)}, f32[96]{0:T(128)}, f32[96]{0:T(128)}, f32[96,768]{1,0:T(8,128)}, f32[96]{0:T(128)}, /*index=5*/f32[96,768]{1,0:T(8,128)}, f32[96]{0...) while((s32[]{:T(128)}, f32[96]{0:T(128)}, f32[96]{0:T(128)}, ...), condition=%wide.region_60.61_spmd.clone.clone, body=%wide.region_0.60_spmd.clone.sunk.clone | while | flops 45781344256 | bytes 794361152 | solution.py:346
  24.6 25.7 %all-reduce.44 = (bf16[768]{0:T(1024)(128)(2,1)S(1)}, bf16[768]{0:T(1024)(128)(2,1)S(1)}, bf16[768]{0:T(1024)(128)(2,1)S(1)}, bf16[768]{0:T(1024)(128)(2,1)S(1)}...) all-reduce(bf16[768]{0:T(1024)(128)(2,1)S(1)} %dynamic-update-slice, ...), channel_id=1, replica_groups=mesh['wide'=8,'narrow'=4] {'wide'}, use_global_device_ids=true, to_apply=%add.6 | all-reduce | flops 6912 | bytes 27648 | tf_op jit(solution)/shard_map/while
  54.0 8.1 all-gather.4
  96.1 51.7 %while.80 = (s32[]{:T(128)}, f32[12,1024,64]{1,2,0:T(8,128)}, f32[12,1024]{1,0:T(8,128)S(1)}, bf16[12,1024,32]{2,1,0:T(8,128)(2,1)}, bf16[12,1024,32]{2,1,0:T(8,...) while((s32[]{:T(128)}, f32[12,1024,64]{1,2,0:T(8,128)}, ...), condition=%wide.region_8.8_spmd.clone, body=%wide.region_6.7_spmd.clone.sunk | while | flops 211811328 | bytes 5273697 | solution.py:203
  156.7 38.0 %multiply_convert_fusion.7 = (bf16[1024,3072]{1,0:T(8,128)(2,1)}, f32[1024,3072]{1,0:T(8,128)}, f32[1024,3072]{1,0:T(8,128)}) fusion(f32[3072]{0:T(1024)S(1)} %bitcast.499, bf16[768,3072]{1,0:T(8,128)(2,1)} %all-gather.26.cloned.1.call-done, f32[1024,768]{0,1:T(8,128)} %copy-done.3, f32[768]{0:T(1024)S(1)} %convert_element_type.664, ...), kind=kOutput, calls=%fused_computation.64.clone.1.clone | convolution fusion | flops 5043388416 | bytes 39348224 | tf_op jit(solution)/shard_map/while/body/eval_jaxpr/dot_general | solution.py:216
  197.3 9.6 add_add_fusion.7
  216.5 29.3 %all-gather.34.cloned.1.call-done = bf16[3072,768]{1,0:T(8,128)(2,1)} async-done(((bf16[384,768]{1,0:T(8,128)(2,1)}), bf16[3072,768]{1,0:T(8,128)(2,1)}) %all-gather.34.cloned.1.call-update) | async-done | bytes 4718608 | tf_op jit(solution)/shard_map/while/body/eval_jaxpr/all_gather | solution.py:91
  245.8 18.6 %convert_reduce_fusion.24 = (f32[3072]{0:T(1024)S(1)}, bf16[1024,3072]{1,0:T(8,128)(2,1)}) fusion(f32[1024,3072]{1,0:T(8,128)} %get-tuple-element.1641, bf16[3072,768]{1,0:T(8,128)(2,1)} %all-gather.34.cloned.1.call-done, bf16[1,1024,768]{2,1,0:T(8,128)(2,1)} %constant_dynamic-slice_fusion.14, f32[1024,3072]{1,0:T(8,128)} %get-tuple-element.1643, ...), kind=kOutput, calls=%fused_computation.62.clone.1.clone | convolution fusion | flops 4885312512 | bytes 37773312 | tf_op jit(solution)/shard_map/while/body/eval_jaxpr/dot_general | solution.py:66
  264.3 22.1 %all-gather.36.cloned.1.call-done = bf16[768,3072]{1,0:T(8,128)(2,1)} async-done(((bf16[96,3072]{1,0:T(8,128)(2,1)}), bf16[768,3072]{1,0:T(8,128)(2,1)}) %all-gather.36.cloned.1.call-update) | async-done | bytes 4718608 | tf_op jit(solution)/shard_map/while/body/eval_jaxpr/all_gather | solution.py:89
  286.5 9.8 fusion.418
  305.9 6.4 all-gather.32.cloned.1.call-done
  316.7 5.9 copy.152
  322.6 148.0 %while.81 = (s32[]{:T(128)}, f32[12,1024,32]{1,2,0:T(8,128)}, f32[12,1024,32]{1,2,0:T(8,128)}, bf16[12,1024,64]{1,2,0:T(8,128)(2,1)S(1)}, f32[12,1024,64]{2,1,0:...) while((s32[]{:T(128)}, f32[12,1024,32]{1,2,0:T(8,128)}, ...), condition=%wide.region_15.15_spmd.clone, body=%wide.region_13.14_spmd.clone.sunk | while | flops 481888256 | bytes 10818697 | solution.py:251
  470.7 5.7 convolution_bitcast_fusion.9
  502.1 9.9 fusion.431
  512.1 10.6 fusion.430
  549.3 26.2 %reduce-scatter.7.cloned.1.call-done = f32[96,768]{1,0:T(8,128)} async-done(((f32[768,768]{1,0:T(8,128)}), f32[96,768]{1,0:T(8,128)}) %reduce-scatter.7.cloned.1.call-update) | async-done | bytes 294928 | tf_op jit(solution)/shard_map/while/body/eval_jaxpr/reduce_scatter | solution.py:100
  577.2 43.9 %reduce-scatter.13.cloned.1.call-done = f32[96,768]{1,0:T(8,128)} async-done(((f32[768,768]{1,0:T(8,128)}), f32[96,768]{1,0:T(8,128)}) %reduce-scatter.13.cloned.1.call-update) | async-done | bytes 294928 | tf_op jit(solution)/shard_map/while/body/eval_jaxpr/reduce_scatter | solution.py:106
  622.7 43.9 %reduce-scatter.11.cloned.1.call-done = f32[96,768]{1,0:T(8,128)} async-done(((f32[768,768]{1,0:T(8,128)}), f32[96,768]{1,0:T(8,128)}) %reduce-scatter.11.cloned.1.call-update) | async-done | bytes 294928 | tf_op jit(solution)/shard_map/while/body/eval_jaxpr/reduce_scatter | solution.py:104
  668.3 78.5 %reduce-scatter.17.cloned.1.call-done = f32[384,768]{1,0:T(8,128)} async-done(((f32[3072,768]{1,0:T(8,128)}), f32[384,768]{1,0:T(8,128)}) %reduce-scatter.17.cloned.1.call-update) | async-done | bytes 1179664 | tf_op jit(solution)/shard_map/while/body/eval_jaxpr/reduce_scatter | solution.py:112
  749.0 78.1 %reduce-scatter.15.cloned.1.call-done = f32[96,3072]{1,0:T(8,128)} async-done(((f32[768,3072]{1,0:T(8,128)}), f32[96,3072]{1,0:T(8,128)}) %reduce-scatter.15.cloned.1.call-update) | async-done | bytes 1179664 | tf_op jit(solution)/shard_map/while/body/eval_jaxpr/reduce_scatter | solution.py:110
  829.2 6.0 add_bitcast_fusion.3
  837.1 25.0 %all-reduce.45 = (bf16[768]{0:T(1024)(128)(2,1)S(1)}, bf16[768]{0:T(1024)(128)(2,1)S(1)}, bf16[768]{0:T(1024)(128)(2,1)S(1)}, bf16[768]{0:T(1024)(128)(2,1)S(1)}...) all-reduce(f32[768]{0:T(1024)S(1)} %get-tuple-element.1666, ...), channel_id=2, replica_groups=mesh['wide'=8,'narrow'=4] {'wide'}, use_global_device_ids=true, to_apply=%region_17.17.clone | all-reduce | flops 9984 | bytes 59904 | tf_op jit(solution)/shard_map/while
  865.3 12.0 all-reduce.46
  879.6 26.1 %all-reduce.50.cloned.1.call-done = (bf16[96,768]{1,0:T(8,128)(2,1)}, bf16[96,768]{1,0:T(8,128)(2,1)}, bf16[96,768]{1,0:T(8,128)(2,1)}, bf16[96,768]{1,0:T(8,128...) async-done(((bf16[96,768]{1,0:T(8,128)(2,1)}, bf16[96,768]{1,0:T(8,128)(2,1)}, bf16[96,768]{1,0:T(8,128)(2,1)}, bf16[96,768]{1,0:T(8,128)(2,1)}, ...) | async-done | bytes 1769488 | tf_op jit(solution)/shard_map/while/body/eval_jaxpr/psum | solution.py:118
  925.8 23.8 %all-reduce.44 = (bf16[768]{0:T(1024)(128)(2,1)S(1)}, bf16[768]{0:T(1024)(128)(2,1)S(1)}, bf16[768]{0:T(1024)(128)(2,1)S(1)}, bf16[768]{0:T(1024)(128)(2,1)S(1)}...) all-reduce(bf16[768]{0:T(1024)(128)(2,1)S(1)} %dynamic-update-slice, ...), channel_id=1, replica_groups=mesh['wide'=8,'narrow'=4] {'wide'}, use_global_device_ids=true, to_apply=%add.6 | all-reduce | flops 6912 | bytes 27648 | tf_op jit(solution)/shard_map/while
  953.3 7.9 all-gather.4
  994.5 51.8 %while.80 = (s32[]{:T(128)}, f32[12,1024,64]{1,2,0:T(8,128)}, f32[12,1024]{1,0:T(8,128)S(1)}, bf16[12,1024,32]{2,1,0:T(8,128)(2,1)}, bf16[12,1024,32]{2,1,0:T(8,...) while((s32[]{:T(128)}, f32[12,1024,64]{1,2,0:T(8,128)}, ...), condition=%wide.region_8.8_spmd.clone, body=%wide.region_6.7_spmd.clone.sunk | while | flops 211811328 | bytes 5273697 | solution.py:203
  1054.4 38.1 %multiply_convert_fusion.7 = (bf16[1024,3072]{1,0:T(8,128)(2,1)}, f32[1024,3072]{1,0:T(8,128)}, f32[1024,3072]{1,0:T(8,128)}) fusion(f32[3072]{0:T(1024)S(1)} %bitcast.499, bf16[768,3072]{1,0:T(8,128)(2,1)} %all-gather.26.cloned.1.call-done, f32[1024,768]{0,1:T(8,128)} %copy-done.3, f32[768]{0:T(1024)S(1)} %convert_element_type.664, ...), kind=kOutput, calls=%fused_computation.64.clone.1.clone | convolution fusion | flops 5043388416 | bytes 39348224 | tf_op jit(solution)/shard_map/while/body/eval_jaxpr/dot_general | solution.py:216
  1094.4 9.6 add_add_fusion.7
  1113.4 29.5 %all-gather.34.cloned.1.call-done = bf16[3072,768]{1,0:T(8,128)(2,1)} async-done(((bf16[384,768]{1,0:T(8,128)(2,1)}), bf16[3072,768]{1,0:T(8,128)(2,1)}) %all-gather.34.cloned.1.call-update) | async-done | bytes 4718608 | tf_op jit(solution)/shard_map/while/body/eval_jaxpr/all_gather | solution.py:91
  1142.9 18.7 %convert_reduce_fusion.24 = (f32[3072]{0:T(1024)S(1)}, bf16[1024,3072]{1,0:T(8,128)(2,1)}) fusion(f32[1024,3072]{1,0:T(8,128)} %get-tuple-element.1641, bf16[3072,768]{1,0:T(8,128)(2,1)} %all-gather.34.cloned.1.call-done, bf16[1,1024,768]{2,1,0:T(8,128)(2,1)} %constant_dynamic-slice_fusion.14, f32[1024,3072]{1,0:T(8,128)} %get-tuple-element.1643, ...), kind=kOutput, calls=%fused_computation.62.clone.1.clone | convolution fusion | flops 4885312512 | bytes 37773312 | tf_op jit(solution)/shard_map/while/body/eval_jaxpr/dot_general | solution.py:66
  1161.6 21.8 %all-gather.36.cloned.1.call-done = bf16[768,3072]{1,0:T(8,128)(2,1)} async-done(((bf16[96,3072]{1,0:T(8,128)(2,1)}), bf16[768,3072]{1,0:T(8,128)(2,1)}) %all-gather.36.cloned.1.call-update) | async-done | bytes 4718608 | tf_op jit(solution)/shard_map/while/body/eval_jaxpr/all_gather | solution.py:89
  1183.4 9.8 fusion.418
  1202.8 6.4 all-gather.32.cloned.1.call-done
  1213.6 5.9 copy.152
  1219.6 147.7 %while.81 = (s32[]{:T(128)}, f32[12,1024,32]{1,2,0:T(8,128)}, f32[12,1024,32]{1,2,0:T(8,128)}, bf16[12,1024,64]{1,2,0:T(8,128)(2,1)S(1)}, f32[12,1024,64]{2,1,0:...) while((s32[]{:T(128)}, f32[12,1024,32]{1,2,0:T(8,128)}, ...), condition=%wide.region_15.15_spmd.clone, body=%wide.region_13.14_spmd.clone.sunk | while | flops 481888256 | bytes 10818697 | solution.py:251
  1398.8 9.9 fusion.431
  1408.8 10.6 fusion.430
  1446.2 25.9 %reduce-scatter.7.cloned.1.call-done = f32[96,768]{1,0:T(8,128)} async-done(((f32[768,768]{1,0:T(8,128)}), f32[96,768]{1,0:T(8,128)}) %reduce-scatter.7.cloned.1.call-update) | async-done | bytes 294928 | tf_op jit(solution)/shard_map/while/body/eval_jaxpr/reduce_scatter | solution.py:100
  1473.7 44.0 %reduce-scatter.13.cloned.1.call-done = f32[96,768]{1,0:T(8,128)} async-done(((f32[768,768]{1,0:T(8,128)}), f32[96,768]{1,0:T(8,128)}) %reduce-scatter.13.cloned.1.call-update) | async-done | bytes 294928 | tf_op jit(solution)/shard_map/while/body/eval_jaxpr/reduce_scatter | solution.py:106
  1519.4 44.1 %reduce-scatter.11.cloned.1.call-done = f32[96,768]{1,0:T(8,128)} async-done(((f32[768,768]{1,0:T(8,128)}), f32[96,768]{1,0:T(8,128)}) %reduce-scatter.11.cloned.1.call-update) | async-done | bytes 294928 | tf_op jit(solution)/shard_map/while/body/eval_jaxpr/reduce_scatter | solution.py:104
  1565.1 78.6 %reduce-scatter.17.cloned.1.call-done = f32[384,768]{1,0:T(8,128)} async-done(((f32[3072,768]{1,0:T(8,128)}), f32[384,768]{1,0:T(8,128)}) %reduce-scatter.17.cloned.1.call-update) | async-done | bytes 1179664 | tf_op jit(solution)/shard_map/while/body/eval_jaxpr/reduce_scatter | solution.py:112
  1645.8 78.1 %reduce-scatter.15.cloned.1.call-done = f32[96,3072]{1,0:T(8,128)} async-done(((f32[768,3072]{1,0:T(8,128)}), f32[96,3072]{1,0:T(8,128)}) %reduce-scatter.15.cloned.1.call-update) | async-done | bytes 1179664 | tf_op jit(solution)/shard_map/while/body/eval_jaxpr/reduce_scatter | solution.py:110
  1726.1 6.0 add_bitcast_fusion.3
  1734.0 25.0 %all-reduce.45 = (bf16[768]{0:T(1024)(128)(2,1)S(1)}, bf16[768]{0:T(1024)(128)(2,1)S(1)}, bf16[768]{0:T(1024)(128)(2,1)S(1)}, bf16[768]{0:T(1024)(128)(2,1)S(1)}...) all-reduce(f32[768]{0:T(1024)S(1)} %get-tuple-element.1666, ...), channel_id=2, replica_groups=mesh['wide'=8,'narrow'=4] {'wide'}, use_global_device_ids=true, to_apply=%region_17.17.clone | all-reduce | flops 9984 | bytes 59904 | tf_op jit(solution)/shard_map/while
  1762.2 12.0 all-reduce.46
  1776.5 26.1 %all-reduce.50.cloned.1.call-done = (bf16[96,768]{1,0:T(8,128)(2,1)}, bf16[96,768]{1,0:T(8,128)(2,1)}, bf16[96,768]{1,0:T(8,128)(2,1)}, bf16[96,768]{1,0:T(8,128...) async-done(((bf16[96,768]{1,0:T(8,128)(2,1)}, bf16[96,768]{1,0:T(8,128)(2,1)}, bf16[96,768]{1,0:T(8,128)(2,1)}, bf16[96,768]{1,0:T(8,128)(2,1)}, ...) | async-done | bytes 1769488 | tf_op jit(solution)/shard_map/while/body/eval_jaxpr/psum | solution.py:118
  (954 shorter events, 719.0 us)
Async XLA Ops:
  9.3 53.4 %all-gather.20.cloned.1.call-start = ((), (), s32[]{:S(2)}) async-start(), calls=%async_computation.7 | async-start | bytes 1327104 | tf_op jit(solution)/shard_map/while/body/eval_jaxpr/all_gather | solution.py:79
  10.0 57.3 %all-gather.18.cloned.1.call-start = ((), (), s32[]{:S(2)}) async-start(), calls=%async_computation.6 | async-start | bytes 1327104 | tf_op jit(solution)/shard_map/while/body/eval_jaxpr/all_gather | solution.py:81
  10.8 79.7 %all-gather.22.cloned.1.call-start = ((), (), s32[]{:S(2)}) async-start(), calls=%async_computation.8 | async-start | bytes 1327104 | tf_op jit(solution)/shard_map/while/body/eval_jaxpr/all_gather | solution.py:83
  11.5 138.8 %all-gather.24.cloned.1.call-start = ((), (), s32[]{:S(2)}) async-start(), calls=%async_computation.9 | async-start | bytes 1327104 | tf_op jit(solution)/shard_map/while/body/eval_jaxpr/all_gather | solution.py:85
  12.1 144.6 %all-gather.26.cloned.1.call-start = ((), (), s32[]{:S(2)}) async-start(), calls=%async_computation.10 | async-start | bytes 5308416 | tf_op jit(solution)/shard_map/while/body/eval_jaxpr/all_gather | solution.py:89
  12.7 184.6 %all-gather.28.cloned.1.call-start = ((), (), s32[]{:S(2)}) async-start(), calls=%async_computation.11 | async-start | bytes 5308416 | tf_op jit(solution)/shard_map/while/body/eval_jaxpr/all_gather | solution.py:91
  13.2 232.5 %all-gather.34.cloned.1.call-start = ((), (), s32[]{:S(2)}) async-start(), calls=%async_computation.14 | async-start | bytes 5308416 | tf_op jit(solution)/shard_map/while/body/eval_jaxpr/all_gather | solution.py:91
  52.7 97.6 %copy-start = (bf16[1,1024,768]{1,2,0:T(8,128)(2,1)}, bf16[1,1024,768]{1,2,0:T(8,128)(2,1)S(1)}, u32[]{:S(2)}) copy-start(bf16[1,1024,768]{1,2,0:T(8,128)(2,1)S(1)} %copy.145) | copy-start | bytes 4718596 | tf_op jit(solution)/shard_map/while
  53.5 94.4 %copy-start.36 = (f32[1024]{0:T(1024)}, f32[1024]{0:T(1024)S(1)}, u32[]{:S(2)}) copy-start(f32[1024]{0:T(1024)S(1)} %compare_convert_fusion.3) | copy-start | bytes 12292 | tf_op jit(solution)/shard_map/while
  206.8 79.6 %all-gather.36.cloned.1.call-start = ((), (), s32[]{:S(2)}) async-start(), calls=%async_computation.15 | async-start | bytes 5308416 | tf_op jit(solution)/shard_map/while/body/eval_jaxpr/all_gather | solution.py:89
  207.6 104.7 %all-gather.32.cloned.1.call-start = ((), (), s32[]{:S(2)}) async-start(), calls=%async_computation.13 | async-start | bytes 1327104 | tf_op jit(solution)/shard_map/while/body/eval_jaxpr/all_gather | solution.py:85
  208.3 321.2 %all-gather.40.cloned.1.call-start = ((), (), s32[]{:S(2)}) async-start(), calls=%async_computation.17 | async-start | bytes 1327104 | tf_op jit(solution)/shard_map/while/body/eval_jaxpr/all_gather | solution.py:81
  208.9 325.4 %all-gather.38.cloned.1.call-start = ((), (), s32[]{:S(2)}) async-start(), calls=%async_computation.16 | async-start | bytes 1327104 | tf_op jit(solution)/shard_map/while/body/eval_jaxpr/all_gather | solution.py:79
  209.6 329.5 %all-gather.30.cloned.1.call-start = ((), (), s32[]{:S(2)}) async-start(), calls=%async_computation.12 | async-start | bytes 1327104 | tf_op jit(solution)/shard_map/while/body/eval_jaxpr/all_gather | solution.py:83
  216.4 331.2 %reduce-scatter.9.cloned.1.call-start = ((), (), s32[]{:S(2)}) async-start(), calls=%async_computation.19 | async-start | bytes 2654208 | tf_op jit(solution)/shard_map/while/body/eval_jaxpr/reduce_scatter | solution.py:102
  322.6 148.0 %copy-start.26 = (f32[64,384]{0,1:T(8,128)S(1)}, f32[64,384]{0,1:T(8,128)}, u32[]{:S(2)}) copy-start(f32[64,384]{0,1:T(8,128)} %get-tuple-element.1969) | copy-start | bytes 294916 | tf_op jit(solution)/shard_map/while
  470.6 68.5 %copy-start.10 = (bf16[12,1024,64]{1,2,0:T(8,128)(2,1)}, bf16[12,1024,64]{1,2,0:T(8,128)(2,1)S(1)}, u32[]{:S(2)}) copy-start(bf16[12,1024,64]{1,2,0:T(8,128)(2,1)S(1)} %get-tuple-element.1653) | copy-start | bytes 4718596 | tf_op jit(solution)/shard_map/while
  487.4 88.1 %reduce-scatter.7.cloned.1.call-start = ((), (), s32[]{:S(2)}) async-start(), calls=%async_computation.18 | async-start | bytes 2654208 | tf_op jit(solution)/shard_map/while/body/eval_jaxpr/reduce_scatter | solution.py:100
  493.9 127.2 %reduce-scatter.13.cloned.1.call-start = ((), (), s32[]{:S(2)}) async-start(), calls=%async_computation.21 | async-start | bytes 2654208 | tf_op jit(solution)/shard_map/while/body/eval_jaxpr/reduce_scatter | solution.py:106
  498.9 167.7 %reduce-scatter.11.cloned.1.call-start = ((), (), s32[]{:S(2)}) async-start(), calls=%async_computation.20 | async-start | bytes 2654208 | tf_op jit(solution)/shard_map/while/body/eval_jaxpr/reduce_scatter | solution.py:104
  502.1 244.8 %reduce-scatter.17.cloned.1.call-start = ((), (), s32[]{:S(2)}) async-start(), calls=%async_computation.23 | async-start | bytes 10616832 | tf_op jit(solution)/shard_map/while/body/eval_jaxpr/reduce_scatter | solution.py:112
  512.0 315.0 %reduce-scatter.15.cloned.1.call-start = ((), (), s32[]{:S(2)}) async-start(), calls=%async_computation.22 | async-start | bytes 10616832 | tf_op jit(solution)/shard_map/while/body/eval_jaxpr/reduce_scatter | solution.py:110
  522.7 383.0 %all-reduce.50.cloned.1.call-start = ((), (), s32[]{:S(2)}) async-start(), calls=%async_computation.24 | async-start | bytes 3538944 | tf_op jit(solution)/shard_map/while/body/eval_jaxpr/psum | solution.py:118
  577.2 252.0 %copy-start.8 = (bf16[1,1024,768]{1,2,0:T(8,128)(2,1)S(1)}, bf16[1,1024,768]{1,2,0:T(8,128)(2,1)}, u32[]{:S(2)}) copy-start(bf16[1,1024,768]{1,2,0:T(8,128)(2,1)} %copy.151) | copy-start | bytes 4718596 | tf_op jit(solution)/shard_map/while
  910.3 51.6 %all-gather.20.cloned.1.call-start = ((), (), s32[]{:S(2)}) async-start(), calls=%async_computation.7 | async-start | bytes 1327104 | tf_op jit(solution)/shard_map/while/body/eval_jaxpr/all_gather | solution.py:79
  910.9 55.6 %all-gather.18.cloned.1.call-start = ((), (), s32[]{:S(2)}) async-start(), calls=%async_computation.6 | async-start | bytes 1327104 | tf_op jit(solution)/shard_map/while/body/eval_jaxpr/all_gather | solution.py:81
  911.6 77.2 %all-gather.22.cloned.1.call-start = ((), (), s32[]{:S(2)}) async-start(), calls=%async_computation.8 | async-start | bytes 1327104 | tf_op jit(solution)/shard_map/while/body/eval_jaxpr/all_gather | solution.py:83
  912.4 136.4 %all-gather.24.cloned.1.call-start = ((), (), s32[]{:S(2)}) async-start(), calls=%async_computation.9 | async-start | bytes 1327104 | tf_op jit(solution)/shard_map/while/body/eval_jaxpr/all_gather | solution.py:85
  913.1 141.3 %all-gather.26.cloned.1.call-start = ((), (), s32[]{:S(2)}) async-start(), calls=%async_computation.10 | async-start | bytes 5308416 | tf_op jit(solution)/shard_map/while/body/eval_jaxpr/all_gather | solution.py:89
  913.7 180.7 %all-gather.28.cloned.1.call-start = ((), (), s32[]{:S(2)}) async-start(), calls=%async_computation.11 | async-start | bytes 5308416 | tf_op jit(solution)/shard_map/while/body/eval_jaxpr/all_gather | solution.py:91
  914.4 228.5 %all-gather.34.cloned.1.call-start = ((), (), s32[]{:S(2)}) async-start(), calls=%async_computation.14 | async-start | bytes 5308416 | tf_op jit(solution)/shard_map/while/body/eval_jaxpr/all_gather | solution.py:91
  952.0 96.8 %copy-start = (bf16[1,1024,768]{1,2,0:T(8,128)(2,1)}, bf16[1,1024,768]{1,2,0:T(8,128)(2,1)S(1)}, u32[]{:S(2)}) copy-start(bf16[1,1024,768]{1,2,0:T(8,128)(2,1)S(1)} %copy.145) | copy-start | bytes 4718596 | tf_op jit(solution)/shard_map/while
  952.8 93.6 %copy-start.36 = (f32[1024]{0:T(1024)}, f32[1024]{0:T(1024)S(1)}, u32[]{:S(2)}) copy-start(f32[1024]{0:T(1024)S(1)} %compare_convert_fusion.3) | copy-start | bytes 12292 | tf_op jit(solution)/shard_map/while
  1104.0 79.5 %all-gather.36.cloned.1.call-start = ((), (), s32[]{:S(2)}) async-start(), calls=%async_computation.15 | async-start | bytes 5308416 | tf_op jit(solution)/shard_map/while/body/eval_jaxpr/all_gather | solution.py:89
  1104.5 104.7 %all-gather.32.cloned.1.call-start = ((), (), s32[]{:S(2)}) async-start(), calls=%async_computation.13 | async-start | bytes 1327104 | tf_op jit(solution)/shard_map/while/body/eval_jaxpr/all_gather | solution.py:85
  1105.3 321.1 %all-gather.40.cloned.1.call-start = ((), (), s32[]{:S(2)}) async-start(), calls=%async_computation.17 | async-start | bytes 1327104 | tf_op jit(solution)/shard_map/while/body/eval_jaxpr/all_gather | solution.py:81
  1106.0 325.2 %all-gather.38.cloned.1.call-start = ((), (), s32[]{:S(2)}) async-start(), calls=%async_computation.16 | async-start | bytes 1327104 | tf_op jit(solution)/shard_map/while/body/eval_jaxpr/all_gather | solution.py:79
  1106.6 329.4 %all-gather.30.cloned.1.call-start = ((), (), s32[]{:S(2)}) async-start(), calls=%async_computation.12 | async-start | bytes 1327104 | tf_op jit(solution)/shard_map/while/body/eval_jaxpr/all_gather | solution.py:83
  1113.3 331.2 %reduce-scatter.9.cloned.1.call-start = ((), (), s32[]{:S(2)}) async-start(), calls=%async_computation.19 | async-start | bytes 2654208 | tf_op jit(solution)/shard_map/while/body/eval_jaxpr/reduce_scatter | solution.py:102
  1219.6 147.7 %copy-start.26 = (f32[64,384]{0,1:T(8,128)S(1)}, f32[64,384]{0,1:T(8,128)}, u32[]{:S(2)}) copy-start(f32[64,384]{0,1:T(8,128)} %get-tuple-element.1969) | copy-start | bytes 294916 | tf_op jit(solution)/shard_map/while
  1367.3 68.8 %copy-start.10 = (bf16[12,1024,64]{1,2,0:T(8,128)(2,1)}, bf16[12,1024,64]{1,2,0:T(8,128)(2,1)S(1)}, u32[]{:S(2)}) copy-start(bf16[12,1024,64]{1,2,0:T(8,128)(2,1)S(1)} %get-tuple-element.1653) | copy-start | bytes 4718596 | tf_op jit(solution)/shard_map/while
  1384.0 88.0 %reduce-scatter.7.cloned.1.call-start = ((), (), s32[]{:S(2)}) async-start(), calls=%async_computation.18 | async-start | bytes 2654208 | tf_op jit(solution)/shard_map/while/body/eval_jaxpr/reduce_scatter | solution.py:100
  1390.6 127.2 %reduce-scatter.13.cloned.1.call-start = ((), (), s32[]{:S(2)}) async-start(), calls=%async_computation.21 | async-start | bytes 2654208 | tf_op jit(solution)/shard_map/while/body/eval_jaxpr/reduce_scatter | solution.py:106
  1395.6 167.9 %reduce-scatter.11.cloned.1.call-start = ((), (), s32[]{:S(2)}) async-start(), calls=%async_computation.20 | async-start | bytes 2654208 | tf_op jit(solution)/shard_map/while/body/eval_jaxpr/reduce_scatter | solution.py:104
  1398.8 244.9 %reduce-scatter.17.cloned.1.call-start = ((), (), s32[]{:S(2)}) async-start(), calls=%async_computation.23 | async-start | bytes 10616832 | tf_op jit(solution)/shard_map/while/body/eval_jaxpr/reduce_scatter | solution.py:112
  1408.7 315.2 %reduce-scatter.15.cloned.1.call-start = ((), (), s32[]{:S(2)}) async-start(), calls=%async_computation.22 | async-start | bytes 10616832 | tf_op jit(solution)/shard_map/while/body/eval_jaxpr/reduce_scatter | solution.py:110
  1419.4 383.2 %all-reduce.50.cloned.1.call-start = ((), (), s32[]{:S(2)}) async-start(), calls=%async_computation.24 | async-start | bytes 3538944 | tf_op jit(solution)/shard_map/while/body/eval_jaxpr/psum | solution.py:118
  1473.7 252.3 %copy-start.8 = (bf16[1,1024,768]{1,2,0:T(8,128)(2,1)S(1)}, bf16[1,1024,768]{1,2,0:T(8,128)(2,1)}, u32[]{:S(2)}) copy-start(bf16[1,1024,768]{1,2,0:T(8,128)(2,1)} %copy.151) | copy-start | bytes 4718596 | tf_op jit(solution)/shard_map/while
  (142 other events, 1479.0 us)
Sparse Core Ops, SparseCore 0:
  12.0 26.7 all-gather.19
  40.6 23.9 all-gather.17
  66.5 23.9 all-gather.21
  92.2 23.9 all-gather.23
  117.9 38.7 all-gather.25
  158.4 38.7 all-gather.27
  207.0 38.7 all-gather.33
  247.7 38.7 all-gather.35
  288.4 23.9 all-gather.31
  314.0 23.9 all-gather.39
  339.9 23.9 all-gather.37
  365.6 23.9 all-gather.29
  487.5 42.3 reduce-scatter.8
  533.1 42.3 reduce-scatter.6
  578.7 42.3 reduce-scatter.12
  624.3 42.3 reduce-scatter.10
  670.0 76.7 reduce-scatter.16
  750.2 76.8 reduce-scatter.14
  829.9 75.8 all-reduce.49
  912.7 22.7 all-gather.19
  937.4 24.0 all-gather.17
  963.3 23.8 all-gather.21
  989.2 23.9 all-gather.23
  1014.8 38.7 all-gather.25
  1055.5 38.7 all-gather.27
  1104.1 38.7 all-gather.33
  1144.6 38.7 all-gather.35
  1185.3 23.9 all-gather.31
  1211.2 23.9 all-gather.39
  1236.8 23.9 all-gather.37
  1262.7 23.9 all-gather.29
  1384.2 42.3 reduce-scatter.8
  1429.7 42.3 reduce-scatter.6
  1475.4 42.3 reduce-scatter.12
  1521.1 42.3 reduce-scatter.10
  1566.9 76.8 reduce-scatter.16
  1647.1 76.8 reduce-scatter.14
  1726.8 75.7 all-reduce.49
where the time goes:
time: 1830 us; the launch traced here: 1810 us
  waiting for transfers between devices  728 us (40%)
  matrix products  639 us (35%)
  local copies, waits for them, and re-layouts  164 us (9%)
  blocking collectives  140 us (8%)
  other arithmetic  117 us (6%)
    dot_general x60, matrix products, times_transposed(): lax.dot_general(left, right, (((1,), (1,)), ((), ())), preferred_element_...  191 us
    dot_general x60, matrix products, contract_rows(): lax.dot_general(left, right, (((0,), (0,)), ((), ())), preferred_element_...  177 us
    reduce_scatter x2, waiting for transfers between devices, settle(): lax.psum_scatter(grads[14], 'wide', scatter_dimension=0, tiled=True)  157 us
    reduce_scatter x2, waiting for transfers between devices, settle(): lax.psum_scatter(grads[12], 'wide', scatter_dimension=0, tiled=True)  156 us
    while x4, blocking collectives  99.5 us
    reduce_scatter x2, waiting for transfers between devices, settle(): lax.psum_scatter(grads[6], 'wide', scatter_dimension=0, tiled=True)  88 us
    reduce_scatter x2, waiting for transfers between devices, settle(): lax.psum_scatter(grads[8], 'wide', scatter_dimension=0, tiled=True)  88 us
    dot_general x2, matrix products, run_layer(): jnp.dot(hidden_two, up_mat, preferred_element_type=jnp.float32)  76.2 us
  transfers between devices with their start and end apart: 38, of which 22 were waited for; matrix products, arithmetic and copies ran while one was open for 48% of the time, Pallas kernels for 0%

commit v1 on v0

v1 whole, which is shorter than its diff:
```python
from functools import partial
import math

import jax
import jax.numpy as jnp
from jax import lax
from jax.sharding import PartitionSpec as P

D = 768
HEADS = 12
HD = 64
FEAT = 32
SEGS = 24
BLOCK = 128

EPSILON = 1e-05
HIGHEST = lax.Precision.HIGHEST


def pieces(lens_row, seq_len):
    seg_end = jnp.cumsum(lens_row)
    seg_start = seg_end - lens_row
    places = jnp.arange(seq_len, dtype=jnp.int32)
    segment = jnp.sum((places[:, None] >= seg_end[None, :]).astype(jnp.int32), axis=1)
    slots = jnp.arange(SEGS, dtype=jnp.int32)
    begins = jnp.sum(jnp.where(segment[:, None] == slots[None, :], seg_start[None, :], 0), axis=1)
    position = places - begins
    valid = (segment < SEGS - 1).astype(jnp.float32)
    return (position, valid, segment)


def rotate(heads_field, position):
    half = HD // 2
    rates = jnp.exp(jnp.arange(half, dtype=jnp.float32) * (-2.0 * math.log(10000.0) / HD))
    angles = position.astype(jnp.float32)[:, None] * rates[None, :]
    cosine = jnp.cos(angles)[:, None, :]
    sine = jnp.sin(angles)[:, None, :]
    first = heads_field[..., :half]
    second = heads_field[..., half:]
    return jnp.concatenate(
        [first * cosine - second * sine, second * cosine + first * sine], axis=-1
    )


def featurize(rotated, features):
    table = features.reshape(HD, HEADS, FEAT)
    scores = jnp.einsum("lhe,ehm->lhm", rotated, table, precision=HIGHEST) * 0.125
    return jax.nn.elu(scores) + 1.0


def normalize(stream, gain, shift):
    average = jnp.mean(stream, axis=-1, keepdims=True)
    centered = stream - average
    variance = jnp.mean(centered * centered, axis=-1, keepdims=True)
    return centered * lax.rsqrt(variance + EPSILON) * gain + shift


def contract_rows(left, right):
    return lax.dot_general(
        left, right, (((0,), (0,)), ((), ())), preferred_element_type=jnp.float32
    )


def times_transposed(left, right):
    return lax.dot_general(
        left, right, (((1,), (1,)), ((), ())), preferred_element_type=jnp.float32
    )


def column_sums(matrix):
    return jnp.sum(matrix.astype(jnp.float32), axis=0)


def gather_rows(shard):
    return lax.all_gather(shard, "wide", axis=0, tiled=True)


def reduce_rows(full):
    share = lax.psum_scatter(full.astype(jnp.bfloat16), "wide", scatter_dimension=0, tiled=True)
    return lax.psum(share, "narrow").astype(jnp.float32)


def to_blocks(field, nseq, width):
    seq_len = field.shape[0] // nseq
    nb = seq_len // BLOCK
    return jnp.transpose(field.reshape(nseq, nb, BLOCK, HEADS, width), (0, 3, 1, 2, 4))


def from_blocks(blocks):
    nseq, heads, nb, block, width = blocks.shape
    return jnp.transpose(blocks, (0, 2, 3, 1, 4)).reshape(nseq * nb * block, heads * width)


def window(blocks, fill=0):
    pad = [(0, 0)] * blocks.ndim
    pad[-3] = (1, 0)
    prev = jnp.pad(blocks, pad, constant_values=fill)[..., :-1, :, :]
    return jnp.concatenate([prev, blocks], axis=-2)


def unwindow(win):
    own = win[..., BLOCK:, :]
    nxt = win[..., 1:, :BLOCK, :]
    pad = [(0, 0)] * win.ndim
    pad[-3] = (0, 1)
    return own + jnp.pad(nxt, pad)


def on_device(
    tokens,
    cotangent,
    lengths,
    features,
    ln1_gain,
    ln1_bias,
    q_weight,
    q_bias,
    k_weight,
    k_bias,
    v_weight,
    v_bias,
    out_weight,
    out_bias,
    ln2_gain,
    ln2_bias,
    up_weight,
    up_bias,
    down_weight,
    down_bias,
):
    nseq = lengths.shape[0]
    total = tokens.shape[0]
    seq_len = total // nseq
    nb = seq_len // BLOCK
    wide = D // ln1_gain.shape[0]

    small_shards = (ln1_gain, ln1_bias, q_bias, k_bias, v_bias, out_bias, ln2_gain, ln2_bias, down_bias, up_bias)
    small_sizes = [piece.shape[0] for piece in small_shards]
    small_all = gather_rows(jnp.concatenate(small_shards)[None, :]).astype(jnp.float32)
    smalls = []
    offset = 0
    for size in small_sizes:
        smalls.append(small_all[:, offset:offset + size].reshape(wide * size))
        offset += size
    g1, b1, bq, bk, bv, bo, g2, b2, bd, bu = smalls
    qkv_mat = gather_rows(jnp.concatenate([q_weight, k_weight, v_weight], axis=1))
    proj_mat = gather_rows(out_weight)
    up_mat = gather_rows(up_weight)
    down_mat = gather_rows(down_weight)

    position, valid, segment = jax.vmap(partial(pieces, seq_len=seq_len))(lengths)
    position = position.reshape(total)
    valid_tok = valid.reshape(total)
    seg_blocks = segment.reshape(nseq, nb, BLOCK)
    seg_win = window(seg_blocks[..., None], fill=-1)[..., 0]
    rel_q = jnp.arange(BLOCK, dtype=jnp.int32)[:, None]
    rel_k = jnp.arange(2 * BLOCK, dtype=jnp.int32)[None, :]
    allowed = (rel_k <= rel_q + BLOCK)[None, None] & (
        seg_win[:, :, None, :] == seg_blocks[:, :, :, None]
    )
    allowed = allowed[:, None]
    valid_blk = valid.reshape(nseq, 1, nb, BLOCK, 1)

    stream = tokens.astype(jnp.float32)
    normed_one, norm_one_back = jax.vjp(normalize, stream, g1, b1)
    hidden_one = normed_one.astype(jnp.bfloat16)
    qkv = jnp.dot(hidden_one, qkv_mat, preferred_element_type=jnp.float32)
    query_pre = qkv[:, :D] + bq
    key_pre = qkv[:, D:2 * D] + bk
    values = (qkv[:, 2 * D:] + bv).astype(jnp.bfloat16)

    def features_of(projected):
        return featurize(rotate(projected.reshape(total, HEADS, HD), position), features)

    query_feat, query_back = jax.vjp(features_of, query_pre)
    key_feat, key_back = jax.vjp(features_of, key_pre)
    pq = to_blocks(query_feat.astype(jnp.bfloat16).reshape(total, HEADS * FEAT), nseq, FEAT)
    pk = window(to_blocks(key_feat.astype(jnp.bfloat16).reshape(total, HEADS * FEAT), nseq, FEAT))
    vb = window(to_blocks(values, nseq, HD))

    scores = jnp.einsum("shnqf,shnkf->shnqk", pq, pk, preferred_element_type=jnp.float32)
    scores = jnp.where(allowed, scores, 0.0)
    denominator = jnp.sum(scores, axis=-1, keepdims=True)
    scores_low = scores.astype(jnp.bfloat16)
    numerator = jnp.einsum("shnqk,shnkd->shnqd", scores_low, vb, preferred_element_type=jnp.float32)
    mixed = numerator / denominator * valid_blk
    attended = from_blocks(mixed).astype(jnp.bfloat16)
    residual = stream + (jnp.dot(attended, proj_mat, preferred_element_type=jnp.float32) + bo)
    normed_two, norm_two_back = jax.vjp(normalize, residual, g2, b2)
    hidden_two = normed_two.astype(jnp.bfloat16)
    upper = jnp.dot(hidden_two, up_mat, preferred_element_type=jnp.float32) + bu
    activated, gelu_back = jax.vjp(partial(jax.nn.gelu, approximate=False), upper)
    act_low = activated.astype(jnp.bfloat16)
    result = residual + (jnp.dot(act_low, down_mat, preferred_element_type=jnp.float32) + bd)
    output = result.astype(jnp.bfloat16)

    upward = cotangent
    grad_out = upward.astype(jnp.float32)
    down_grad = contract_rows(act_low, upward)
    down_bias_grad = column_sums(upward)
    grad_act = times_transposed(upward, down_mat)
    grad_upper = gelu_back(grad_act)[0].astype(jnp.bfloat16)
    up_grad = contract_rows(hidden_two, grad_upper)
    up_bias_grad = column_sums(grad_upper)
    grad_hidden_two = times_transposed(grad_upper, up_mat)
    grad_residual_norm, gain_two_grad, shift_two_grad = norm_two_back(grad_hidden_two)
    grad_residual = grad_out + grad_residual_norm
    grad_proj_in = grad_residual.astype(jnp.bfloat16)
    proj_grad = contract_rows(attended, grad_proj_in)
    proj_bias_grad = column_sums(grad_proj_in)
    grad_attended = times_transposed(grad_proj_in, proj_mat)

    head_grad = to_blocks(grad_attended, nseq, HD)
    scaled = head_grad * valid_blk
    grad_num = (scaled / denominator).astype(jnp.bfloat16)
    grad_den = -jnp.sum(scaled * numerator, axis=-1, keepdims=True) / (denominator * denominator)
    grad_scores = jnp.einsum("shnqd,shnkd->shnqk", grad_num, vb, preferred_element_type=jnp.float32)
    grad_scores = (grad_scores + grad_den).astype(jnp.bfloat16)
    grad_scores = jnp.where(allowed, grad_scores, jnp.zeros((), jnp.bfloat16))
    grad_vwin = jnp.einsum("shnqk,shnqd->shnkd", scores_low, grad_num, preferred_element_type=jnp.float32)
    grad_qf = jnp.einsum("shnqk,shnkf->shnqf", grad_scores, pk, preferred_element_type=jnp.float32)
    grad_kwin = jnp.einsum("shnqk,shnqf->shnkf", grad_scores, pq, preferred_element_type=jnp.float32)
    grad_value = from_blocks(unwindow(grad_vwin)).astype(jnp.bfloat16)
    grad_qf = from_blocks(grad_qf).reshape(total, HEADS, FEAT)
    grad_kf = from_blocks(unwindow(grad_kwin)).reshape(total, HEADS, FEAT)
    grad_query = query_back(grad_qf)[0].astype(jnp.bfloat16)
    grad_key = key_back(grad_kf)[0].astype(jnp.bfloat16)
    grad_qkv = jnp.concatenate([grad_query, grad_key, grad_value], axis=1)
    qkv_grad = contract_rows(hidden_one, grad_qkv)
    qkv_bias_grad = column_sums(grad_qkv)
    grad_hidden_one = times_transposed(grad_qkv, qkv_mat)
    grad_stream_norm, gain_one_grad, shift_one_grad = norm_one_back(grad_hidden_one)
    input_grad = grad_residual + grad_stream_norm

    down_share = reduce_rows(down_grad)
    up_share = reduce_rows(up_grad)
    proj_share = reduce_rows(proj_grad)
    qkv_share = reduce_rows(qkv_grad)
    small_grads = (
        gain_one_grad,
        shift_one_grad,
        qkv_bias_grad[:D],
        qkv_bias_grad[D:2 * D],
        qkv_bias_grad[2 * D:],
        proj_bias_grad,
        gain_two_grad,
        shift_two_grad,
        down_bias_grad,
        up_bias_grad,
    )
    packed = jnp.concatenate([piece.reshape(wide, -1) for piece in small_grads], axis=1)
    packed = lax.psum_scatter(packed, "wide", scatter_dimension=0, tiled=True)
    packed = lax.psum(packed, "narrow").reshape(-1)
    small_out = []
    offset = 0
    for size in small_sizes:
        small_out.append(packed[offset:offset + size])
        offset += size
    (
        gain_one_share,
        shift_one_share,
        query_bias_share,
        key_bias_share,
        value_bias_share,
        proj_bias_share,
        gain_two_share,
        shift_two_share,
        down_bias_share,
        up_bias_share,
    ) = small_out
    return (
        output,
        input_grad,
        gain_one_share,
        shift_one_share,
        qkv_share[:, :D],
        query_bias_share,
        qkv_share[:, D:2 * D],
        key_bias_share,
        qkv_share[:, 2 * D:],
        value_bias_share,
        proj_share,
        proj_bias_share,
        gain_two_share,
        shift_two_share,
        up_share,
        up_bias_share,
        down_share,
        down_bias_share,
    )


def solution(mesh):
    in_specs = (
        P(("wide", "narrow"), None),
        P(("wide", "narrow"), None),
        P(("wide", "narrow"), None),
        P(),
        P("wide"),
        P("wide"),
        P("wide", None),
        P("wide"),
        P("wide", None),
        P("wide"),
        P("wide", None),
        P("wide"),
        P("wide", None),
        P("wide"),
        P("wide"),
        P("wide"),
        P("wide", None),
        P("wide"),
        P("wide", None),
        P("wide"),
    )
    out_specs = (
        P(("wide", "narrow"), None),
        P(("wide", "narrow"), None),
        P("wide"),
        P("wide"),
        P("wide", None),
        P("wide"),
        P("wide", None),
        P("wide"),
        P("wide", None),
        P("wide"),
        P("wide", None),
        P("wide"),
        P("wide"),
        P("wide"),
        P("wide", None),
        P("wide"),
        P("wide", None),
        P("wide"),
    )
    return jax.shard_map(
        on_device, mesh=mesh, in_specs=in_specs, out_specs=out_specs, check_vma=False
    )
```

time: 1830 us -> 706 us (0.39)
  waiting for transfers between devices: 728 us -> 105 us
  matrix products: 639 us -> 308 us
  blocking collectives: 140 us -> 63.5 us
  other arithmetic: 117 us -> 76.9 us
  local copies, waits for them, and re-layouts: 164 us -> 127 us
    reduce_scatter x12 -> x4, waiting for transfers between devices: 541 us -> 82.9 us  [reduce_rows(): lax.psum_scatter(full.astype(jnp.bfloat16), 'wide', scatter_dimension=0,...]
    dot_general x60 -> x4, matrix products: 191 us -> 60.6 us  [times_transposed(): lax.dot_general(left, right, (((1,), (1,)), ((), ())), preferred_element_...]
    dot_general x60 -> x4, matrix products: 177 us -> 50.8 us  [contract_rows(): lax.dot_general(left, right, (((0,), (0,)), ((), ())), preferred_element_...]
    all_gather x24 -> x4, waiting for transfers between devices: 121 us -> 0.03 us  [gather_rows(): return lax.all_gather(shard, 'wide', axis=0, tiled=True)]
    while x4 -> x0, blocking collectives: 99.5 us -> none
    dot_general x60 -> x10, matrix products: 235 us -> 168 us  [the longest x1 67.9 us: on_device(): upper = jnp.dot(hidden_two, up_mat, preferred_element_type=jnp.float32) + bu]
    dynamic_slice x80 -> x0, local copies, waits for them, and re-layouts: 61.7 us -> none  [the longest x72 46.5 us: run_layer(): lax.map(partial(head_backward, allowed=allowed, valid=valid), (heads_quer...]
    while x368 -> x0, local copies, waits for them, and re-layouts: 53.6 us -> none
  transfers between devices with their start and end apart: 38 -> 9, of which waited for: 22 -> 3; matrix products, arithmetic and copies ran while one was open for 48% -> 49% of each run, Pallas kernels for 0% -> 0%
where the time goes in v1:
time: 706 us; the launch traced here: 696 us
  matrix products  308 us (44%)
  local copies, waits for them, and re-layouts  127 us (18%)
  waiting for transfers between devices  105 us (15%)
  other arithmetic  76.9 us (11%)
  blocking collectives  63.5 us (9%)
  between operations  15.7 us (2%)
    reduce_scatter x4, waiting for transfers between devices, reduce_rows(): lax.psum_scatter(full.astype(jnp.bfloat16), 'wide', scatter_dimension=0,...  82.9 us
    dot_general x1, matrix products, on_device(): upper = jnp.dot(hidden_two, up_mat, preferred_element_type=jnp.float32) + bu  67.9 us
    dot_general x4, matrix products, times_transposed(): lax.dot_general(left, right, (((1,), (1,)), ((), ())), preferred_element_...  60.6 us
    dot_general x4, matrix products, contract_rows(): lax.dot_general(left, right, (((0,), (0,)), ((), ())), preferred_element_...  50.8 us
    unnamed x2, blocking collectives  50.7 us
    unnamed x147, local copies, waits for them, and re-layouts  36 us
    dot_general x4, matrix products, featurize(): jnp.einsum('lhe,ehm->lhm', rotated, table, precision=HIGHEST) * 0.125  27.8 us
    psum x1, waiting for transfers between devices, reduce_rows(): return lax.psum(share, 'narrow').astype(jnp.float32)  19.9 us
  transfers between devices with their start and end apart: 9, of which 3 were waited for; matrix products, arithmetic and copies ran while one was open for 49% of the time, Pallas kernels for 0%

profile of v1, /device:TPU:0, one launch (start us, length us, event | category | flops | bytes accessed | tf_op | source)
XLA Modules:
  0.0 695.9 jit_solution(3166410063749181828)
XLA Ops:
  14.9 6.8 concatenate.28
  22.0 26.2 %all-reduce.9 = bf16[9984]{0:T(1024)(128)(2,1)S(1)} all-reduce(bf16[9984]{0:T(1024)(128)(2,1)S(1)} %dynamic-update-slice), channel_id=2, replica_groups=mesh['wide'=8,'narrow'=4] {'wide'}, use_global_device_ids=true, to_apply=%add.9 | all-reduce | flops 9984 | bytes 39936
  55.3 4.8 copy.114
  63.0 10.4 %fusion.93 = f32[2048,2304]{1,0:T(8,128)S(1)} fusion(bf16[768,2304]{1,0:T(8,128)(2,1)} %all-gather.6.cloned.1.call-done, bf16[2048,768]{0,1:T(8,128)(2,1)S(1)} %copy.104, f32[768]{0:T(1024)S(1)} %add.190, f32[768]{0:T(1024)S(1)} %mul.332, f32[2048]{0:T(1024)S(1)} %fusion.78, f32[2048]{0:T(1024)S(1)} %broadcast_multiply_fusion.1), kind=kOutput, calls=%fused_computation.195 | convolution fusion | flops 7257194496 | bytes 25581568 | tf_op jit(solution)/shard_map/dot_general | solution.py:167
  73.4 6.2 fusion.19
  79.6 6.7 copy.105
  86.2 6.6 copy.108
  92.8 5.9 multiply_subtract_fusion.1
  98.7 6.4 fusion.42
  106.7 6.5 fusion.40
  116.6 4.8 copy.110
  128.8 8.2 %select_reduce_fusion = (f32[2,12,8,128]{3,2,1,0:T(8,128)S(1)}, bf16[2,12,8,128,256]{4,3,2,1,0:T(8,128)(2,1)}) fusion(pred[2,8,128,256]{3,2,1,0:T(8,128)(4,1)S(1)} %copy-done.28, bf16[2,12,8,128,32]{3,4,2,1,0:T(8,128)(2,1)S(1)} %bitcast.205, bf16[2,12,8,128,32]{3,4,2,1,0:T(8,128)(2,1)S(1)} %copy-done.16, bf16[2,8,128,12,32]{2,1,0,4,3:T(8,128)(2,1)S(1)} %bitcast.219), kind=kOutput, calls=%fused_computation.19 | convolution fusion | flops 427794432 | bytes 17924096 | tf_op jit(solution)/shard_map/shnqf,shnkf->shnqk/dot_general | solution.py:181
  137.0 11.0 %fusion.31 = (bf16[2,8,128,12,64]{2,4,1,3,0:T(8,128)(2,1)}, f32[2,12,8,128,64]{3,4,2,1,0:T(8,128)}) fusion(f32[2,8,128]{2,1,0:T(8,128)S(1)} %compare_convert_fusion, f32[2,8,128,12]{2,1,3,0:T(8,128)S(1)} %bitcast.234, bf16[2,12,8,128,64]{3,4,2,1,0:T(8,128)(2,1)S(1)} %bitcast.214, bf16[2,12,8,128,64]{3,4,2,1,0:T(8,128)(2,1)} %pad_slice_fusion, ...), kind=kOutput, calls=%fused_computation.63 | convolution fusion | flops 828899328 | bytes 28942336 | tf_op jit(solution)/shard_map/shnqk,shnkd->shnqd/dot_general | solution.py:185
  147.9 6.0 copy.112
  153.9 6.0 convert_element_type.147
  160.0 5.5 fusion.106
  171.4 67.9 %multiply_convert_fusion = (bf16[2048,3072]{1,0:T(8,128)(2,1)}, f32[2048,3072]{1,0:T(8,128)}, f32[2048,3072]{1,0:T(8,128)}) fusion(f32[3072]{0:T(1024)S(1)} %add.214, bf16[768,3072]{1,0:T(8,128)(2,1)} %all-gather.10.cloned.1.call-done, bf16[2048,768]{0,1:T(8,128)(2,1)} %add_convert_fusion.7.clone.4), kind=kOutput, calls=%fused_computation.5 | convolution fusion | flops 10078912512 | bytes 70791168 | tf_op jit(solution)/shard_map/dot_general | solution.py:191
  239.3 28.4 %convert_reduce_fusion = (f32[3072]{0:T(1024)}, bf16[2048,3072]{1,0:T(8,128)(2,1)}) fusion(f32[2048,3072]{1,0:T(8,128)} %get-tuple-element.103, bf16[2048,768]{1,0:T(8,128)(2,1)S(1)} %copy-done.18, bf16[3072,768]{1,0:T(8,128)(2,1)} %all-gather.12.cloned.1.call-done, f32[2048,3072]{1,0:T(8,128)} %get-tuple-element.161, f32[3072]{0:T(1024)S(1)} %add.214), kind=kOutput, calls=%fused_computation.2 | convolution fusion | flops 9770628096 | bytes 70803456 | tf_op jit(solution)/shard_map/dot_general | solution.py:65
  267.6 16.6 %fusion.108 = (f32[768]{0:T(1024)}, f32[2048,768]{1,0:T(8,128)}) fusion(bf16[2048,3072]{1,0:T(8,128)(2,1)} %get-tuple-element.167, bf16[768,3072]{1,0:T(8,128)(2,1)} %all-gather.10.cloned.1.call-done), kind=kOutput, calls=%fused_computation.205 | convolution fusion | flops 9665248256 | bytes 23596032 | tf_op jit(solution)/shard_map/dot_general | solution.py:65
  284.2 6.7 copy.115
  291.0 7.0 %multiply_reduce_fusion = (f32[768]{0:T(1024)}, f32[2048]{0:T(1024)S(1)}) fusion(f32[2048,768]{0,1:T(8,128)} %copy.115, f32[2048,768]{0,1:T(8,128)} %copy-done.2, f32[2048]{0:T(1024)S(1)} %copy-done.34, f32[2048]{0:T(1024)S(1)} %copy-done.30, f32[768]{0:T(1024)S(1)} %copy-done.49), kind=kLoop, calls=%fused_computation.65 | loop fusion | flops 11007232 | bytes 12613632 | tf_op jit(solution)/shard_map/transpose(jvp())/reduce_sum | solution.py:55
  312.4 13.3 %fusion.6 = bf16[2,12,8,128,256]{4,3,2,1,0:T(8,128)(2,1)} fusion(f32[2,12,8,128]{3,2,1,0:T(8,128)S(1)} %multiply_divide_fusion, pred[2,8,128,256]{3,2,1,0:T(8,128)(4,1)} %compare_and_fusion, bf16[2,12,8,128,64]{3,4,2,1,0:T(8,128)(2,1)S(1)} %bitcast.215, bf16[2,12,8,128,64]{3,4,2,1,0:T(8,128)(2,1)} %pad_slice_fusion, f32[2,8,128,12,64]{2,1,0,4,3:T(8,128)} %bitcast.200, ...), kind=kOutput, calls=%fused_computation.22 | convolution fusion | flops 841482240 | bytes 25894912 | tf_op jit(solution)/shard_map/shnqd,shnkd->shnqk/dot_general | solution.py:217
  325.8 9.7 %fusion.68 = f32[2,12,8,256,32]{3,4,2,1,0:T(8,128)} fusion(bf16[2,12,8,128,256]{4,3,2,1,0:T(8,128)(2,1)} %fusion.6, bf16[2,8,128,12,32]{2,1,0,4,3:T(8,128)(2,1)} %bitcast.218), kind=kOutput, calls=%fused_computation.132 | convolution fusion | flops 402653184 | bytes 20447232 | tf_op jit(solution)/shard_map/shnqk,shnqf->shnkf/dot_general | solution.py:222
  335.4 10.6 %fusion.67 = f32[2,8,128,12,32]{2,4,1,3,0:T(8,128)} fusion(bf16[2,12,8,128,256]{4,3,2,1,0:T(8,128)(2,1)} %fusion.6, bf16[2,12,8,128,32]{3,4,2,1,0:T(8,128)(2,1)S(1)} %bitcast.206, bf16[2,12,8,128,32]{3,4,2,1,0:T(8,128)(2,1)S(1)} %copy-done.17), kind=kOutput, calls=%fused_computation.130 | convolution fusion | flops 408944640 | bytes 18874368 | tf_op jit(solution)/shard_map/shnqk,shnkf->shnqf/dot_general | solution.py:221
  346.1 14.4 %fusion.32 = f32[2,12,8,256,64]{3,4,2,1,0:T(8,128)} fusion(bf16[2,12,8,128,256]{4,3,2,1,0:T(8,128)(2,1)} %get-tuple-element.156, pred[2,8,128,256]{3,2,1,0:T(8,128)(4,1)} %compare_and_fusion, f32[2,8,128,12,64]{2,1,0,4,3:T(8,128)} %bitcast.201, f32[2,12,8,128]{3,2,1,0:T(8,128)S(1)} %copy-done.37, f32[2,8,128]{2,1,0:T(8,128)S(1)} %copy-done.51), kind=kOutput, calls=%fused_computation.77 | convolution fusion | flops 816316416 | bytes 32088064 | tf_op jit(solution)/shard_map/shnqk,shnqd->shnkd/dot_general | solution.py:220
  360.5 5.5 convolution_convert_fusion.3
  370.8 4.0 copy.119
  374.8 4.5 reshape_reshape.15
  379.4 3.8 copy.118
  389.1 5.9 fusion.35
  395.2 8.5 %convolution_bitcast_fusion = f32[2048,12,64]{0,2,1:T(8,128)S(1)} fusion(f32[64,12,32]{0,2,1:T(8,128)S(1)} %bitcast.225, f32[2048,12,32]{0,2,1:T(8,128)} %reshape_reshape.15, f32[12,2048,32]{1,2,0:T(8,128)} %get-tuple-element.152), kind=kOutput, calls=%fused_computation.80 | convolution fusion | flops 610271232 | bytes 12681216 | tf_op jit(solution)/shard_map/transpose(jvp(lhe,ehm->lhm))/dot_general | solution.py:47
  403.7 6.4 convolution_bitcast_fusion.1
  416.7 4.2 copy.120
  420.9 5.8 convert_element_type.162
  426.7 13.4 %convolution_convert_fusion.2 = bf16[768,2304]{1,0:T(8,128)(2,1)} fusion(bf16[2048,768]{0,1:T(8,128)(2,1)S(1)} %copy-done.1, f32[768]{0:T(1024)S(1)} %copy-done.60, f32[768]{0:T(1024)S(1)} %copy-done.47, f32[2048]{0:T(1024)S(1)} %copy-done.45, f32[2048]{0:T(1024)S(1)} %copy-done.32, bf16[2048,768]{0,1:T(8,128)(2,1)} %convert_element_type.162, ...), kind=kOutput, calls=%fused_computation.76 | convolution fusion | flops 7287275520 | bytes 16144384 | tf_op jit(solution)/shard_map/dot_general | solution.py:59
  440.2 16.3 %convolution_convert_fusion.1 = bf16[768,3072]{1,0:T(8,128)(2,1)} fusion(bf16[2048,3072]{1,0:T(8,128)(2,1)} %get-tuple-element.167, f32[2048,768]{0,1:T(8,128)} %copy-done.2, f32[768]{0:T(1024)S(1)} %copy-done.55, f32[768]{0:T(1024)S(1)} %copy-done.49, f32[2048]{0:T(1024)S(1)} %copy-done.34, f32[2048]{0:T(1024)S(1)} %copy-done.30), kind=kOutput, calls=%fused_computation.75 | convolution fusion | flops 9673900032 | bytes 23615488 | tf_op jit(solution)/shard_map/dot_general | solution.py:59
  456.6 15.6 %convolution_convert_fusion = bf16[3072,768]{1,0:T(8,128)(2,1)} fusion(bf16[2048,3072]{1,0:T(8,128)(2,1)} %get-tuple-element.102, bf16[2048,768]{1,0:T(8,128)(2,1)} %param.21), kind=kOutput, calls=%fused_computation.74 | convolution fusion | flops 9666035712 | bytes 20447232 | tf_op jit(solution)/shard_map/dot_general | solution.py:59
  472.3 13.0 %fusion.107 = (f32[768]{0:T(1024)S(1)}, f32[2048,768]{1,0:T(8,128)}) fusion(bf16[768,2304]{1,0:T(8,128)(2,1)} %all-gather.6.cloned.1.call-done, bf16[2048,768]{0,1:T(8,128)(2,1)} %convert_element_type.162, bf16[2048,768]{0,1:T(8,128)(2,1)} %bitcast.208, bf16[2048,768]{0,1:T(8,128)(2,1)} %bitcast.211), kind=kOutput, calls=%fused_computation.204 | convolution fusion | flops 7277640704 | bytes 19270656 | tf_op jit(solution)/shard_map/dot_general | solution.py:65
  485.3 6.6 copy.121
  491.9 5.1 convert_reduce_fusion.1
  502.3 17.3 %add_convert_fusion.4 = bf16[2048,768]{0,1:T(8,128)(2,1)} fusion(f32[2048,768]{0,1:T(8,128)} %copy-done.2, bf16[2048,3072]{1,0:T(8,128)(2,1)} %get-tuple-element.102, bf16[3072,768]{1,0:T(8,128)(2,1)} %all-gather.12.cloned.1.call-done, f32[768]{0:T(1024)S(1)} %add.217), kind=kOutput, calls=%fused_computation.71 | convolution fusion | flops 9668395008 | bytes 26741760 | tf_op jit(solution)/shard_map/dot_general | solution.py:194
  519.7 25.7 %reduce-scatter.9.cloned.1.call-done = bf16[96,3072]{1,0:T(8,128)(2,1)} async-done(((bf16[768,3072]{1,0:T(8,128)(2,1)}), bf16[96,3072]{1,0:T(8,128)(2,1)}) %reduce-scatter.9.cloned.1.call-update) | async-done | bytes 589840 | tf_op jit(solution)/shard_map/reduce_scatter | solution.py:79
  545.3 57.3 %reduce-scatter.11.cloned.1.call-done = bf16[384,768]{1,0:T(8,128)(2,1)} async-done(((bf16[3072,768]{1,0:T(8,128)(2,1)}), bf16[384,768]{1,0:T(8,128)(2,1)}) %reduce-scatter.11.cloned.1.call-update) | async-done | bytes 589840 | tf_op jit(solution)/shard_map/reduce_scatter | solution.py:79
  602.9 9.0 %convert_reduce_fusion.3 = (f32[768]{0:T(1024)S(1)}, f32[2048,768]{0,1:T(8,128)}) fusion(bf16[2048,768]{0,1:T(8,128)(2,1)} %copy.114, f32[2048]{0:T(1024)S(1)} %negate_multiply_fusion.1, f32[2048]{0:T(1024)S(1)} %multiply_multiply_fusion.5, f32[2048]{0:T(1024)S(1)} %copy-done.32, bf16[2048,768]{0,1:T(8,128)(2,1)S(1)} %copy-done.1, f32[2048]{0:T(1024)S(1)} %copy-done.45, ...), kind=kLoop, calls=%fused_computation.33 | loop fusion | flops 20446464 | bytes 25212928 | tf_op jit(solution)/shard_map/reduce_sum | solution.py:71
  612.4 6.7 copy.125
  622.0 24.5 %all-reduce.10 = f32[8,1248]{1,0:T(8,128)S(1)} all-reduce(f32[8,1248]{1,0:T(8,128)S(1)} %concatenate.35), channel_id=3, replica_groups=mesh['wide'=8,'narrow'=4] {'wide'}, use_global_device_ids=true, to_apply=%region_21.22.clone | all-reduce | flops 9984 | bytes 79872
  647.1 12.8 %psum.35 = f32[1,1248]{1,0:T(1,128)S(1)} all-reduce(f32[1,1248]{1,0:T(1,128)S(1)} %constant_dynamic-slice_fusion), channel_id=1, replica_groups=mesh['wide'=8,'narrow'=4] {'narrow'}, use_global_device_ids=true, to_apply=%region_22.23 | all-reduce | flops 1248 | bytes 9984 | tf_op jit(solution)/shard_map/psum | solution.py:253
  661.3 19.9 %all-reduce.14.cloned.1.call-done = (bf16[96,2304]{1,0:T(8,128)(2,1)}, bf16[96,768]{1,0:T(8,128)(2,1)}, bf16[96,3072]{1,0:T(8,128)(2,1)}, bf16[384,768]{1,0:T(8,128)(2,1)}) async-done(((bf16[96,2304]{1,0:T(8,128)(2,1)}, bf16[96,768]{1,0:T(8,128)(2,1)}, bf16[96,3072]{1,0:T(8,128)(2,1)}, bf16[384,768]{1,0:T(8,128)(2,1)}), (bf16[96,2304]{1,0:T(8,128)(2,1)}, bf16[96,768]{1,0:T(8,128)(2,1)}, ...) | async-done | bytes 1769488 | tf_op jit(solution)/shard_map/psum | solution.py:80
  (245 shorter events, 85.9 us)
Async XLA Ops:
  7.2 55.8 %all-gather.6.cloned.1.call-start = ((), (), s32[]{:S(2)}) async-start(), calls=%async_computation.4 | async-start | bytes 3981312 | tf_op jit(solution)/shard_map/all_gather | solution.py:75
  9.1 150.8 %all-gather.8.cloned.1.call-start = ((), (), s32[]{:S(2)}) async-start(), calls=%async_computation.5 | async-start | bytes 1327104 | tf_op jit(solution)/shard_map/all_gather | solution.py:75
  9.9 161.5 %all-gather.10.cloned.1.call-start = ((), (), s32[]{:S(2)}) async-start(), calls=%async_computation.6 | async-start | bytes 5308416 | tf_op jit(solution)/shard_map/all_gather | solution.py:75
  10.6 228.7 %all-gather.12.cloned.1.call-start = ((), (), s32[]{:S(2)}) async-start(), calls=%async_computation.7 | async-start | bytes 5308416 | tf_op jit(solution)/shard_map/all_gather | solution.py:75
  11.2 508.5 %reduce-scatter.7.cloned.1.call-start = ((), (), s32[]{:S(2)}) async-start(), calls=%async_computation.9 | async-start | bytes 1327104 | tf_op jit(solution)/shard_map/reduce_scatter | solution.py:79
  12.9 124.0 %copy-start.50 = (f32[2,8,128]{2,1,0:T(8,128)}, f32[2,8,128]{2,1,0:T(8,128)S(1)}, u32[]{:S(2)}) copy-start(f32[2,8,128]{2,1,0:T(8,128)S(1)} %compare_convert_fusion) | copy-start | bytes 24580
  52.2 107.7 %copy-start = (bf16[2048,768]{0,1:T(8,128)(2,1)}, bf16[2048,768]{0,1:T(8,128)(2,1)S(1)}, u32[]{:S(2)}) copy-start(bf16[2048,768]{0,1:T(8,128)(2,1)S(1)} %copy.104) | copy-start | bytes 9437188
  52.7 20.6 %copy-start.31 = (f32[2048]{0:T(1024)}, f32[2048]{0:T(1024)S(1)}, u32[]{:S(2)}) copy-start(f32[2048]{0:T(1024)S(1)} %broadcast_multiply_fusion.1) | copy-start | bytes 24580
  53.6 19.8 %copy-start.44 = (f32[2048]{0:T(1024)}, f32[2048]{0:T(1024)S(1)}, u32[]{:S(2)}) copy-start(f32[2048]{0:T(1024)S(1)} %fusion.78) | copy-start | bytes 24580
  53.7 19.7 %copy-start.46 = (f32[768]{0:T(1024)}, f32[768]{0:T(1024)S(1)}, u32[]{:S(2)}) copy-start(f32[768]{0:T(1024)S(1)} %mul.332) | copy-start | bytes 9220
  53.8 19.6 %copy-start.59 = (f32[768]{0:T(1024)}, f32[768]{0:T(1024)S(1)}, u32[]{:S(2)}) copy-start(f32[768]{0:T(1024)S(1)} %add.190) | copy-start | bytes 9220
  55.2 112.1 %copy-start.48 = (f32[768]{0:T(1024)}, f32[768]{0:T(1024)S(1)}, u32[]{:S(2)}) copy-start(f32[768]{0:T(1024)S(1)} %mul.358) | copy-start | bytes 9220
  55.3 112.0 %copy-start.54 = (f32[768]{0:T(1024)}, f32[768]{0:T(1024)S(1)}, u32[]{:S(2)}) copy-start(f32[768]{0:T(1024)S(1)} %add.211) | copy-start | bytes 9220
  61.8 31.0 %copy-start.23 = (f32[2048,32]{0,1:T(8,128)}, f32[2048,32]{0,1:T(8,128)S(1)}, u32[]{:S(2)}) copy-start(f32[2048,32]{0,1:T(8,128)S(1)} %get-tuple-element.136) | copy-start | bytes 786436
  125.4 11.6 %copy-start.13 = (bf16[2,8,128,12,64]{2,4,1,3,0:T(8,128)(2,1)}, bf16[2,8,128,12,64]{2,4,1,3,0:T(8,128)(2,1)S(1)}, u32[]{:S(2)}) copy-start(bf16[2,8,128,12,64]{2,4,1,3,0:T(8,128)(2,1)S(1)} %copy.159) | copy-start | bytes 9437188
  137.0 11.0 %copy-start.36 = (f32[2,12,8,128]{3,2,1,0:T(8,128)}, f32[2,12,8,128]{3,2,1,0:T(8,128)S(1)}, u32[]{:S(2)}) copy-start(f32[2,12,8,128]{3,2,1,0:T(8,128)S(1)} %get-tuple-element.155) | copy-start | bytes 294916
  171.4 67.9 %copy-start.18 = (bf16[2048,768]{1,0:T(8,128)(2,1)S(1)}, bf16[2048,768]{1,0:T(8,128)(2,1)}, u32[]{:S(2)}) copy-start(bf16[2048,768]{1,0:T(8,128)(2,1)} %param.21) | copy-start | bytes 9437188
  284.2 6.7 copy-start.30
  284.2 6.7 copy-start.34
  284.2 6.7 copy-start.49
  284.2 13.8 %slice-start = ((s8[6291456]{0:T(1024)(128)(4,1)}), s8[2097152]{0:T(1024)(128)(4,1)S(1)}, s32[]{:S(2)}) async-start(s8[6291456]{0:T(1024)(128)(4,1)} %bitcast.197), calls=%async_computation.13 | async-start | bytes 4194304
  290.9 7.0 %copy-start.43 = (f32[2048]{0:T(1024)S(1)}, f32[2048]{0:T(1024)}, u32[]{:S(2)}) copy-start(f32[2048]{0:T(1024)} %copy-done.42) | copy-start | bytes 24580
  291.0 7.1 %slice-start.1 = ((s8[6291456]{0:T(1024)(128)(4,1)}), s8[4194304]{0:T(1024)(128)(4,1)S(1)}, s32[]{:S(2)}) async-start(s8[6291456]{0:T(1024)(128)(4,1)} %bitcast.197), calls=%async_computation.14 | async-start | bytes 8388608
  291.0 7.7 %copy-start.4 = (f32[2048,768]{0,1:T(8,128)S(1)}, f32[2048,768]{0,1:T(8,128)}, u32[]{:S(2)}) copy-start(f32[2048,768]{0,1:T(8,128)} %copy.115) | copy-start | bytes 18874372
  300.9 7.3 %slice-start.2 = ((s8[6291456]{0:T(1024)(128)(4,1)}), s8[2097152]{0:T(1024)(128)(4,1)S(1)}, s32[]{:S(2)}) async-start(s8[6291456]{0:T(1024)(128)(4,1)} %bitcast.221), calls=%async_computation.15 | async-start | bytes 4194304
  325.7 9.7 %copy-start.10 = (bf16[2,8,128,12,32]{2,4,1,3,0:T(8,128)(2,1)S(1)}, bf16[2,8,128,12,32]{2,4,1,3,0:T(8,128)(2,1)}, u32[]{:S(2)}) copy-start(bf16[2,8,128,12,32]{2,4,1,3,0:T(8,128)(2,1)} %copy-done.8) | copy-start | bytes 4718596
  325.7 9.7 %copy-start.17 = (bf16[2,12,8,128,32]{3,4,2,1,0:T(8,128)(2,1)S(1)}, bf16[2,12,8,128,32]{3,4,2,1,0:T(8,128)(2,1)}, u32[]{:S(2)}) copy-start(bf16[2,12,8,128,32]{3,4,2,1,0:T(8,128)(2,1)} %pad_slice_fusion.1) | copy-start | bytes 4718596
  346.1 14.4 %copy-start.19 = (bf16[2048,768]{0,1:T(8,128)(2,1)S(1)}, bf16[2048,768]{0,1:T(8,128)(2,1)}, u32[]{:S(2)}) copy-start(bf16[2048,768]{0,1:T(8,128)(2,1)} %convert_element_type.147) | copy-start | bytes 9437188
  370.8 8.6 %copy-start.12 = (f32[2,8,128,12,32]{2,4,1,3,0:T(8,128)S(1)}, f32[2,8,128,12,32]{2,4,1,3,0:T(8,128)}, u32[]{:S(2)}) copy-start(f32[2,8,128,12,32]{2,4,1,3,0:T(8,128)} %fusion.67) | copy-start | bytes 9437188
  395.1 124.6 %reduce-scatter.5.cloned.1.call-start = ((), (), s32[]{:S(2)}) async-start(), calls=%async_computation.8 | async-start | bytes 3981312 | tf_op jit(solution)/shard_map/reduce_scatter | solution.py:79
  395.1 8.5 %copy-start.21 = (f32[12,2048,32]{1,2,0:T(8,128)S(1)}, f32[12,2048,32]{1,2,0:T(8,128)}, u32[]{:S(2)}) copy-start(f32[12,2048,32]{1,2,0:T(8,128)} %get-tuple-element.154) | copy-start | bytes 9437188
  403.7 6.5 copy-start.24
  416.6 10.0 %copy-start.1 = (bf16[2048,768]{0,1:T(8,128)(2,1)S(1)}, bf16[2048,768]{0,1:T(8,128)(2,1)}, u32[]{:S(2)}) copy-start(bf16[2048,768]{0,1:T(8,128)(2,1)} %copy-done) | copy-start | bytes 9437188
  416.7 10.0 %copy-start.32 = (f32[2048]{0:T(1024)S(1)}, f32[2048]{0:T(1024)}, u32[]{:S(2)}) copy-start(f32[2048]{0:T(1024)} %copy-done.31) | copy-start | bytes 24580
  416.7 10.0 %copy-start.45 = (f32[2048]{0:T(1024)S(1)}, f32[2048]{0:T(1024)}, u32[]{:S(2)}) copy-start(f32[2048]{0:T(1024)} %copy-done.44) | copy-start | bytes 24580
  416.7 10.0 %copy-start.47 = (f32[768]{0:T(1024)S(1)}, f32[768]{0:T(1024)}, u32[]{:S(2)}) copy-start(f32[768]{0:T(1024)} %copy-done.46) | copy-start | bytes 9220
  416.7 10.0 %copy-start.60 = (f32[768]{0:T(1024)S(1)}, f32[768]{0:T(1024)}, u32[]{:S(2)}) copy-start(f32[768]{0:T(1024)} %copy-done.59) | copy-start | bytes 9220
  426.7 13.5 %copy-start.55 = (f32[768]{0:T(1024)S(1)}, f32[768]{0:T(1024)}, u32[]{:S(2)}) copy-start(f32[768]{0:T(1024)} %copy-done.54) | copy-start | bytes 9220
  440.1 105.2 %reduce-scatter.9.cloned.1.call-start = ((), (), s32[]{:S(2)}) async-start(), calls=%async_computation.10 | async-start | bytes 5308416 | tf_op jit(solution)/shard_map/reduce_scatter | solution.py:79
  456.5 146.1 %reduce-scatter.11.cloned.1.call-start = ((), (), s32[]{:S(2)}) async-start(), calls=%async_computation.11 | async-start | bytes 5308416 | tf_op jit(solution)/shard_map/reduce_scatter | solution.py:79
  456.6 15.7 %copy-start.56 = (f32[8,96]{1,0:T(8,128)S(1)}, f32[8,96]{1,0:T(8,128)}, u32[]{:S(2)}) copy-start(f32[8,96]{1,0:T(8,128)} %get-tuple-element.124) | copy-start | bytes 9220
  472.2 209.0 %all-reduce.14.cloned.1.call-start = ((), (), s32[]{:S(2)}) async-start(), calls=%async_computation.12 | async-start | bytes 3538944 | tf_op jit(solution)/shard_map/psum | solution.py:80
  502.3 100.5 %copy-start.39 = (f32[2048]{0:T(1024)S(1)}, f32[2048]{0:T(1024)}, u32[]{:S(2)}) copy-start(f32[2048]{0:T(1024)} %copy-done.38) | copy-start | bytes 24580
  602.8 9.3 %copy-start.52 = (f32[768]{0:T(1024)S(1)}, f32[768]{0:T(1024)}, u32[]{:S(2)}) copy-start(f32[768]{0:T(1024)} %get-tuple-element.98) | copy-start | bytes 9220
  602.8 9.3 %copy-start.53 = (f32[768]{0:T(1024)S(1)}, f32[768]{0:T(1024)}, u32[]{:S(2)}) copy-start(f32[768]{0:T(1024)} %get-tuple-element.90) | copy-start | bytes 9220
  602.9 9.4 %copy-start.58 = (f32[768]{0:T(1024)S(1)}, f32[768]{0:T(1024)}, u32[]{:S(2)}) copy-start(f32[768]{0:T(1024)} %get-tuple-element.164) | copy-start | bytes 9220
  602.9 9.5 %copy-start.57 = (f32[3072]{0:T(1024)S(1)}, f32[3072]{0:T(1024)}, u32[]{:S(2)}) copy-start(f32[3072]{0:T(1024)} %get-tuple-element.166) | copy-start | bytes 36868
  612.4 6.7 copy-start.20
  (27 other events, 95.0 us)
Sparse Core Ops, SparseCore 0:
  10.5 36.7 all-gather.5
  49.1 23.9 all-gather.7
  75.0 38.7 all-gather.9
  115.5 38.7 all-gather.11
  395.2 36.4 reduce-scatter.6
  440.2 47.7 reduce-scatter.4
  491.5 53.7 reduce-scatter.8
  548.8 53.7 reduce-scatter.10
  605.2 75.8 all-reduce.13

commit v2 on v1

--- a/solution.py
+++ b/solution.py
@@ -75,9 +75,40 @@
     return lax.all_gather(shard, "wide", axis=0, tiled=True)
 
 
+def narrow_sum(share):
+    size = lax.psum(1, "narrow")
+    steps = size.bit_length() - 1
+    assert 1 << steps == size
+    me = lax.axis_index("narrow")
+    rows = share.shape[0]
+    assert rows % size == 0
+    acc = share.astype(jnp.float32)
+    for k in range(steps):
+        half = acc.shape[0] // 2
+        upper = ((me >> k) & 1) == 1
+        lo, hi = acc[:half], acc[half:]
+        keep = jnp.where(upper, hi, lo)
+        send = jnp.where(upper, lo, hi).astype(jnp.bfloat16)
+        pairs = [(i, i ^ (1 << k)) for i in range(size)]
+        acc = keep + lax.ppermute(send, "narrow", pairs).astype(jnp.float32)
+    part = acc.astype(jnp.bfloat16)
+    for k in reversed(range(steps)):
+        upper = ((me >> k) & 1) == 1
+        pairs = [(i, i ^ (1 << k)) for i in range(size)]
+        other = lax.ppermute(part, "narrow", pairs)
+        part = jnp.where(upper, jnp.concatenate([other, part]), jnp.concatenate([part, other]))
+    return part.astype(jnp.float32)
+
+
 def reduce_rows(full):
     share = lax.psum_scatter(full.astype(jnp.bfloat16), "wide", scatter_dimension=0, tiled=True)
-    return lax.psum(share, "narrow").astype(jnp.float32)
+    return narrow_sum(share)
+
+
+def gelu_parts(upper):
+    cdf = 0.5 * (1.0 + lax.erf(upper * math.sqrt(0.5)))
+    slope = cdf + upper * jnp.exp(-0.5 * upper * upper) * (1.0 / math.sqrt(2.0 * math.pi))
+    return upper * cdf, slope
 
 
 def to_blocks(field, nseq, width):
@@ -104,6 +135,10 @@
     pad = [(0, 0)] * win.ndim
     pad[-3] = (0, 1)
     return own + jnp.pad(nxt, pad)
+
+
+def as_columns(vectors, rows):
+    return jnp.concatenate([v.reshape(rows, -1) for v in vectors], axis=1)
 
 
 def on_device(
@@ -132,25 +167,27 @@
     total = tokens.shape[0]
     seq_len = total // nseq
     nb = seq_len // BLOCK
-    wide = D // ln1_gain.shape[0]
+    shard_rows = ln1_gain.shape[0]
+    wide = D // shard_rows
 
     small_shards = (ln1_gain, ln1_bias, q_bias, k_bias, v_bias, out_bias, ln2_gain, ln2_bias, down_bias, up_bias)
-    small_sizes = [piece.shape[0] for piece in small_shards]
-    small_all = gather_rows(jnp.concatenate(small_shards)[None, :]).astype(jnp.float32)
+    small_cols = [piece.shape[0] // shard_rows for piece in small_shards]
+    query_ext = gather_rows(jnp.concatenate([q_weight, as_columns(small_shards, shard_rows)], axis=1))
+    query_mat = query_ext[:, :D]
     smalls = []
-    offset = 0
-    for size in small_sizes:
-        smalls.append(small_all[:, offset:offset + size].reshape(wide * size))
-        offset += size
+    offset = D
+    for cols in small_cols:
+        smalls.append(query_ext[:, offset:offset + cols].astype(jnp.float32).reshape(-1))
+        offset += cols
     g1, b1, bq, bk, bv, bo, g2, b2, bd, bu = smalls
-    qkv_mat = gather_rows(jnp.concatenate([q_weight, k_weight, v_weight], axis=1))
+    key_mat = gather_rows(k_weight)
+    value_mat = gather_rows(v_weight)
     proj_mat = gather_rows(out_weight)
     up_mat = gather_rows(up_weight)
     down_mat = gather_rows(down_weight)
 
     position, valid, segment = jax.vmap(partial(pieces, seq_len=seq_len))(lengths)
     position = position.reshape(total)
-    valid_tok = valid.reshape(total)
     seg_blocks = segment.reshape(nseq, nb, BLOCK)
     seg_win = window(seg_blocks[..., None], fill=-1)[..., 0]
     rel_q = jnp.arange(BLOCK, dtype=jnp.int32)[:, None]
@@ -164,10 +201,9 @@
     stream = tokens.astype(jnp.float32)
     normed_one, norm_one_back = jax.vjp(normalize, stream, g1, b1)
     hidden_one = normed_one.astype(jnp.bfloat16)
-    qkv = jnp.dot(hidden_one, qkv_mat, preferred_element_type=jnp.float32)
-    query_pre = qkv[:, :D] + bq
-    key_pre = qkv[:, D:2 * D] + bk
-    values = (qkv[:, 2 * D:] + bv).astype(jnp.bfloat16)
+    query_pre = jnp.dot(hidden_one, query_mat, preferred_element_type=jnp.float32) + bq
+    key_pre = jnp.dot(hidden_one, key_mat, preferred_element_type=jnp.float32) + bk
+    values = (jnp.dot(hidden_one, value_mat, preferred_element_type=jnp.float32) + bv).astype(jnp.bfloat16)
 
     def features_of(projected):
         return featurize(rotate(projected.reshape(total, HEADS, HD), position), features)
@@ -189,7 +225,7 @@
     normed_two, norm_two_back = jax.vjp(normalize, residual, g2, b2)
     hidden_two = normed_two.astype(jnp.bfloat16)
     upper = jnp.dot(hidden_two, up_mat, preferred_element_type=jnp.float32) + bu
-    activated, gelu_back = jax.vjp(partial(jax.nn.gelu, approximate=False), upper)
+    activated, slope = gelu_parts(upper)
     act_low = activated.astype(jnp.bfloat16)
     result = residual + (jnp.dot(act_low, down_mat, preferred_element_type=jnp.float32) + bd)
     output = result.astype(jnp.bfloat16)
@@ -197,16 +233,19 @@
     upward = cotangent
     grad_out = upward.astype(jnp.float32)
     down_grad = contract_rows(act_low, upward)
+    down_share = reduce_rows(down_grad)
     down_bias_grad = column_sums(upward)
     grad_act = times_transposed(upward, down_mat)
-    grad_upper = gelu_back(grad_act)[0].astype(jnp.bfloat16)
+    grad_upper = (grad_act * slope).astype(jnp.bfloat16)
     up_grad = contract_rows(hidden_two, grad_upper)
+    up_share = reduce_rows(up_grad)
     up_bias_grad = column_sums(grad_upper)
     grad_hidden_two = times_transposed(grad_upper, up_mat)
     grad_residual_norm, gain_two_grad, shift_two_grad = norm_two_back(grad_hidden_two)
     grad_residual = grad_out + grad_residual_norm
     grad_proj_in = grad_residual.astype(jnp.bfloat16)
     proj_grad = contract_rows(attended, grad_proj_in)
+    proj_share = reduce_rows(proj_grad)
     proj_bias_grad = column_sums(grad_proj_in)
     grad_attended = times_transposed(grad_proj_in, proj_mat)
 
@@ -218,44 +257,48 @@
     grad_scores = (grad_scores + grad_den).astype(jnp.bfloat16)
     grad_scores = jnp.where(allowed, grad_scores, jnp.zeros((), jnp.bfloat16))
     grad_vwin = jnp.einsum("shnqk,shnqd->shnkd", scores_low, grad_num, preferred_element_type=jnp.float32)
+    grad_value = from_blocks(unwindow(grad_vwin)).astype(jnp.bfloat16)
+    value_grad = contract_rows(hidden_one, grad_value)
+    value_share = reduce_rows(value_grad)
+    value_bias_grad = column_sums(grad_value)
     grad_qf = jnp.einsum("shnqk,shnkf->shnqf", grad_scores, pk, preferred_element_type=jnp.float32)
     grad_kwin = jnp.einsum("shnqk,shnqf->shnkf", grad_scores, pq, preferred_element_type=jnp.float32)
-    grad_value = from_blocks(unwindow(grad_vwin)).astype(jnp.bfloat16)
     grad_qf = from_blocks(grad_qf).reshape(total, HEADS, FEAT)
     grad_kf = from_blocks(unwindow(grad_kwin)).reshape(total, HEADS, FEAT)
+    grad_key = key_back(grad_kf)[0].astype(jnp.bfloat16)
+    key_grad = contract_rows(hidden_one, grad_key)
+    key_share = reduce_rows(key_grad)
+    key_bias_grad = column_sums(grad_key)
     grad_query = query_back(grad_qf)[0].astype(jnp.bfloat16)
-    grad_key = key_back(grad_kf)[0].astype(jnp.bfloat16)
-    grad_qkv = jnp.concatenate([grad_query, grad_key, grad_value], axis=1)
-    qkv_grad = contract_rows(hidden_one, grad_qkv)
-    qkv_bias_grad = column_sums(grad_qkv)
-    grad_hidden_one = times_transposed(grad_qkv, qkv_mat)
+    query_grad = contract_rows(hidden_one, grad_query)
+    query_bias_grad = column_sums(grad_query)
+    grad_hidden_one = (
+        times_transposed(grad_query, query_mat)
+        + times_transposed(grad_key, key_mat)
+        + times_transposed(grad_value, value_mat)
+    )
     grad_stream_norm, gain_one_grad, shift_one_grad = norm_one_back(grad_hidden_one)
     input_grad = grad_residual + grad_stream_norm
 
-    down_share = reduce_rows(down_grad)
-    up_share = reduce_rows(up_grad)
-    proj_share = reduce_rows(proj_grad)
-    qkv_share = reduce_rows(qkv_grad)
     small_grads = (
         gain_one_grad,
         shift_one_grad,
-        qkv_bias_grad[:D],
-        qkv_bias_grad[D:2 * D],
-        qkv_bias_grad[2 * D:],
+        query_bias_grad,
+        key_bias_grad,
+        value_bias_grad,
         proj_bias_grad,
         gain_two_grad,
         shift_two_grad,
         down_bias_grad,
         up_bias_grad,
     )
-    packed = jnp.concatenate([piece.reshape(wide, -1) for piece in small_grads], axis=1)
-    packed = lax.psum_scatter(packed, "wide", scatter_dimension=0, tiled=True)
-    packed = lax.psum(packed, "narrow").reshape(-1)
+    query_ext_share = reduce_rows(jnp.concatenate([query_grad, as_columns(small_grads, D)], axis=1))
+    query_share = query_ext_share[:, :D]
     small_out = []
-    offset = 0
-    for size in small_sizes:
-        small_out.append(packed[offset:offset + size])
-        offset += size
+    offset = D
+    for cols in small_cols:
+        small_out.append(query_ext_share[:, offset:offset + cols].reshape(-1))
+        offset += cols
     (
         gain_one_share,
         shift_one_share,
@@ -273,11 +316,11 @@
         input_grad,
         gain_one_share,
         shift_one_share,
-        qkv_share[:, :D],
+        query_share,
         query_bias_share,
-        qkv_share[:, D:2 * D],
+        key_share,
         key_bias_share,
-        qkv_share[:, 2 * D:],
+        value_share,
         value_bias_share,
         proj_share,
         proj_bias_share,

time: 706 us -> 656 us (0.929)
  blocking collectives: 63.5 us -> 0 us
  matrix products: 308 us -> 251 us
  waiting for transfers between devices: 105 us -> 158 us
  starting transfers between devices: 0.36 us -> 34.5 us
  local copies, waits for them, and re-layouts: 127 us -> 116 us
    unnamed x2 -> x0, blocking collectives: 50.7 us -> none
    dot_general x1, matrix products: 67.9 us -> 21.6 us  [on_device(): upper = jnp.dot(hidden_two, up_mat, preferred_element_type=jnp.float32) + bu]
    all_gather x4 -> x6, waiting for transfers between devices: 0.03 us -> 46 us  [gather_rows(): return lax.all_gather(shard, 'wide', axis=0, tiled=True)]
    ppermute x0 -> x24, starting transfers between devices: none -> 33.6 us  [the longest x12 17.7 us: narrow_sum(): acc = keep + lax.ppermute(send, 'narrow', pairs).astype(jnp.float32)]
    ppermute x0 -> x24, waiting for transfers between devices: none -> 33.5 us  [the longest x12 17.7 us: narrow_sum(): acc = keep + lax.ppermute(send, 'narrow', pairs).astype(jnp.float32)]
    psum x1 -> x0, waiting for transfers between devices: 19.9 us -> none  [reduce_rows(): return lax.psum(share, 'narrow').astype(jnp.float32)]
    add x0 -> x9, other arithmetic: none -> 14.4 us  [the longest x1 8.95 us: on_device(): input_grad = grad_residual + grad_stream_norm]
    add x9 -> x0, local copies, waits for them, and re-layouts: 13.7 us -> none  [the longest x2 6.74 us: on_device(): query_pre = qkv[:, :D] + bq]
  transfers between devices with their start and end apart: 9 -> 36, of which waited for: 3 -> 16; matrix products, arithmetic and copies ran while one was open for 49% -> 56% of each run, Pallas kernels for 0% -> 0%
where the time goes in v2:
time: 656 us; the launch traced here: 646 us
  matrix products  251 us (38%)
  waiting for transfers between devices  158 us (24%)
  local copies, waits for them, and re-layouts  116 us (18%)
  other arithmetic  70 us (11%)
  starting transfers between devices  34.5 us (5%)
  between operations  15.9 us (2%)
    reduce_scatter x6, waiting for transfers between devices, reduce_rows(): lax.psum_scatter(full.astype(jnp.bfloat16), 'wide', scatter_dimension=0,...  75.2 us
    dot_general x6, matrix products, contract_rows(): lax.dot_general(left, right, (((0,), (0,)), ((), ())), preferred_element_...  51.6 us
    dot_general x6, matrix products, times_transposed(): lax.dot_general(left, right, (((1,), (1,)), ((), ())), preferred_element_...  49.6 us
    all_gather x6, waiting for transfers between devices, gather_rows(): return lax.all_gather(shard, 'wide', axis=0, tiled=True)  46 us
    unnamed x148, local copies, waits for them, and re-layouts  41.9 us
    dot_general x4, matrix products, featurize(): jnp.einsum('lhe,ehm->lhm', rotated, table, precision=HIGHEST) * 0.125  28.4 us
    dot_general x1, matrix products, on_device(): upper = jnp.dot(hidden_two, up_mat, preferred_element_type=jnp.float32) + bu  21.6 us
    ppermute x12, waiting for transfers between devices, narrow_sum(): acc = keep + lax.ppermute(send, 'narrow', pairs).astype(jnp.float32)  17.7 us
  transfers between devices with their start and end apart: 36, of which 16 were waited for; matrix products, arithmetic and copies ran while one was open for 56% of the time, Pallas kernels for 0%

profile of v2, /device:TPU:0, one launch (start us, length us, event | category | flops | bytes accessed | tf_op | source)
XLA Modules:
  0.0 646.1 jit_solution(10862315083315045527)
XLA Ops:
  27.4 4.7 copy.222
  38.1 6.3 all-gather.7.cloned.1.call-done
  44.4 4.2 convert_reduce_fusion.1
  51.5 4.6 convolution_add_fusion.1
  56.1 14.1 %all-gather.9.cloned.1.call-done = bf16[768,768]{1,0:T(8,128)(2,1)} async-done(((bf16[96,768]{1,0:T(8,128)(2,1)}), bf16[768,768]{1,0:T(8,128)(2,1)}) %all-gather.9.cloned.1.call-update) | async-done | bytes 1179664 | tf_op jit(solution)/shard_map/all_gather | solution.py:75
  70.2 5.2 convolution_add_fusion
  79.2 6.5 %fusion.38 = (bf16[2048,12,32]{0,2,1:T(8,128)(2,1)}, f32[12,2048,32]{1,2,0:T(8,128)}) fusion(f32[64,12,32]{0,2,1:T(8,128)S(1)} %bitcast.223, f32[2048,12,32]{0,2,1:T(8,128)S(1)} %get-tuple-element.170, f32[2048,12,32]{0,2,1:T(8,128)S(1)} %get-tuple-element.171), kind=kOutput, calls=%fused_computation.78 | convolution fusion | flops 610271232 | bytes 11108352 | tf_op jit(solution)/shard_map/jvp(lhe,ehm->lhm)/dot_general | solution.py:47
  85.7 10.3 %all-gather.11.cloned.1.call-done = bf16[768,768]{1,0:T(8,128)(2,1)} async-done(((bf16[96,768]{1,0:T(8,128)(2,1)}), bf16[768,768]{1,0:T(8,128)(2,1)}) %all-gather.11.cloned.1.call-update) | async-done | bytes 1179664 | tf_op jit(solution)/shard_map/all_gather | solution.py:75
  96.1 6.8 %add_convert_fusion.5 = bf16[2048,768]{1,0:T(8,128)(2,1)} fusion(bf16[2048,768]{0,1:T(8,128)(2,1)} %copy-done.20, bf16[768,768]{1,0:T(8,128)(2,1)} %all-gather.11.cloned.1.call-done, f32[768]{0:T(1024)S(1)} %get-tuple-element.136), kind=kOutput, calls=%fused_computation.58 | convolution fusion | flops 2419064832 | bytes 7474176 | tf_op jit(solution)/shard_map/dot_general | solution.py:206
  102.9 6.5 %fusion.40 = (bf16[2048,12,32]{0,2,1:T(8,128)(2,1)S(1)}, f32[12,2048,32]{1,2,0:T(8,128)}) fusion(f32[64,12,32]{0,2,1:T(8,128)S(1)} %bitcast.224, f32[2048,12,32]{0,2,1:T(8,128)S(1)} %copy-done.19, f32[2048,12,32]{0,2,1:T(8,128)S(1)} %copy-done.18), kind=kOutput, calls=%fused_computation.83 | convolution fusion | flops 610271232 | bytes 11108352 | tf_op jit(solution)/shard_map/jvp(lhe,ehm->lhm)/dot_general | solution.py:47
  113.0 5.0 copy.218
  125.8 8.2 %select_reduce_fusion = (f32[2,12,8,128]{3,2,1,0:T(8,128)S(1)}, bf16[2,12,8,128,256]{4,3,2,1,0:T(8,128)(2,1)}) fusion(pred[2,8,128,256]{3,2,1,0:T(8,128)(4,1)S(1)} %copy-done.35, bf16[2,12,8,128,32]{3,4,2,1,0:T(8,128)(2,1)S(1)} %bitcast.204, bf16[2,12,8,128,32]{3,4,2,1,0:T(8,128)(2,1)S(1)} %pad_slice_fusion.1, bf16[2,8,128,12,32]{2,1,0,4,3:T(8,128)(2,1)S(1)} %bitcast.213), kind=kOutput, calls=%fused_computation.10 | convolution fusion | flops 427794432 | bytes 17924096 | tf_op jit(solution)/shard_map/shnqf,shnkf->shnqk/dot_general | solution.py:217
  133.9 10.2 %fusion.30 = (bf16[2,8,128,12,64]{2,4,1,3,0:T(8,128)(2,1)}, f32[2,12,8,128,64]{3,4,2,1,0:T(8,128)}) fusion(f32[2,8,128]{2,1,0:T(8,128)S(1)} %compare_convert_fusion, f32[2,8,128,12]{2,1,3,0:T(8,128)S(1)} %bitcast.234, bf16[2,12,8,128,64]{3,4,2,1,0:T(8,128)(2,1)S(1)} %bitcast.207, bf16[2,12,8,128,64]{3,4,2,1,0:T(8,128)(2,1)} %pad_slice_fusion, ...), kind=kOutput, calls=%fused_computation.46 | convolution fusion | flops 828899328 | bytes 28942336 | tf_op jit(solution)/shard_map/shnqk,shnkd->shnqd/dot_general | solution.py:221
  144.1 6.0 copy.220
  150.1 6.0 convert_element_type.285
  158.0 5.3 fusion.110
  166.0 21.6 %multiply_convert_fusion = (bf16[2048,3072]{1,0:T(8,128)(2,1)}, f32[2048,3072]{1,0:T(8,128)}) fusion(f32[3072]{0:T(1024)S(1)} %copy-done.57, bf16[768,3072]{1,0:T(8,128)(2,1)} %all-gather.15.cloned.1.call-done, f32[2048,768]{0,1:T(8,128)} %copy-done.3, f32[768]{0:T(1024)S(1)} %get-tuple-element.133, f32[768]{0:T(1024)S(1)} %get-tuple-element.134, ...), kind=kOutput, calls=%fused_computation.8 | convolution fusion | flops 9709289472 | bytes 48793600 | tf_op jit(solution)/shard_map/dot_general | solution.py:227
  187.6 15.2 %all-gather.17.cloned.1.call-done = bf16[3072,768]{1,0:T(8,128)(2,1)} async-done(((bf16[384,768]{1,0:T(8,128)(2,1)}), bf16[3072,768]{1,0:T(8,128)(2,1)}) %all-gather.17.cloned.1.call-update) | async-done | bytes 4718608 | tf_op jit(solution)/shard_map/all_gather | solution.py:75
  202.9 23.3 %fusion.112 = (bf16[3072]{0:T(1024)(128)(2,1)}, bf16[2048,3072]{1,0:T(8,128)(2,1)S(1)}) fusion(f32[2048,3072]{1,0:T(8,128)} %get-tuple-element.187, f32[3072]{0:T(1024)S(1)} %copy-done.57, bf16[2048,768]{1,0:T(8,128)(2,1)S(1)} %copy-done.11, bf16[3072,768]{1,0:T(8,128)(2,1)} %all-gather.17.cloned.1.call-done), kind=kOutput, calls=%fused_computation.244 | convolution fusion | flops 9739170816 | bytes 45631488 | tf_op jit(solution)/shard_map/dot_general | solution.py:65
  226.2 12.0 %fusion.111 = (bf16[768]{0:T(1024)(128)(2,1)S(1)}, f32[2048,768]{1,0:T(8,128)}) fusion(bf16[2048,3072]{1,0:T(8,128)(2,1)S(1)} %get-tuple-element.192, bf16[768,3072]{1,0:T(8,128)(2,1)S(1)} %copy-done.62), kind=kOutput, calls=%fused_computation.243 | convolution fusion | flops 9665248256 | bytes 23594496 | tf_op jit(solution)/shard_map/dot_general | solution.py:65
  238.2 6.7 %copy.223 = f32[2048,768]{0,1:T(8,128)} copy(f32[2048,768]{1,0:T(8,128)} %get-tuple-element.190) | data formatting | bytes 12582912 | tf_op jit(solution)/shard_map/dot_general | solution.py:65
  244.9 6.4 multiply_reduce_fusion
  263.0 3.9 convolution_bitcast_fusion.2
  266.9 4.1 copy.250
  271.0 14.5 %fusion.31 = f32[2,12,8,256,64]{3,4,2,1,0:T(8,128)} fusion(bf16[2,12,8,128,256]{4,3,2,1,0:T(8,128)(2,1)} %get-tuple-element.181, pred[2,8,128,256]{3,2,1,0:T(8,128)(4,1)S(1)} %copy-done.36, f32[2,8,128,12,64]{2,1,0,4,3:T(8,128)} %bitcast.200, f32[2,12,8,128]{3,2,1,0:T(8,128)S(1)} %copy-done.47, f32[2,8,128]{2,1,0:T(8,128)S(1)} %compare_convert_fusion), kind=kOutput, calls=%fused_computation.61 | convolution fusion | flops 816316416 | bytes 32088064 | tf_op jit(solution)/shard_map/shnqk,shnqd->shnkd/dot_general | solution.py:259
  288.6 4.3 fusion.105
  298.8 7.3 %fusion.28 = f32[2,12,8,128]{3,2,1,0:T(8,128)S(1)} fusion(f32[2,12,8,128,64]{3,4,2,1,0:T(8,128)} %get-tuple-element.183, f32[2,8,128,12,64]{2,1,0,4,3:T(8,128)} %bitcast.201, f32[2,8,128]{2,1,0:T(8,128)S(1)} %compare_convert_fusion), kind=kLoop, calls=%fused_computation.43 | loop fusion | flops 4694016 | bytes 12689408 | tf_op jit(solution)/shard_map/reduce_sum | solution.py:255
  306.2 12.5 %fusion.6 = bf16[2,12,8,128,256]{4,3,2,1,0:T(8,128)(2,1)} fusion(f32[2,12,8,128]{3,2,1,0:T(8,128)S(1)} %multiply_divide_fusion, pred[2,8,128,256]{3,2,1,0:T(8,128)(4,1)} %compare_and_fusion, bf16[2,12,8,128,64]{3,4,2,1,0:T(8,128)(2,1)} %bitcast.208, bf16[2,12,8,128,64]{3,4,2,1,0:T(8,128)(2,1)} %pad_slice_fusion, f32[2,8,128,12,64]{2,1,0,4,3:T(8,128)} %bitcast.202, ...), kind=kOutput, calls=%fused_computation.12 | convolution fusion | flops 841482240 | bytes 25894912 | tf_op jit(solution)/shard_map/shnqd,shnkd->shnqk/dot_general | solution.py:256
  318.7 10.6 %fusion.65 = f32[2,8,128,12,32]{2,4,1,3,0:T(8,128)} fusion(bf16[2,12,8,128,256]{4,3,2,1,0:T(8,128)(2,1)} %fusion.6, bf16[2,12,8,128,32]{3,4,2,1,0:T(8,128)(2,1)S(1)} %bitcast.205, bf16[2,12,8,128,32]{3,4,2,1,0:T(8,128)(2,1)S(1)} %copy-done.16), kind=kOutput, calls=%fused_computation.115 | convolution fusion | flops 408944640 | bytes 18874368 | tf_op jit(solution)/shard_map/shnqk,shnkf->shnqf/dot_general | solution.py:264
  329.3 4.1 copy.226
  335.9 6.8 %fusion.66 = f32[2,12,8,256,32]{3,4,2,1,0:T(8,128)S(1)} fusion(bf16[2,12,8,128,256]{4,3,2,1,0:T(8,128)(2,1)} %fusion.6, bf16[2,8,128,12,32]{2,1,0,4,3:T(8,128)(2,1)} %bitcast.212), kind=kOutput, calls=%fused_computation.117 | convolution fusion | flops 402653184 | bytes 20447232 | tf_op jit(solution)/shard_map/shnqk,shnqf->shnkf/dot_general | solution.py:265
  347.6 4.7 reshape_reshape.15
  352.3 5.6 convolution_convert_fusion.3
  358.1 9.0 %convolution_bitcast_fusion.1 = f32[2048,12,64]{0,2,1:T(8,128)S(1)} fusion(f32[64,12,32]{0,2,1:T(8,128)S(1)} %bitcast.225, f32[2048,12,32]{0,2,1:T(8,128)} %reshape_reshape.14, f32[12,2048,32]{1,2,0:T(8,128)} %get-tuple-element.179), kind=kOutput, calls=%fused_computation.65 | convolution fusion | flops 610271232 | bytes 12681216 | tf_op jit(solution)/shard_map/transpose(jvp(lhe,ehm->lhm))/dot_general | solution.py:47
  367.1 6.4 convolution_bitcast_fusion
  383.2 4.0 fusion.113
  398.5 6.5 %convolution_convert_fusion.5 = bf16[768,768]{0,1:T(8,128)(2,1)} fusion(bf16[2048,768]{0,1:T(8,128)(2,1)} %copy-done.20, bf16[2048,768]{0,1:T(8,128)(2,1)} %bitcast.219), kind=kOutput, calls=%fused_computation.128 | convolution fusion | flops 2416508928 | bytes 7471104 | tf_op jit(solution)/shard_map/dot_general | solution.py:59
  405.1 7.1 %concatenate.100 = bf16[768,781]{0,1:T(8,128)(2,1)} concatenate(bf16[768,768]{0,1:T(8,128)(2,1)} %convolution_convert_fusion.5, bf16[768,1]{0,1:T(2,128)(2,1)S(1)} %reshape.371, bf16[768,1]{0,1:T(2,128)(2,1)S(1)} %reshape.372, bf16[768,1]{0,1:T(2,128)(2,1)S(1)} %reshape.373, bf16[768,1]{0,1:T(2,128)(2,1)S(1)} %reshape.374, bf16[768,1]{0,1:T(2,128)(2,1)S(1)} %reshape.375, ...), dimensions={1} | concatenate | bytes 2399232 | tf_op jit(solution)/shard_map/concatenate | solution.py:295
  414.7 15.5 %convolution_convert_fusion = bf16[3072,768]{1,0:T(8,128)(2,1)} fusion(bf16[2048,3072]{1,0:T(8,128)(2,1)} %get-tuple-element.186, bf16[2048,768]{1,0:T(8,128)(2,1)} %param.21), kind=kOutput, calls=%fused_computation.59 | convolution fusion | flops 9666035712 | bytes 20447232 | tf_op jit(solution)/shard_map/dot_general | solution.py:59
  430.8 9.0 %add_add_fusion.2 = f32[2048,768]{0,1:T(8,128)} fusion(f32[2048,768]{0,1:T(8,128)} %copy-done.4, bf16[2048,768]{0,1:T(8,128)(2,1)} %copy.222, f32[2048]{0:T(1024)S(1)} %negate_multiply_fusion, f32[2048]{0:T(1024)S(1)} %copy-done.49, f32[2048]{0:T(1024)S(1)} %multiply_multiply_fusion.1, f32[2048]{0:T(1024)S(1)} %copy-done.38, ...), kind=kLoop, calls=%fused_computation.49 | loop fusion | flops 18874368 | bytes 25209856 | tf_op jit(solution)/shard_map/add | solution.py:281
  439.8 6.6 %copy.236 = f32[2048,768]{1,0:T(8,128)} copy(f32[2048,768]{0,1:T(8,128)} %add_add_fusion.2) | data formatting | bytes 12582912
  446.4 16.6 %convolution_convert_fusion.1 = bf16[768,3072]{1,0:T(8,128)(2,1)} fusion(bf16[2048,3072]{1,0:T(8,128)(2,1)} %copy-done.63, f32[2048,768]{0,1:T(8,128)} %copy-done.3, f32[768]{0:T(1024)S(1)} %copy-done.61, f32[768]{0:T(1024)S(1)} %copy-done.55, f32[2048]{0:T(1024)S(1)} %copy-done.53, f32[2048]{0:T(1024)S(1)} %copy-done.44), kind=kOutput, calls=%fused_computation.60 | convolution fusion | flops 9673900032 | bytes 23615488 | tf_op jit(solution)/shard_map/dot_general | solution.py:59
  463.8 15.4 %add_convert_fusion.3 = bf16[2048,768]{0,1:T(8,128)(2,1)S(1)} fusion(f32[2048,768]{0,1:T(8,128)} %copy-done.3, bf16[2048,3072]{1,0:T(8,128)(2,1)} %get-tuple-element.186, bf16[3072,768]{1,0:T(8,128)(2,1)} %all-gather.17.cloned.1.call-done, f32[768]{0:T(1024)S(1)} %copy-done.59), kind=kOutput, calls=%fused_computation.55 | convolution fusion | flops 9668395008 | bytes 26741760 | tf_op jit(solution)/shard_map/dot_general | solution.py:230
  512.5 20.9 %reduce-scatter.17.cloned.1.call-done = bf16[384,768]{1,0:T(8,128)(2,1)} async-done(((bf16[3072,768]{1,0:T(8,128)(2,1)}), bf16[384,768]{1,0:T(8,128)(2,1)}) %reduce-scatter.17.cloned.1.call-update) | async-done | bytes 589840 | tf_op jit(solution)/shard_map/reduce_scatter | solution.py:104
  536.1 54.4 %reduce-scatter.15.cloned.1.call-done = bf16[96,3072]{1,0:T(8,128)(2,1)} async-done(((bf16[768,3072]{1,0:T(8,128)(2,1)}), bf16[96,3072]{1,0:T(8,128)(2,1)}) %reduce-scatter.15.cloned.1.call-update) | async-done | bytes 589840 | tf_op jit(solution)/shard_map/reduce_scatter | solution.py:104
  595.9 7.6 %collective-permute-done.16 = bf16[48,3072]{1,0:T(8,128)(2,1)S(1)} collective-permute-done((bf16[48,3072]{1,0:T(8,128)(2,1)S(1)}, bf16[48,3072]{1,0:T(8,128)(2,1)S(1)}, u32[]{:S(2)}, u32[]{:S(2)}) %collective-permute-start.16) | collective-permute-done | bytes 294944 | tf_op jit(solution)/shard_map/ppermute | solution.py:93
  606.8 9.5 %collective-permute-done.17 = bf16[24,3072]{1,0:T(8,128)(2,1)S(1)} collective-permute-done((bf16[24,3072]{1,0:T(8,128)(2,1)S(1)}, bf16[24,3072]{1,0:T(8,128)(2,1)S(1)}, u32[]{:S(2)}, u32[]{:S(2)}) %collective-permute-start.17) | collective-permute-done | bytes 147488 | tf_op jit(solution)/shard_map/ppermute | solution.py:93
  632.5 5.1 collective-permute-done.19
  (340 shorter events, 162.9 us)
Async XLA Ops:
  7.2 37.2 %all-gather.7.cloned.1.call-start = ((), (), s32[]{:S(2)}) async-start(), calls=%async_computation.6 | async-start | bytes 1548288 | tf_op jit(solution)/shard_map/all_gather | solution.py:75
  16.7 53.5 %all-gather.9.cloned.1.call-start = ((), (), s32[]{:S(2)}) async-start(), calls=%async_computation.7 | async-start | bytes 1327104 | tf_op jit(solution)/shard_map/all_gather | solution.py:75
  17.5 78.6 %all-gather.11.cloned.1.call-start = ((), (), s32[]{:S(2)}) async-start(), calls=%async_computation.8 | async-start | bytes 1327104 | tf_op jit(solution)/shard_map/all_gather | solution.py:75
  18.2 139.8 %all-gather.13.cloned.1.call-start = ((), (), s32[]{:S(2)}) async-start(), calls=%async_computation.9 | async-start | bytes 1327104 | tf_op jit(solution)/shard_map/all_gather | solution.py:75
  18.8 147.1 %all-gather.15.cloned.1.call-start = ((), (), s32[]{:S(2)}) async-start(), calls=%async_computation.10 | async-start | bytes 5308416 | tf_op jit(solution)/shard_map/all_gather | solution.py:75
  19.4 183.5 %all-gather.17.cloned.1.call-start = ((), (), s32[]{:S(2)}) async-start(), calls=%async_computation.11 | async-start | bytes 5308416 | tf_op jit(solution)/shard_map/all_gather | solution.py:75
  20.0 462.3 %reduce-scatter.13.cloned.1.call-start = ((), (), s32[]{:S(2)}) async-start(), calls=%async_computation.14 | async-start | bytes 1327104 | tf_op jit(solution)/shard_map/reduce_scatter | solution.py:104
  24.9 133.1 %copy-start = (bf16[2048,768]{0,1:T(8,128)(2,1)}, bf16[2048,768]{0,1:T(8,128)(2,1)S(1)}, u32[]{:S(2)}) copy-start(bf16[2048,768]{0,1:T(8,128)(2,1)S(1)} %copy.205) | copy-start | bytes 9437188
  25.5 23.1 %copy-start.37 = (f32[2048]{0:T(1024)}, f32[2048]{0:T(1024)S(1)}, u32[]{:S(2)}) copy-start(f32[2048]{0:T(1024)S(1)} %broadcast_multiply_fusion.1) | copy-start | bytes 24580
  26.3 22.2 %copy-start.41 = (f32[2048]{0:T(1024)}, f32[2048]{0:T(1024)S(1)}, u32[]{:S(2)}) copy-start(f32[2048]{0:T(1024)S(1)} %fusion.85) | copy-start | bytes 24580
  36.9 38.6 %copy-start.27 = (f32[2048,32]{0,1:T(8,128)}, f32[2048,32]{0,1:T(8,128)S(1)}, u32[]{:S(2)}) copy-start(f32[2048,32]{0,1:T(8,128)S(1)} %get-tuple-element.172) | copy-start | bytes 786436
  48.6 117.4 %copy-start.60 = (f32[768]{0:T(1024)}, f32[768]{0:T(1024)S(1)}, u32[]{:S(2)}) copy-start(f32[768]{0:T(1024)S(1)} %get-tuple-element.133) | copy-start | bytes 9220
  48.6 202.7 %copy-start.54 = (f32[768]{0:T(1024)}, f32[768]{0:T(1024)S(1)}, u32[]{:S(2)}) copy-start(f32[768]{0:T(1024)S(1)} %get-tuple-element.134) | copy-start | bytes 9220
  163.4 88.0 %copy-start.43 = (f32[2048]{0:T(1024)}, f32[2048]{0:T(1024)S(1)}, u32[]{:S(2)}) copy-start(f32[2048]{0:T(1024)S(1)} %broadcast_multiply_fusion) | copy-start | bytes 24580
  165.9 85.4 %copy-start.52 = (f32[2048]{0:T(1024)}, f32[2048]{0:T(1024)S(1)}, u32[]{:S(2)}) copy-start(f32[2048]{0:T(1024)S(1)} %fusion.86) | copy-start | bytes 24580
  166.0 36.9 %copy-start.11 = (bf16[2048,768]{1,0:T(8,128)(2,1)S(1)}, bf16[2048,768]{1,0:T(8,128)(2,1)}, u32[]{:S(2)}) copy-start(bf16[2048,768]{1,0:T(8,128)(2,1)} %param.21) | copy-start | bytes 9437188
  202.9 23.3 %copy-start.62 = (bf16[768,3072]{1,0:T(8,128)(2,1)S(1)}, bf16[768,3072]{1,0:T(8,128)(2,1)}, u32[]{:S(2)}) copy-start(bf16[768,3072]{1,0:T(8,128)(2,1)} %all-gather.15.cloned.1.call-done) | copy-start | bytes 14155780
  238.2 13.1 %slice-start = ((s8[6291456]{0:T(1024)(128)(4,1)}), s8[2097152]{0:T(1024)(128)(4,1)S(1)}, s32[]{:S(2)}) async-start(s8[6291456]{0:T(1024)(128)(4,1)} %bitcast.198), calls=%async_computation.18 | async-start | bytes 4194304
  262.5 222.2 %reduce-scatter.11.cloned.1.call-start = ((), (), s32[]{:S(2)}) async-start(), calls=%async_computation.13 | async-start | bytes 1327104 | tf_op jit(solution)/shard_map/reduce_scatter | solution.py:104
  306.1 12.5 %copy-start.8 = (bf16[2,8,128,12,32]{2,4,1,3,0:T(8,128)(2,1)S(1)}, bf16[2,8,128,12,32]{2,4,1,3,0:T(8,128)(2,1)}, u32[]{:S(2)}) copy-start(bf16[2,8,128,12,32]{2,4,1,3,0:T(8,128)(2,1)} %copy.276) | copy-start | bytes 4718596
  358.0 128.4 %reduce-scatter.9.cloned.1.call-start = ((), (), s32[]{:S(2)}) async-start(), calls=%async_computation.12 | async-start | bytes 1327104 | tf_op jit(solution)/shard_map/reduce_scatter | solution.py:104
  383.1 105.8 %reduce-scatter.19.cloned.1.call-start = ((), (), s32[]{:S(2)}) async-start(), calls=%async_computation.17 | async-start | bytes 1548288 | tf_op jit(solution)/shard_map/reduce_scatter | solution.py:104
  414.6 118.7 %reduce-scatter.17.cloned.1.call-start = ((), (), s32[]{:S(2)}) async-start(), calls=%async_computation.16 | async-start | bytes 5308416 | tf_op jit(solution)/shard_map/reduce_scatter | solution.py:104
  430.2 160.3 %reduce-scatter.15.cloned.1.call-start = ((), (), s32[]{:S(2)}) async-start(), calls=%async_computation.15 | async-start | bytes 5308416 | tf_op jit(solution)/shard_map/reduce_scatter | solution.py:104
  483.2 7.3 %collective-permute-start.12 = (bf16[48,768]{1,0:T(8,128)(2,1)S(1)}, bf16[48,768]{1,0:T(8,128)(2,1)S(1)}, u32[]{:S(2)}, u32[]{:S(2)}) collective-permute-start(bf16[48,768]{1,0:T(8,128)(2,1)S(1)} %select_convert_fusion.8), channel_id=1, source_target_pairs={{0,1},{1,0},{2,3},{3,2},{4,5},{5,4},{6,7},{7,6},{8,9},{9,8},{10,11... | collective-permute-start | bytes 221192 | tf_op jit(solution)/shard_map/ppermute | solution.py:93
  485.8 7.3 %collective-permute-start.8 = (bf16[48,768]{1,0:T(8,128)(2,1)S(1)}, bf16[48,768]{1,0:T(8,128)(2,1)S(1)}, u32[]{:S(2)}, u32[]{:S(2)}) collective-permute-start(bf16[48,768]{1,0:T(8,128)(2,1)S(1)} %select_convert_fusion.9), channel_id=1, source_target_pairs={{0,1},{1,0},{2,3},{3,2},{4,5},{5,4},{6,7},{7,6},{8,9},{9,8},{10,11... | collective-permute-start | bytes 221192 | tf_op jit(solution)/shard_map/ppermute | solution.py:93
  487.3 6.3 collective-permute-start.4
  489.9 6.3 collective-permute-start
  490.5 6.4 collective-permute-start.13
  493.1 6.2 collective-permute-start.9
  493.7 7.0 %collective-permute-start.5 = (bf16[24,768]{1,0:T(8,128)(2,1)S(1)}, bf16[24,768]{1,0:T(8,128)(2,1)S(1)}, u32[]{:S(2)}, u32[]{:S(2)}) collective-permute-start(bf16[24,768]{1,0:T(8,128)(2,1)S(1)} %select_convert_fusion.14), channel_id=1, source_target_pairs={{0,2},{1,3},{2,0},{3,1},{4,6},{5,7},{6,4},{7,5},{8,10},{9,11},{10,... | collective-permute-start | bytes 110600 | tf_op jit(solution)/shard_map/ppermute | solution.py:93
  496.2 6.2 collective-permute-start.1
  497.0 7.1 %collective-permute-start.14 = (bf16[24,768]{1,0:T(8,128)(2,1)S(1)}, bf16[24,768]{1,0:T(8,128)(2,1)S(1)}, u32[]{:S(2)}, u32[]{:S(2)}) collective-permute-start(bf16[24,768]{1,0:T(8,128)(2,1)S(1)} %add_convert_fusion.9), channel_id=1, source_target_pairs={{0,2},{1,3},{2,0},{3,1},{4,6},{5,7},{6,4},{7,5},{8,10},{9,11},{10,... | collective-permute-start | bytes 110600 | tf_op jit(solution)/shard_map/ppermute | solution.py:98
  499.3 8.0 %collective-permute-start.10 = (bf16[24,768]{1,0:T(8,128)(2,1)S(1)}, bf16[24,768]{1,0:T(8,128)(2,1)S(1)}, u32[]{:S(2)}, u32[]{:S(2)}) collective-permute-start(bf16[24,768]{1,0:T(8,128)(2,1)S(1)} %add_convert_fusion.10), channel_id=1, source_target_pairs={{0,2},{1,3},{2,0},{3,1},{4,6},{5,7},{6,4},{7,5},{8,10},{9,11},{10,... | collective-permute-start | bytes 110600 | tf_op jit(solution)/shard_map/ppermute | solution.py:98
  500.7 6.7 %collective-permute-start.6 = (bf16[24,768]{1,0:T(8,128)(2,1)S(1)}, bf16[24,768]{1,0:T(8,128)(2,1)S(1)}, u32[]{:S(2)}, u32[]{:S(2)}) collective-permute-start(bf16[24,768]{1,0:T(8,128)(2,1)S(1)} %add_convert_fusion.11), channel_id=1, source_target_pairs={{0,2},{1,3},{2,0},{3,1},{4,6},{5,7},{6,4},{7,5},{8,10},{9,11},{10,... | collective-permute-start | bytes 110600 | tf_op jit(solution)/shard_map/ppermute | solution.py:98
  502.4 7.1 %collective-permute-start.2 = (bf16[24,781]{1,0:T(8,128)(2,1)S(1)}, bf16[24,781]{1,0:T(8,128)(2,1)S(1)}, u32[]{:S(2)}, u32[]{:S(2)}) collective-permute-start(bf16[24,781]{1,0:T(8,128)(2,1)S(1)} %add_convert_fusion.8), channel_id=1, source_target_pairs={{0,2},{1,3},{2,0},{3,1},{4,6},{5,7},{6,4},{7,5},{8,10},{9,11},{10,... | collective-permute-start | bytes 112472 | tf_op jit(solution)/shard_map/ppermute | solution.py:98
  504.1 6.1 collective-permute-start.15
  507.3 4.4 collective-permute-start.11
  507.4 109.0 %collective-permute-start.7 = (bf16[48,768]{1,0:T(8,128)(2,1)S(1)}, bf16[48,768]{1,0:T(8,128)(2,1)S(1)}, u32[]{:S(2)}, u32[]{:S(2)}) collective-permute-start(bf16[48,768]{1,0:T(8,128)(2,1)S(1)} %maximum_select_fusion.9), channel_id=1, source_target_pairs={{0,1},{1,0},{2,3},{3,2},{4,5},{5,4},{6,7},{7,6},{8,9},{9,8},{10,11... | collective-permute-start | bytes 221192 | tf_op jit(solution)/shard_map/ppermute | solution.py:98
  509.5 115.7 %collective-permute-start.3 = (bf16[48,781]{1,0:T(8,128)(2,1)S(1)}, bf16[48,781]{1,0:T(8,128)(2,1)S(1)}, u32[]{:S(2)}, u32[]{:S(2)}) collective-permute-start(bf16[48,781]{1,0:T(8,128)(2,1)S(1)} %maximum_select_fusion.8), channel_id=1, source_target_pairs={{0,1},{1,0},{2,3},{3,2},{4,5},{5,4},{6,7},{7,6},{8,9},{9,8},{10,11... | collective-permute-start | bytes 224936 | tf_op jit(solution)/shard_map/ppermute | solution.py:98
  534.5 58.7 %collective-permute-start.20 = (bf16[192,768]{1,0:T(8,128)(2,1)S(1)}, bf16[192,768]{1,0:T(8,128)(2,1)S(1)}, u32[]{:S(2)}, u32[]{:S(2)}) collective-permute-start(bf16[192,768]{1,0:T(8,128)(2,1)S(1)} %select_convert_fusion.3), channel_id=1, source_target_pairs={{0,1},{1,0},{2,3},{3,2},{4,5},{5,4},{6,7},{7,6},{8,9},{9,8},{10,11... | collective-permute-start | bytes 884744 | tf_op jit(solution)/shard_map/ppermute | solution.py:93
  591.7 11.8 %collective-permute-start.16 = (bf16[48,3072]{1,0:T(8,128)(2,1)S(1)}, bf16[48,3072]{1,0:T(8,128)(2,1)S(1)}, u32[]{:S(2)}, u32[]{:S(2)}) collective-permute-start(bf16[48,3072]{1,0:T(8,128)(2,1)S(1)} %select_convert_fusion.4), channel_id=1, source_target_pairs={{0,1},{1,0},{2,3},{3,2},{4,5},{5,4},{6,7},{7,6},{8,9},{9,8},{10,11... | collective-permute-start | bytes 884744 | tf_op jit(solution)/shard_map/ppermute | solution.py:93
  593.4 11.7 %collective-permute-start.21 = (bf16[96,768]{1,0:T(8,128)(2,1)S(1)}, bf16[96,768]{1,0:T(8,128)(2,1)S(1)}, u32[]{:S(2)}, u32[]{:S(2)}) collective-permute-start(bf16[96,768]{1,0:T(8,128)(2,1)S(1)} %select_convert_fusion.5), channel_id=1, source_target_pairs={{0,2},{1,3},{2,0},{3,1},{4,6},{5,7},{6,4},{7,5},{8,10},{9,11},{10,... | collective-permute-start | bytes 442376 | tf_op jit(solution)/shard_map/ppermute | solution.py:93
  603.6 12.6 %collective-permute-start.17 = (bf16[24,3072]{1,0:T(8,128)(2,1)S(1)}, bf16[24,3072]{1,0:T(8,128)(2,1)S(1)}, u32[]{:S(2)}, u32[]{:S(2)}) collective-permute-start(bf16[24,3072]{1,0:T(8,128)(2,1)S(1)} %select_convert_fusion.6), channel_id=1, source_target_pairs={{0,2},{1,3},{2,0},{3,1},{4,6},{5,7},{6,4},{7,5},{8,10},{9,11},{10,... | collective-permute-start | bytes 442376 | tf_op jit(solution)/shard_map/ppermute | solution.py:93
  605.2 13.7 %collective-permute-start.22 = (bf16[96,768]{1,0:T(8,128)(2,1)S(1)}, bf16[96,768]{1,0:T(8,128)(2,1)S(1)}, u32[]{:S(2)}, u32[]{:S(2)}) collective-permute-start(bf16[96,768]{1,0:T(8,128)(2,1)S(1)} %add_convert_fusion.6), channel_id=1, source_target_pairs={{0,2},{1,3},{2,0},{3,1},{4,6},{5,7},{6,4},{7,5},{8,10},{9,11},{10,... | collective-permute-start | bytes 442376 | tf_op jit(solution)/shard_map/ppermute | solution.py:98
  616.3 8.8 %collective-permute-start.18 = (bf16[24,3072]{1,0:T(8,128)(2,1)S(1)}, bf16[24,3072]{1,0:T(8,128)(2,1)S(1)}, u32[]{:S(2)}, u32[]{:S(2)}) collective-permute-start(bf16[24,3072]{1,0:T(8,128)(2,1)S(1)} %add_convert_fusion.7), channel_id=1, source_target_pairs={{0,2},{1,3},{2,0},{3,1},{4,6},{5,7},{6,4},{7,5},{8,10},{9,11},{10,... | collective-permute-start | bytes 442376 | tf_op jit(solution)/shard_map/ppermute | solution.py:98
  618.9 12.5 %collective-permute-start.23 = (bf16[192,768]{1,0:T(8,128)(2,1)S(1)}, bf16[192,768]{1,0:T(8,128)(2,1)S(1)}, u32[]{:S(2)}, u32[]{:S(2)}) collective-permute-start(bf16[192,768]{1,0:T(8,128)(2,1)S(1)} %maximum_select_fusion.3), channel_id=1, source_target_pairs={{0,1},{1,0},{2,3},{3,2},{4,5},{5,4},{6,7},{7,6},{8,9},{9,8},{10,11... | collective-permute-start | bytes 884744 | tf_op jit(solution)/shard_map/ppermute | solution.py:98
  625.2 12.5 %collective-permute-start.19 = (bf16[48,3072]{1,0:T(8,128)(2,1)S(1)}, bf16[48,3072]{1,0:T(8,128)(2,1)S(1)}, u32[]{:S(2)}, u32[]{:S(2)}) collective-permute-start(bf16[48,3072]{1,0:T(8,128)(2,1)S(1)} %maximum_select_fusion.2), channel_id=1, source_target_pairs={{0,1},{1,0},{2,3},{3,2},{4,5},{5,4},{6,7},{7,6},{8,9},{9,8},{10,11... | collective-permute-start | bytes 884744 | tf_op jit(solution)/shard_map/ppermute | solution.py:98
  (56 other events, 272.5 us)
Sparse Core Ops, SparseCore 0:
  16.9 27.5 all-gather.6
  46.3 23.8 all-gather.8
  72.1 23.9 all-gather.10
  97.8 23.9 all-gather.12
  123.5 38.7 all-gather.14
  164.1 38.7 all-gather.16
  262.7 36.6 reduce-scatter.12
  358.1 36.7 reduce-scatter.10
  398.7 36.6 reduce-scatter.8
  438.5 37.4 reduce-scatter.18
  479.5 53.7 reduce-scatter.16
  536.6 53.7 reduce-scatter.14

commit v3 on v2

--- a/solution.py
+++ b/solution.py
@@ -172,19 +172,25 @@
 
     small_shards = (ln1_gain, ln1_bias, q_bias, k_bias, v_bias, out_bias, ln2_gain, ln2_bias, down_bias, up_bias)
     small_cols = [piece.shape[0] // shard_rows for piece in small_shards]
-    query_ext = gather_rows(jnp.concatenate([q_weight, as_columns(small_shards, shard_rows)], axis=1))
-    query_mat = query_ext[:, :D]
+    first = gather_rows(
+        jnp.concatenate([q_weight, k_weight, v_weight, as_columns(small_shards, shard_rows)], axis=1)
+    )
+    query_mat = first[:, :D]
+    key_mat = first[:, D:2 * D]
+    value_mat = first[:, 2 * D:3 * D]
     smalls = []
-    offset = D
+    offset = 3 * D
     for cols in small_cols:
-        smalls.append(query_ext[:, offset:offset + cols].astype(jnp.float32).reshape(-1))
+        smalls.append(first[:, offset:offset + cols].astype(jnp.float32).reshape(-1))
         offset += cols
     g1, b1, bq, bk, bv, bo, g2, b2, bd, bu = smalls
-    key_mat = gather_rows(k_weight)
-    value_mat = gather_rows(v_weight)
-    proj_mat = gather_rows(out_weight)
-    up_mat = gather_rows(up_weight)
-    down_mat = gather_rows(down_weight)
+    ff = up_weight.shape[1]
+    second = gather_rows(
+        jnp.concatenate([out_weight, up_weight, down_weight.reshape(shard_rows, -1)], axis=1)
+    )
+    proj_mat = second[:, :D]
+    up_mat = second[:, D:D + ff]
+    down_mat = second[:, D + ff:].reshape(ff, D)
 
     position, valid, segment = jax.vmap(partial(pieces, seq_len=seq_len))(lengths)
     position = position.reshape(total)
@@ -232,22 +238,22 @@
 
     upward = cotangent
     grad_out = upward.astype(jnp.float32)
-    down_grad = contract_rows(act_low, upward)
-    down_share = reduce_rows(down_grad)
-    down_bias_grad = column_sums(upward)
     grad_act = times_transposed(upward, down_mat)
     grad_upper = (grad_act * slope).astype(jnp.bfloat16)
-    up_grad = contract_rows(hidden_two, grad_upper)
-    up_share = reduce_rows(up_grad)
-    up_bias_grad = column_sums(grad_upper)
     grad_hidden_two = times_transposed(grad_upper, up_mat)
     grad_residual_norm, gain_two_grad, shift_two_grad = norm_two_back(grad_hidden_two)
     grad_residual = grad_out + grad_residual_norm
     grad_proj_in = grad_residual.astype(jnp.bfloat16)
-    proj_grad = contract_rows(attended, grad_proj_in)
-    proj_share = reduce_rows(proj_grad)
+    grad_attended = times_transposed(grad_proj_in, proj_mat)
+    down_grad = contract_rows(act_low, upward).astype(jnp.bfloat16)
+    up_grad = contract_rows(hidden_two, grad_upper).astype(jnp.bfloat16)
+    proj_grad = contract_rows(attended, grad_proj_in).astype(jnp.bfloat16)
+    packed_one = jnp.concatenate([down_grad.reshape(D, -1), up_grad, proj_grad], axis=1)
+    packed_one, grad_attended = lax.optimization_barrier((packed_one, grad_attended))
+    scattered_one = lax.psum_scatter(packed_one, "wide", scatter_dimension=0, tiled=True)
+    down_bias_grad = column_sums(upward)
+    up_bias_grad = column_sums(grad_upper)
     proj_bias_grad = column_sums(grad_proj_in)
-    grad_attended = times_transposed(grad_proj_in, proj_mat)
 
     head_grad = to_blocks(grad_attended, nseq, HD)
     scaled = head_grad * valid_blk
@@ -258,46 +264,41 @@
     grad_scores = jnp.where(allowed, grad_scores, jnp.zeros((), jnp.bfloat16))
     grad_vwin = jnp.einsum("shnqk,shnqd->shnkd", scores_low, grad_num, preferred_element_type=jnp.float32)
     grad_value = from_blocks(unwindow(grad_vwin)).astype(jnp.bfloat16)
-    value_grad = contract_rows(hidden_one, grad_value)
-    value_share = reduce_rows(value_grad)
-    value_bias_grad = column_sums(grad_value)
     grad_qf = jnp.einsum("shnqk,shnkf->shnqf", grad_scores, pk, preferred_element_type=jnp.float32)
     grad_kwin = jnp.einsum("shnqk,shnqf->shnkf", grad_scores, pq, preferred_element_type=jnp.float32)
     grad_qf = from_blocks(grad_qf).reshape(total, HEADS, FEAT)
     grad_kf = from_blocks(unwindow(grad_kwin)).reshape(total, HEADS, FEAT)
     grad_key = key_back(grad_kf)[0].astype(jnp.bfloat16)
-    key_grad = contract_rows(hidden_one, grad_key)
-    key_share = reduce_rows(key_grad)
-    key_bias_grad = column_sums(grad_key)
     grad_query = query_back(grad_qf)[0].astype(jnp.bfloat16)
-    query_grad = contract_rows(hidden_one, grad_query)
-    query_bias_grad = column_sums(grad_query)
-    grad_hidden_one = (
-        times_transposed(grad_query, query_mat)
-        + times_transposed(grad_key, key_mat)
-        + times_transposed(grad_value, value_mat)
-    )
+    grad_qkv = jnp.concatenate([grad_query, grad_key, grad_value], axis=1)
+    scattered_one, grad_qkv = lax.optimization_barrier((scattered_one, grad_qkv))
+    share_one = narrow_sum(scattered_one)
+    grad_hidden_one = times_transposed(grad_qkv, first[:, :3 * D])
     grad_stream_norm, gain_one_grad, shift_one_grad = norm_one_back(grad_hidden_one)
     input_grad = grad_residual + grad_stream_norm
+    qkv_grad = contract_rows(hidden_one, grad_qkv)
+    qkv_bias_grad = column_sums(grad_qkv)
 
     small_grads = (
         gain_one_grad,
         shift_one_grad,
-        query_bias_grad,
-        key_bias_grad,
-        value_bias_grad,
+        qkv_bias_grad[:D],
+        qkv_bias_grad[D:2 * D],
+        qkv_bias_grad[2 * D:],
         proj_bias_grad,
         gain_two_grad,
         shift_two_grad,
         down_bias_grad,
         up_bias_grad,
     )
-    query_ext_share = reduce_rows(jnp.concatenate([query_grad, as_columns(small_grads, D)], axis=1))
-    query_share = query_ext_share[:, :D]
+    down_share = share_one[:, :ff].reshape(-1, D)
+    up_share = share_one[:, ff:2 * ff]
+    proj_share = share_one[:, 2 * ff:]
+    share_two = reduce_rows(jnp.concatenate([qkv_grad, as_columns(small_grads, D)], axis=1))
     small_out = []
-    offset = D
+    offset = 3 * D
     for cols in small_cols:
-        small_out.append(query_ext_share[:, offset:offset + cols].reshape(-1))
+        small_out.append(share_two[:, offset:offset + cols].reshape(-1))
         offset += cols
     (
         gain_one_share,
@@ -316,11 +317,11 @@
         input_grad,
         gain_one_share,
         shift_one_share,
-        query_share,
+        share_two[:, :D],
         query_bias_share,
-        key_share,
+        share_two[:, D:2 * D],
         key_bias_share,
-        value_share,
+        share_two[:, 2 * D:3 * D],
         value_bias_share,
         proj_share,
         proj_bias_share,

time: 656 us -> 629 us (0.959)
  waiting for transfers between devices: 158 us -> 76.5 us
  local copies, waits for them, and re-layouts: 116 us -> 164 us
  starting transfers between devices: 34.5 us -> 11.4 us
  other arithmetic: 70 us -> 92.8 us
  matrix products: 251 us -> 258 us
    reduce_scatter x6 -> x1, waiting for transfers between devices: 75.2 us -> 21.4 us  [reduce_rows(): lax.psum_scatter(full.astype(jnp.bfloat16), 'wide', scatter_dimension=0,...]
    all_gather x6 -> x2, waiting for transfers between devices: 46 us -> 18.8 us  [gather_rows(): return lax.all_gather(shard, 'wide', axis=0, tiled=True)]
    reshape x1 -> x5, local copies, waits for them, and re-layouts: 0.69 us -> 20.4 us  [the longest x1 8.48 us: on_device(): down_mat = second[:, D + ff:].reshape(ff, D)]
    concatenate x0 -> x3, other arithmetic: none -> 16 us  [the longest x1 9.28 us: on_device(): jnp.concatenate([down_grad.reshape(D, -1), up_grad, proj_grad], axis=1)]
    ppermute x12 -> x4, waiting for transfers between devices: 15.8 us -> 29.9 us  [narrow_sum(): other = lax.ppermute(part, 'narrow', pairs)]
    ppermute x12 -> x4, starting transfers between devices: 15.9 us -> 4.6 us  [narrow_sum(): other = lax.ppermute(part, 'narrow', pairs)]
    ppermute x12 -> x4, waiting for transfers between devices: 17.7 us -> 6.45 us  [narrow_sum(): acc = keep + lax.ppermute(send, 'narrow', pairs).astype(jnp.float32)]
    ppermute x12 -> x4, starting transfers between devices: 17.7 us -> 6.49 us  [narrow_sum(): acc = keep + lax.ppermute(send, 'narrow', pairs).astype(jnp.float32)]
  transfers between devices with their start and end apart: 36 -> 12, of which waited for: 16 -> 7; matrix products, arithmetic and copies ran while one was open for 56% -> 45% of each run, Pallas kernels for 0% -> 0%
where the time goes in v3:
time: 629 us; the launch traced here: 618 us
  matrix products  258 us (41%)
  local copies, waits for them, and re-layouts  164 us (26%)
  other arithmetic  92.8 us (15%)
  waiting for transfers between devices  76.5 us (12%)
  between operations  15.2 us (2%)
  starting transfers between devices  11.4 us (2%)
    dot_general x4, matrix products, times_transposed(): lax.dot_general(left, right, (((1,), (1,)), ((), ())), preferred_element_...  57.3 us
    dot_general x4, matrix products, contract_rows(): lax.dot_general(left, right, (((0,), (0,)), ((), ())), preferred_element_...  46.2 us
    unnamed x137, local copies, waits for them, and re-layouts  42.5 us
    ppermute x4, waiting for transfers between devices, narrow_sum(): other = lax.ppermute(part, 'narrow', pairs)  29.9 us
    dot_general x4, matrix products, featurize(): jnp.einsum('lhe,ehm->lhm', rotated, table, precision=HIGHEST) * 0.125  28.1 us
    dot_general x1, matrix products, on_device(): upper = jnp.dot(hidden_two, up_mat, preferred_element_type=jnp.float32) + bu  24 us
    reduce_scatter x1, waiting for transfers between devices, reduce_rows(): lax.psum_scatter(full.astype(jnp.bfloat16), 'wide', scatter_dimension=0,...  21.4 us
    all_gather x2, waiting for transfers between devices, gather_rows(): return lax.all_gather(shard, 'wide', axis=0, tiled=True)  18.8 us
  transfers between devices with their start and end apart: 12, of which 7 were waited for; matrix products, arithmetic and copies ran while one was open for 45% of the time, Pallas kernels for 0%

profile of v3, /device:TPU:0, one launch (start us, length us, event | category | flops | bytes accessed | tf_op | source)
XLA Modules:
  0.0 618.2 jit_solution(6670956705364769276)
XLA Ops:
  25.8 4.8 copy.122
  35.7 18.8 %all-gather.3.cloned.1.call-done = bf16[768,2317]{1,0:T(8,128)(2,1)} async-done(((bf16[96,2317]{1,0:T(8,128)(2,1)}), bf16[768,2317]{1,0:T(8,128)(2,1)}) %all-gather.3.cloned.1.call-update) | async-done | bytes 3558928 | tf_op jit(solution)/shard_map/all_gather | solution.py:75
  63.0 4.7 convolution_add_fusion.1
  70.8 6.6 %fusion.47 = (bf16[2048,12,32]{0,2,1:T(8,128)(2,1)S(1)}, f32[12,2048,32]{1,2,0:T(8,128)}) fusion(f32[64,12,32]{0,2,1:T(8,128)S(1)} %bitcast.204, f32[2048,12,32]{0,2,1:T(8,128)S(1)} %get-tuple-element.111, f32[2048,12,32]{0,2,1:T(8,128)S(1)} %get-tuple-element.110), kind=kOutput, calls=%fused_computation.92 | convolution fusion | flops 610271232 | bytes 11108352 | tf_op jit(solution)/shard_map/jvp(lhe,ehm->lhm)/dot_general | solution.py:47
  79.0 6.5 %fusion.45 = (bf16[2048,12,32]{0,2,1:T(8,128)(2,1)S(1)}, f32[12,2048,32]{1,2,0:T(8,128)}) fusion(f32[64,12,32]{0,2,1:T(8,128)S(1)} %bitcast.205, f32[2048,12,32]{0,2,1:T(8,128)S(1)} %get-tuple-element.121, f32[2048,12,32]{0,2,1:T(8,128)S(1)} %get-tuple-element.122), kind=kOutput, calls=%fused_computation.87 | convolution fusion | flops 610271232 | bytes 11108352 | tf_op jit(solution)/shard_map/jvp(lhe,ehm->lhm)/dot_general | solution.py:47
  87.5 6.7 %add_convert_fusion.5 = bf16[2048,768]{1,0:T(8,128)(2,1)} fusion(f32[768]{0:T(1024)S(1)} %get-tuple-element.88, bf16[768,2317]{1,0:T(8,128)(2,1)} %all-gather.3.cloned.1.call-done, bf16[2048,768]{0,1:T(8,128)(2,1)S(1)} %copy.105, f32[768]{0:T(1024)S(1)} %get-tuple-element.91, f32[768]{0:T(1024)S(1)} %get-tuple-element.92, f32[2048]{0:T(1024)S(1)} %fusion.91, ...), kind=kOutput, calls=%fused_computation.59 | convolution fusion | flops 2428502016 | bytes 7496704 | tf_op jit(solution)/shard_map/dot_general | solution.py:212
  94.3 4.6 copy.118
  105.8 8.3 %select_reduce_fusion = (f32[2,12,8,128]{3,2,1,0:T(8,128)S(1)}, bf16[2,12,8,128,256]{4,3,2,1,0:T(8,128)(2,1)}) fusion(pred[2,8,128,256]{3,2,1,0:T(8,128)(4,1)S(1)} %copy-done.33, bf16[2,12,8,128,32]{3,4,2,1,0:T(8,128)(2,1)S(1)} %bitcast.190, bf16[2,12,8,128,32]{3,4,2,1,0:T(8,128)(2,1)S(1)} %pad_slice_fusion.1, bf16[2,8,128,12,32]{2,1,0,4,3:T(8,128)(2,1)S(1)} %bitcast.200), kind=kOutput, calls=%fused_computation.10 | convolution fusion | flops 427794432 | bytes 17924096 | tf_op jit(solution)/shard_map/shnqf,shnkf->shnqk/dot_general | solution.py:223
  114.1 10.6 %fusion.30 = (bf16[2,8,128,12,64]{2,4,1,3,0:T(8,128)(2,1)}, f32[2,12,8,128,64]{3,4,2,1,0:T(8,128)}) fusion(f32[2,8,128]{2,1,0:T(8,128)S(1)} %compare_convert_fusion, f32[2,8,128,12]{2,1,3,0:T(8,128)S(1)} %bitcast.215, bf16[2,12,8,128,64]{3,4,2,1,0:T(8,128)(2,1)S(1)} %bitcast.195, bf16[2,12,8,128,64]{3,4,2,1,0:T(8,128)(2,1)} %pad_slice_fusion, ...), kind=kOutput, calls=%fused_computation.48 | convolution fusion | flops 828899328 | bytes 28942336 | tf_op jit(solution)/shard_map/shnqk,shnkd->shnqd/dot_general | solution.py:227
  124.7 6.0 copy.120
  130.7 5.8 convert_element_type.181
  137.8 5.3 fusion.117
  146.4 4.8 slice.241
  151.2 8.5 %reshape.377 = bf16[3072,768]{1,0:T(8,128)(2,1)} reshape(bf16[768,3072]{1,0:T(8,128)(2,1)} %slice.241) | data formatting | bytes 9437184 | tf_op jit(solution)/shard_map/reshape | solution.py:193
  159.7 24.0 %multiply_convert_fusion = (bf16[2048,3072]{1,0:T(8,128)(2,1)}, f32[2048,3072]{1,0:T(8,128)}) fusion(f32[3072]{0:T(1024)S(1)} %reshape.409, bf16[768,6912]{1,0:T(8,128)(2,1)} %all-gather.5.cloned.1.call-done, f32[2048,768]{0,1:T(8,128)} %copy-done.4, f32[768]{0:T(1024)S(1)} %copy-done.55, f32[768]{0:T(1024)S(1)} %get-tuple-element.86, f32[2048]{0:T(1024)S(1)} %fusion.92, ...), kind=kOutput, calls=%fused_computation.8 | convolution fusion | flops 9709289472 | bytes 48793600 | tf_op jit(solution)/shard_map/dot_general | solution.py:233
  183.8 22.2 %fusion.120 = (bf16[3072]{0:T(1024)(128)(2,1)}, bf16[2048,3072]{1,0:T(8,128)(2,1)}) fusion(f32[2048,3072]{1,0:T(8,128)} %get-tuple-element.141, f32[3072]{0:T(1024)S(1)} %reshape.409, bf16[3072,768]{1,0:T(8,128)(2,1)S(1)} %copy-done.22, bf16[2048,768]{1,0:T(8,128)(2,1)S(1)} %copy-done.12), kind=kOutput, calls=%fused_computation.224 | convolution fusion | flops 9739170816 | bytes 45631488 | tf_op jit(solution)/shard_map/dot_general | solution.py:65
  206.0 14.8 %convolution_convert_fusion = bf16[768,3072]{1,0:T(8,128)(2,1)} fusion(bf16[2048,3072]{1,0:T(8,128)(2,1)} %get-tuple-element.147, f32[2048,768]{0,1:T(8,128)S(1)} %bitcast.182, f32[768]{0:T(1024)S(1)} %copy-done.55, f32[768]{0:T(1024)S(1)} %get-tuple-element.86, f32[2048]{0:T(1024)S(1)} %fusion.92, f32[2048]{0:T(1024)S(1)} %broadcast_multiply_fusion), kind=kOutput, calls=%fused_computation.60 | convolution fusion | flops 9673900032 | bytes 23615488 | tf_op jit(solution)/shard_map/dot_general | solution.py:59
  220.8 14.2 %fusion.119 = (bf16[768]{0:T(1024)(128)(2,1)S(1)}, f32[2048,768]{1,0:T(8,128)}) fusion(bf16[2048,3072]{1,0:T(8,128)(2,1)S(1)} %copy-done.58, bf16[768,6912]{1,0:T(8,128)(2,1)} %all-gather.5.cloned.1.call-done), kind=kOutput, calls=%fused_computation.223 | convolution fusion | flops 9665248256 | bytes 23594496 | tf_op jit(solution)/shard_map/dot_general | solution.py:65
  234.9 6.7 %copy.123 = f32[2048,768]{0,1:T(8,128)} copy(f32[2048,768]{1,0:T(8,128)} %get-tuple-element.145) | data formatting | bytes 12582912 | tf_op jit(solution)/shard_map/dot_general | solution.py:65
  241.7 6.2 %multiply_reduce_fusion = (bf16[768]{0:T(1024)(128)(2,1)S(1)}, f32[2048]{0:T(1024)S(1)}) fusion(f32[2048,768]{0,1:T(8,128)} %copy.123, f32[2048,768]{0,1:T(8,128)} %copy-done.4, f32[2048]{0:T(1024)S(1)} %fusion.92, f32[2048]{0:T(1024)S(1)} %broadcast_multiply_fusion, f32[768]{0:T(1024)S(1)} %get-tuple-element.86), kind=kLoop, calls=%fused_computation.50 | loop fusion | flops 11007232 | bytes 12612096 | tf_op jit(solution)/shard_map/transpose(jvp())/reduce_sum | solution.py:55
  259.7 14.5 %convolution_convert_fusion.1 = bf16[3072,768]{1,0:T(8,128)(2,1)} fusion(bf16[2048,3072]{1,0:T(8,128)(2,1)} %get-tuple-element.140, bf16[2048,768]{1,0:T(8,128)(2,1)S(1)} %copy-done.13), kind=kOutput, calls=%fused_computation.61 | convolution fusion | flops 9666035712 | bytes 20447232 | tf_op jit(solution)/shard_map/dot_general | solution.py:59
  274.2 8.5 %reshape.378 = bf16[768,3072]{1,0:T(8,128)(2,1)} reshape(bf16[3072,768]{1,0:T(8,128)(2,1)} %convolution_convert_fusion.1) | data formatting | bytes 9437184 | tf_op jit(solution)/shard_map/reshape | solution.py:251
  282.7 9.3 %pad_maximum_fusion = bf16[768,6912]{1,0:T(8,128)(2,1)} fusion(bf16[768,768]{1,0:T(8,128)(2,1)} %convolution_convert_fusion.3, bf16[768,3072]{1,0:T(8,128)(2,1)} %convolution_convert_fusion, bf16[768,3072]{1,0:T(8,128)(2,1)} %reshape.378), kind=kLoop, calls=%fused_computation.13 | loop fusion | flops 31850496 | bytes 21233664 | tf_op jit(solution)/shard_map/concatenate | solution.py:251
  292.0 7.5 %fusion.86 = f32[2048,768]{1,0:T(8,128)} fusion(bf16[2048,768]{0,1:T(8,128)(2,1)} %copy-done.25, bf16[768,6912]{1,0:T(8,128)(2,1)} %all-gather.5.cloned.1.call-done), kind=kOutput, calls=%fused_computation.144 | convolution fusion | flops 2415919104 | bytes 10616832 | tf_op jit(solution)/shard_map/dot_general | solution.py:65
  301.1 7.0 %copy.125 = f32[2048,768]{0,1:T(8,128)} copy(f32[2048,768]{1,0:T(8,128)} %fusion.86) | data formatting | bytes 12582912 | tf_op jit(solution)/shard_map/optimization_barrier | solution.py:252
  308.1 5.7 copy.152
  313.9 9.2 %fusion.28 = f32[2,12,8,128]{3,2,1,0:T(8,128)S(1)} fusion(f32[2,12,8,128,64]{3,4,2,1,0:T(8,128)} %get-tuple-element.137, f32[2,8,128,12,64]{2,1,0,4,3:T(8,128)S(1)} %bitcast.186, f32[2,8,128]{2,1,0:T(8,128)S(1)} %copy-done.49), kind=kLoop, calls=%fused_computation.45 | loop fusion | flops 4694016 | bytes 12689408 | tf_op jit(solution)/shard_map/reduce_sum | solution.py:261
  323.2 13.1 %fusion.6 = bf16[2,12,8,128,256]{4,3,2,1,0:T(8,128)(2,1)} fusion(f32[2,12,8,128]{3,2,1,0:T(8,128)S(1)} %multiply_divide_fusion, pred[2,8,128,256]{3,2,1,0:T(8,128)(4,1)} %compare_and_fusion, bf16[2,12,8,128,64]{3,4,2,1,0:T(8,128)(2,1)S(1)} %bitcast.196, bf16[2,12,8,128,64]{3,4,2,1,0:T(8,128)(2,1)} %pad_slice_fusion, f32[2,8,128,12,64]{2,1,0,4,3:T(8,128)} %bitcast.187, ...), kind=kOutput, calls=%fused_computation.12 | convolution fusion | flops 841482240 | bytes 25894912 | tf_op jit(solution)/shard_map/shnqd,shnkd->shnqk/dot_general | solution.py:262
  336.3 7.2 %fusion.73 = f32[2,12,8,256,32]{3,4,2,1,0:T(8,128)S(1)} fusion(bf16[2,12,8,128,256]{4,3,2,1,0:T(8,128)(2,1)} %fusion.6, bf16[2,8,128,12,32]{2,1,0,4,3:T(8,128)(2,1)} %bitcast.199), kind=kOutput, calls=%fused_computation.125 | convolution fusion | flops 402653184 | bytes 20447232 | tf_op jit(solution)/shard_map/shnqk,shnqf->shnkf/dot_general | solution.py:268
  348.4 4.6 reshape_reshape.15
  353.0 10.7 %fusion.72 = f32[2,8,128,12,32]{2,4,1,3,0:T(8,128)} fusion(bf16[2,12,8,128,256]{4,3,2,1,0:T(8,128)(2,1)} %fusion.6, bf16[2,12,8,128,32]{3,4,2,1,0:T(8,128)(2,1)S(1)} %bitcast.191, bf16[2,12,8,128,32]{3,4,2,1,0:T(8,128)(2,1)S(1)} %copy-done.21), kind=kOutput, calls=%fused_computation.123 | convolution fusion | flops 408944640 | bytes 18874368 | tf_op jit(solution)/shard_map/shnqk,shnkf->shnqf/dot_general | solution.py:267
  363.8 4.7 copy.127
  371.2 14.5 %fusion.31 = f32[2,12,8,256,64]{3,4,2,1,0:T(8,128)} fusion(bf16[2,12,8,128,256]{4,3,2,1,0:T(8,128)(2,1)} %get-tuple-element.135, pred[2,8,128,256]{3,2,1,0:T(8,128)(4,1)} %compare_and_fusion, f32[2,8,128,12,64]{2,1,0,4,3:T(8,128)} %bitcast.188, f32[2,12,8,128]{3,2,1,0:T(8,128)S(1)} %copy-done.38, f32[2,8,128]{2,1,0:T(8,128)S(1)} %copy-done.49), kind=kOutput, calls=%fused_computation.63 | convolution fusion | flops 816316416 | bytes 32088064 | tf_op jit(solution)/shard_map/shnqk,shnqd->shnkd/dot_general | solution.py:265
  401.8 16.5 %add_convert_fusion.3 = bf16[2048,768]{0,1:T(8,128)(2,1)} fusion(f32[2048,768]{0,1:T(8,128)} %copy-done.4, bf16[2048,3072]{1,0:T(8,128)(2,1)} %get-tuple-element.140, bf16[3072,768]{1,0:T(8,128)(2,1)} %reshape.377, f32[768]{0:T(1024)S(1)} %copy-done.54), kind=kOutput, calls=%fused_computation.56 | convolution fusion | flops 9668395008 | bytes 26741760 | tf_op jit(solution)/shard_map/dot_general | solution.py:236
  418.3 4.9 copy.142
  423.3 8.4 %convolution_bitcast_fusion = f32[2048,12,64]{0,2,1:T(8,128)S(1)} fusion(f32[64,12,32]{0,2,1:T(8,128)S(1)} %bitcast.206, f32[2048,12,32]{0,2,1:T(8,128)S(1)} %copy-done.16, f32[12,2048,32]{1,2,0:T(8,128)} %get-tuple-element.131), kind=kOutput, calls=%fused_computation.70 | convolution fusion | flops 610271232 | bytes 12681216 | tf_op jit(solution)/shard_map/transpose(jvp(lhe,ehm->lhm))/dot_general | solution.py:47
  431.7 6.6 %convolution_bitcast_fusion.1 = f32[2048,12,64]{0,2,1:T(8,128)S(1)} fusion(f32[64,12,32]{0,2,1:T(8,128)S(1)} %bitcast.207, f32[2048,12,32]{0,2,1:T(8,128)S(1)} %copy-done.17, f32[12,2048,32]{1,2,0:T(8,128)S(1)} %copy-done.24), kind=kOutput, calls=%fused_computation.71 | convolution fusion | flops 610271232 | bytes 12681216 | tf_op jit(solution)/shard_map/transpose(jvp(lhe,ehm->lhm))/dot_general | solution.py:47
  447.6 13.2 %convolution_convert_fusion.2 = bf16[768,2304]{1,0:T(8,128)(2,1)} fusion(bf16[2048,2304]{0,1:T(8,128)(2,1)} %pad_maximum_fusion.1, bf16[2048,768]{0,1:T(8,128)(2,1)S(1)} %copy-done.1, f32[768]{0:T(1024)S(1)} %copy-done.53, f32[768]{0:T(1024)S(1)} %copy-done.46, f32[2048]{0:T(1024)S(1)} %copy-done.40, f32[2048]{0:T(1024)S(1)} %copy-done.35), kind=kOutput, calls=%fused_computation.62 | convolution fusion | flops 7258963968 | bytes 16144384 | tf_op jit(solution)/shard_map/dot_general | solution.py:59
  460.7 5.6 reduce
  469.3 13.4 %fusion.118 = (bf16[768]{0:T(1024)(128)(2,1)}, f32[2048,768]{1,0:T(8,128)}) fusion(bf16[2048,2304]{0,1:T(8,128)(2,1)} %pad_maximum_fusion.1, bf16[768,2317]{1,0:T(8,128)(2,1)} %all-gather.3.cloned.1.call-done), kind=kOutput, calls=%fused_computation.222 | convolution fusion | flops 7249329152 | bytes 19269120 | tf_op jit(solution)/shard_map/dot_general | solution.py:65
  482.7 6.8 %copy.130 = f32[2048,768]{0,1:T(8,128)} copy(f32[2048,768]{1,0:T(8,128)} %get-tuple-element.143) | data formatting | bytes 12582912 | tf_op jit(solution)/shard_map/dot_general | solution.py:65
  502.2 7.7 %concatenate.64 = bf16[768,2317]{1,0:T(8,128)(2,1)} concatenate(bf16[768,2304]{1,0:T(8,128)(2,1)} %convolution_convert_fusion.2, bf16[768,1]{1,0:T(8,128)(2,1)} %reshape.411, bf16[768,1]{1,0:T(8,128)(2,1)} %reshape.412, bf16[768,1]{1,0:T(8,128)(2,1)} %reshape.413, bf16[768,1]{1,0:T(8,128)(2,1)} %reshape.414, bf16[768,1]{1,0:T(8,128)(2,1)} %reshape.415, ...), dimensions={1} | concatenate | bytes 7117824 | tf_op jit(solution)/shard_map/concatenate | solution.py:297
  515.0 11.0 %add_add_fusion.2 = f32[2048,768]{0,1:T(8,128)} fusion(f32[2048,768]{0,1:T(8,128)} %copy-done.3, bf16[2048,768]{0,1:T(8,128)(2,1)} %copy.122, f32[2048]{0:T(1024)S(1)} %negate_multiply_fusion, f32[2048]{0:T(1024)} %copy-done.42, f32[2048]{0:T(1024)S(1)} %multiply_multiply_fusion.1, f32[2048]{0:T(1024)S(1)} %copy-done.35, bf16[2048,768]{0,1:T(8,128)(2,1)S(1)} %copy-done.1, ...), kind=kLoop, calls=%fused_computation.51 | loop fusion | flops 18874368 | bytes 25209856 | tf_op jit(solution)/shard_map/add | solution.py:278
  526.0 6.7 %copy.143 = f32[2048,768]{1,0:T(8,128)} copy(f32[2048,768]{0,1:T(8,128)} %add_add_fusion.2) | data formatting | bytes 12582912
  537.8 21.4 %reduce-scatter.5.cloned.1.call-done = bf16[96,2317]{1,0:T(8,128)(2,1)} async-done(((bf16[768,2317]{1,0:T(8,128)(2,1)}), bf16[96,2317]{1,0:T(8,128)(2,1)}) %reduce-scatter.5.cloned.1.call-update) | async-done | bytes 444880 | tf_op jit(solution)/shard_map/reduce_scatter | solution.py:104
  565.7 5.3 collective-permute-done
  571.6 12.6 %collective-permute-done.6 = bf16[24,6912]{1,0:T(8,128)(2,1)S(1)} collective-permute-done((bf16[24,6912]{1,0:T(8,128)(2,1)S(1)}, bf16[24,6912]{1,0:T(8,128)(2,1)S(1)}, u32[]{:S(2)}, u32[]{:S(2)}) %collective-permute-start.6) | collective-permute-done | bytes 331808 | tf_op jit(solution)/shard_map/ppermute | solution.py:98
  587.4 14.7 %collective-permute-done.7 = bf16[48,6912]{1,0:T(8,128)(2,1)S(1)} collective-permute-done((bf16[48,6912]{1,0:T(8,128)(2,1)S(1)}, bf16[48,6912]{1,0:T(8,128)(2,1)S(1)}, u32[]{:S(2)}, u32[]{:S(2)}) %collective-permute-start.7) | collective-permute-done | bytes 663584 | tf_op jit(solution)/shard_map/ppermute | solution.py:98
  (254 shorter events, 141.4 us)
Async XLA Ops:
  7.2 47.3 %all-gather.3.cloned.1.call-start = ((), (), s32[]{:S(2)}) async-start(), calls=%async_computation.2 | async-start | bytes 4202496 | tf_op jit(solution)/shard_map/all_gather | solution.py:75
  15.0 9.1 %copy-start.56 = (s32[2,24]{1,0:T(2,128)S(1)}, s32[2,24]{1,0:T(2,128)}, u32[]{:S(2)}) copy-start(s32[2,24]{1,0:T(2,128)} %param.22) | copy-start | bytes 580
  15.0 9.5 %copy-start.36 = (f32[64,384]{1,0:T(8,128)S(1)}, f32[64,384]{1,0:T(8,128)}, u32[]{:S(2)}) copy-start(f32[64,384]{1,0:T(8,128)} %param.23) | copy-start | bytes 294916
  17.0 120.8 %all-gather.5.cloned.1.call-start = ((), (), s32[]{:S(2)}) async-start(), calls=%async_computation.3 | async-start | bytes 11943936 | tf_op jit(solution)/shard_map/all_gather | solution.py:75
  20.8 426.7 %reduce-scatter.3.cloned.1.call-start = ((), (), s32[]{:S(2)}) async-start(), calls=%async_computation.4 | async-start | bytes 11943936 | tf_op jit(solution)/shard_map/reduce_scatter | solution.py:253
  24.1 113.7 %copy-start = (bf16[2048,768]{0,1:T(8,128)(2,1)}, bf16[2048,768]{0,1:T(8,128)(2,1)S(1)}, u32[]{:S(2)}) copy-start(bf16[2048,768]{0,1:T(8,128)(2,1)S(1)} %copy.105) | copy-start | bytes 9437188
  30.7 83.4 %copy-start.48 = (f32[2,8,128]{2,1,0:T(8,128)}, f32[2,8,128]{2,1,0:T(8,128)S(1)}, u32[]{:S(2)}) copy-start(f32[2,8,128]{2,1,0:T(8,128)S(1)} %compare_convert_fusion) | copy-start | bytes 24580
  31.2 56.3 %copy-start.34 = (f32[2048]{0:T(1024)}, f32[2048]{0:T(1024)S(1)}, u32[]{:S(2)}) copy-start(f32[2048]{0:T(1024)S(1)} %broadcast_multiply_fusion.1) | copy-start | bytes 24580
  32.7 54.9 %copy-start.39 = (f32[2048]{0:T(1024)}, f32[2048]{0:T(1024)S(1)}, u32[]{:S(2)}) copy-start(f32[2048]{0:T(1024)S(1)} %fusion.91) | copy-start | bytes 24580
  35.7 32.0 %copy-start.26 = (f32[2048,32]{0,1:T(8,128)}, f32[2048,32]{0,1:T(8,128)S(1)}, u32[]{:S(2)}) copy-start(f32[2048,32]{0,1:T(8,128)S(1)} %get-tuple-element.123) | copy-start | bytes 786436
  58.5 29.0 %copy-start.45 = (f32[768]{0:T(1024)}, f32[768]{0:T(1024)S(1)}, u32[]{:S(2)}) copy-start(f32[768]{0:T(1024)S(1)} %get-tuple-element.92) | copy-start | bytes 9220
  58.5 29.0 %copy-start.52 = (f32[768]{0:T(1024)}, f32[768]{0:T(1024)S(1)}, u32[]{:S(2)}) copy-start(f32[768]{0:T(1024)S(1)} %get-tuple-element.91) | copy-start | bytes 9220
  102.7 11.3 %copy-start.14 = (bf16[2,8,128,12,64]{2,4,1,3,0:T(8,128)(2,1)}, bf16[2,8,128,12,64]{2,4,1,3,0:T(8,128)(2,1)S(1)}, u32[]{:S(2)}) copy-start(bf16[2,8,128,12,64]{2,4,1,3,0:T(8,128)(2,1)S(1)} %copy.177) | copy-start | bytes 9437188
  103.2 10.9 %copy-start.20 = (bf16[2,12,8,128,32]{3,4,2,1,0:T(8,128)(2,1)}, bf16[2,12,8,128,32]{3,4,2,1,0:T(8,128)(2,1)S(1)}, u32[]{:S(2)}) copy-start(bf16[2,12,8,128,32]{3,4,2,1,0:T(8,128)(2,1)S(1)} %pad_slice_fusion.1) | copy-start | bytes 4718596
  114.1 10.6 %copy-start.37 = (f32[2,12,8,128]{3,2,1,0:T(8,128)}, f32[2,12,8,128]{3,2,1,0:T(8,128)S(1)}, u32[]{:S(2)}) copy-start(f32[2,12,8,128]{3,2,1,0:T(8,128)S(1)} %get-tuple-element.134) | copy-start | bytes 294916
  151.2 8.5 %copy-start.55 = (f32[768]{0:T(1024)S(1)}, f32[768]{0:T(1024)}, u32[]{:S(2)}) copy-start(f32[768]{0:T(1024)} %get-tuple-element.85) | copy-start | bytes 9220
  159.7 24.1 %copy-start.12 = (bf16[2048,768]{1,0:T(8,128)(2,1)S(1)}, bf16[2048,768]{1,0:T(8,128)(2,1)}, u32[]{:S(2)}) copy-start(bf16[2048,768]{1,0:T(8,128)(2,1)} %param.21) | copy-start | bytes 9437188
  159.7 24.1 %copy-start.22 = (bf16[3072,768]{1,0:T(8,128)(2,1)S(1)}, bf16[3072,768]{1,0:T(8,128)(2,1)}, u32[]{:S(2)}) copy-start(bf16[3072,768]{1,0:T(8,128)(2,1)} %reshape.377) | copy-start | bytes 14155780
  159.7 46.3 %slice-start = ((s8[6291456]{0:T(1024)(128)(4,1)}), s8[4194304]{0:T(1024)(128)(4,1)S(1)}, s32[]{:S(2)}) async-start(s8[6291456]{0:T(1024)(128)(4,1)} %bitcast.181), calls=%async_computation.6 | async-start | bytes 8388608
  183.7 22.2 %slice-start.1 = ((s8[6291456]{0:T(1024)(128)(4,1)}), s8[2097152]{0:T(1024)(128)(4,1)S(1)}, s32[]{:S(2)}) async-start(s8[6291456]{0:T(1024)(128)(4,1)} %bitcast.181), calls=%async_computation.7 | async-start | bytes 4194304
  206.0 14.8 %copy-start.58 = (bf16[2048,3072]{1,0:T(8,128)(2,1)S(1)}, bf16[2048,3072]{1,0:T(8,128)(2,1)}, u32[]{:S(2)}) copy-start(bf16[2048,3072]{1,0:T(8,128)(2,1)} %get-tuple-element.147) | copy-start | bytes 37748740
  234.9 12.9 %slice-start.2 = ((s8[6291456]{0:T(1024)(128)(4,1)}), s8[2097152]{0:T(1024)(128)(4,1)S(1)}, s32[]{:S(2)}) async-start(s8[6291456]{0:T(1024)(128)(4,1)} %bitcast.183), calls=%async_computation.8 | async-start | bytes 4194304
  241.6 6.2 %slice-start.3 = ((s8[6291456]{0:T(1024)(128)(4,1)}), s8[4194304]{0:T(1024)(128)(4,1)S(1)}, s32[]{:S(2)}) async-start(s8[6291456]{0:T(1024)(128)(4,1)} %bitcast.183), calls=%async_computation.9 | async-start | bytes 8388608
  241.6 7.7 %copy-start.5 = (f32[2048,768]{0,1:T(8,128)S(1)}, f32[2048,768]{0,1:T(8,128)}, u32[]{:S(2)}) copy-start(f32[2048,768]{0,1:T(8,128)} %copy.123) | copy-start | bytes 18874372
  299.5 259.6 %reduce-scatter.5.cloned.1.call-start = ((), (), s32[]{:S(2)}) async-start(), calls=%async_computation.5 | async-start | bytes 4202496 | tf_op jit(solution)/shard_map/reduce_scatter | solution.py:104
  308.1 5.7 copy-start.49
  313.9 9.3 %copy-start.7 = (f32[96,8,16,128]{3,2,1,0:T(8,128)}, f32[96,8,16,128]{3,2,1,0:T(8,128)S(1)}, u32[]{:S(2)}) copy-start(f32[96,8,16,128]{3,2,1,0:T(8,128)S(1)} %copy.152) | copy-start | bytes 18874372
  313.9 9.3 %copy-start.38 = (f32[2,12,8,128]{3,2,1,0:T(8,128)S(1)}, f32[2,12,8,128]{3,2,1,0:T(8,128)}, u32[]{:S(2)}) copy-start(f32[2,12,8,128]{3,2,1,0:T(8,128)} %copy-done.37) | copy-start | bytes 294916
  313.9 9.3 %copy-start.15 = (bf16[2,8,128,12,64]{2,4,1,3,0:T(8,128)(2,1)S(1)}, bf16[2,8,128,12,64]{2,4,1,3,0:T(8,128)(2,1)}, u32[]{:S(2)}) copy-start(bf16[2,8,128,12,64]{2,4,1,3,0:T(8,128)(2,1)} %copy-done.14) | copy-start | bytes 9437188
  344.6 8.4 %copy-start.10 = (bf16[2,8,128,12,32]{2,4,1,3,0:T(8,128)(2,1)S(1)}, bf16[2,8,128,12,32]{2,4,1,3,0:T(8,128)(2,1)}, u32[]{:S(2)}) copy-start(bf16[2,8,128,12,32]{2,4,1,3,0:T(8,128)(2,1)} %copy.178) | copy-start | bytes 4718596
  344.6 8.4 %copy-start.21 = (bf16[2,12,8,128,32]{3,4,2,1,0:T(8,128)(2,1)S(1)}, bf16[2,12,8,128,32]{3,4,2,1,0:T(8,128)(2,1)}, u32[]{:S(2)}) copy-start(bf16[2,12,8,128,32]{3,4,2,1,0:T(8,128)(2,1)} %copy-done.20) | copy-start | bytes 4718596
  393.0 7.7 %copy-start.51 = (bf16[3072]{0:T(1024)(128)(2,1)S(1)}, bf16[3072]{0:T(1024)(128)(2,1)}, u32[]{:S(2)}) copy-start(bf16[3072]{0:T(1024)(128)(2,1)} %get-tuple-element.146) | copy-start | bytes 18436
  393.0 8.8 %copy-start.54 = (f32[768]{0:T(1024)S(1)}, f32[768]{0:T(1024)}, u32[]{:S(2)}) copy-start(f32[768]{0:T(1024)} %get-tuple-element.84) | copy-start | bytes 9220
  423.3 8.4 %copy-start.17 = (f32[2048,12,32]{0,2,1:T(8,128)S(1)}, f32[2048,12,32]{0,2,1:T(8,128)}, u32[]{:S(2)}) copy-start(f32[2048,12,32]{0,2,1:T(8,128)} %reshape_reshape.14) | copy-start | bytes 9437188
  423.3 8.4 %copy-start.24 = (f32[12,2048,32]{1,2,0:T(8,128)S(1)}, f32[12,2048,32]{1,2,0:T(8,128)}, u32[]{:S(2)}) copy-start(f32[12,2048,32]{1,2,0:T(8,128)} %get-tuple-element.133) | copy-start | bytes 9437188
  431.7 6.7 %copy-start.27 = (f32[2048,32]{0,1:T(8,128)S(1)}, f32[2048,32]{0,1:T(8,128)}, u32[]{:S(2)}) copy-start(f32[2048,32]{0,1:T(8,128)} %copy-done.26) | copy-start | bytes 786436
  431.7 6.7 %copy-start.29 = (f32[2048,32]{0,1:T(8,128)S(1)}, f32[2048,32]{0,1:T(8,128)}, u32[]{:S(2)}) copy-start(f32[2048,32]{0,1:T(8,128)} %get-tuple-element.124) | copy-start | bytes 786436
  493.6 6.0 copy-start.50
  493.6 8.6 %copy-start.32 = (bf16[768,1]{1,0:T(8,128)(2,1)S(1)}, bf16[768,1]{1,0:T(8,128)(2,1)}, u32[]{:S(2)}) copy-start(bf16[768,1]{1,0:T(8,128)(2,1)} %reshape.419) | copy-start | bytes 4612
  512.6 20.2 %collective-permute-start.4 = (bf16[48,6912]{1,0:T(8,128)(2,1)}, bf16[48,6912]{1,0:T(8,128)(2,1)}, u32[]{:S(2)}, u32[]{:S(2)}) collective-permute-start(bf16[48,6912]{1,0:T(8,128)(2,1)} %select_convert_fusion.3), channel_id=1, source_target_pairs={{0,1},{1,0},{2,3},{3,2},{4,5},{5,4},{6,7},{7,6},{8,9},{9,8},{10,11... | collective-permute-start | bytes 1990664 | tf_op jit(solution)/shard_map/ppermute | solution.py:93
  526.0 6.7 %copy-start.8 = (f32[96,6912]{1,0:T(8,128)S(1)}, f32[96,6912]{1,0:T(8,128)}, u32[]{:S(2)}) copy-start(f32[96,6912]{1,0:T(8,128)} %convert_element_type.210) | copy-start | bytes 7962628
  535.1 26.7 %collective-permute-start.5 = (bf16[24,6912]{1,0:T(8,128)(2,1)S(1)}, bf16[24,6912]{1,0:T(8,128)(2,1)S(1)}, u32[]{:S(2)}, u32[]{:S(2)}) collective-permute-start(bf16[24,6912]{1,0:T(8,128)(2,1)S(1)} %select_convert_fusion.4), channel_id=1, source_target_pairs={{0,2},{1,3},{2,0},{3,1},{4,6},{5,7},{6,4},{7,5},{8,10},{9,11},{10,... | collective-permute-start | bytes 995336 | tf_op jit(solution)/shard_map/ppermute | solution.py:93
  560.3 10.7 %collective-permute-start = (bf16[48,2317]{1,0:T(8,128)(2,1)S(1)}, bf16[48,2317]{1,0:T(8,128)(2,1)S(1)}, u32[]{:S(2)}, u32[]{:S(2)}) collective-permute-start(bf16[48,2317]{1,0:T(8,128)(2,1)S(1)} %select_convert_fusion.5), channel_id=1, source_target_pairs={{0,1},{1,0},{2,3},{3,2},{4,5},{5,4},{6,7},{7,6},{8,9},{9,8},{10,11... | collective-permute-start | bytes 667304 | tf_op jit(solution)/shard_map/ppermute | solution.py:93
  563.2 20.9 %collective-permute-start.6 = (bf16[24,6912]{1,0:T(8,128)(2,1)S(1)}, bf16[24,6912]{1,0:T(8,128)(2,1)S(1)}, u32[]{:S(2)}, u32[]{:S(2)}) collective-permute-start(bf16[24,6912]{1,0:T(8,128)(2,1)S(1)} %add_convert_fusion.6), channel_id=1, source_target_pairs={{0,2},{1,3},{2,0},{3,1},{4,6},{5,7},{6,4},{7,5},{8,10},{9,11},{10,... | collective-permute-start | bytes 995336 | tf_op jit(solution)/shard_map/ppermute | solution.py:98
  571.1 14.4 %collective-permute-start.1 = (bf16[24,2317]{1,0:T(8,128)(2,1)S(1)}, bf16[24,2317]{1,0:T(8,128)(2,1)S(1)}, u32[]{:S(2)}, u32[]{:S(2)}) collective-permute-start(bf16[24,2317]{1,0:T(8,128)(2,1)S(1)} %select_convert_fusion.6), channel_id=1, source_target_pairs={{0,2},{1,3},{2,0},{3,1},{4,6},{5,7},{6,4},{7,5},{8,10},{9,11},{10,... | collective-permute-start | bytes 333656 | tf_op jit(solution)/shard_map/ppermute | solution.py:93
  584.3 17.9 %collective-permute-start.7 = (bf16[48,6912]{1,0:T(8,128)(2,1)S(1)}, bf16[48,6912]{1,0:T(8,128)(2,1)S(1)}, u32[]{:S(2)}, u32[]{:S(2)}) collective-permute-start(bf16[48,6912]{1,0:T(8,128)(2,1)S(1)} %maximum_select_fusion.1), channel_id=1, source_target_pairs={{0,1},{1,0},{2,3},{3,2},{4,5},{5,4},{6,7},{7,6},{8,9},{9,8},{10,11... | collective-permute-start | bytes 1990664 | tf_op jit(solution)/shard_map/ppermute | solution.py:98
  585.6 16.8 %collective-permute-start.2 = (bf16[24,2317]{1,0:T(8,128)(2,1)S(1)}, bf16[24,2317]{1,0:T(8,128)(2,1)S(1)}, u32[]{:S(2)}, u32[]{:S(2)}) collective-permute-start(bf16[24,2317]{1,0:T(8,128)(2,1)S(1)} %add_convert_fusion.7), channel_id=1, source_target_pairs={{0,2},{1,3},{2,0},{3,1},{4,6},{5,7},{6,4},{7,5},{8,10},{9,11},{10,... | collective-permute-start | bytes 333656 | tf_op jit(solution)/shard_map/ppermute | solution.py:98
  602.4 6.1 collective-permute-start.3
  (27 other events, 100.1 us)
Sparse Core Ops, SparseCore 0:
  17.1 37.3 all-gather.2
  56.4 63.6 all-gather.4
  299.6 82.5 reduce-scatter.2
  510.0 49.0 reduce-scatter.4
